TPU v7x, 32 devices: a whole 2x2x4 slice. The times are simulated.
32 devices in a mesh: slab: 16 (over z, y, x), sub: 2 (over core).
Axes of the slice: x: 2, y: 2, z: 4, core: 2. Of those that a mesh axis runs over, the one named last changes fastest.
Arguments:
- start: float32 [4, 96, 32, 256], P(None, 'slab', 'sub'), may hold values from -6 to 6
- wind: float32 [3, 96, 32, 256], P(None, 'slab', 'sub'), may hold values from -4 to 4
- reaction: float32 [96, 32, 256], P('slab', 'sub'), may hold values from 0.5 to 4
- mass: float32 [96, 32, 256], P('slab', 'sub'), may hold values from 0.5 to 2
Outputs:
- basis: float32 [4, 4, 96, 32, 256], P(None, None, 'slab', 'sub')
- search: float32 [3, 4, 96, 32, 256], P(None, None, 'slab', 'sub')
- hessenberg: float32 [4, 3], replicated
All inputs are finite; a program needn't handle non-finite values.
Results may differ from a plain program's by a relative error of at most 0.0003.
Values sent between devices are 32-bit elements; how exact they have to be, the bound alone decides.
No kernel may reach another device: no remote copies, remote signals or barrier semaphores. Data moves between devices by JAX's collectives and lax.ppermute only.
A program may use at most 64 MiB of HBM per device.

v0:
```python
import jax
import jax.numpy as jnp
from jax import lax
from jax.sharding import PartitionSpec as P

ITERS = 3


def padded_2(shard, sides, width):
    for axis, dim in sides:
        devices, length = (lax.axis_size(axis), shard.shape[dim])
        up = [(i, (i + 1) % devices) for i in range(devices - 1)]
        down = [(j, i) for i, j in up]
        last = lax.slice_in_dim(shard, length - width, length, axis=dim)
        leading = lax.slice_in_dim(shard, 0, width, axis=dim)
        before = lax.ppermute(last, axis, up)
        after = lax.ppermute(leading, axis, down)
        shard = jnp.concatenate([before, shard, after], axis=dim)
    return shard


def neighbour_sets(padded):
    center = padded[..., 1:-1, 1:-1, :]
    zero_face = jnp.zeros_like(center[..., :1])
    plus_side = (
        padded[..., 2:, 1:-1, :],
        padded[..., 1:-1, 2:, :],
        jnp.concatenate([center[..., 1:], zero_face], -1),
    )
    minus_side = (
        padded[..., :-2, 1:-1, :],
        padded[..., 1:-1, :-2, :],
        jnp.concatenate([zero_face, center[..., :-1]], -1),
    )
    return (center, plus_side, minus_side)


def six_sum(plus_side, minus_side):
    total = plus_side[0] + minus_side[0]
    total = total + plus_side[1] + minus_side[1]
    return total + plus_side[2] + minus_side[2]


def transport(padded, reaction_k, wind_k):
    center, plus_side, minus_side = neighbour_sets(padded)
    convect = wind_k[0] * (plus_side[0] - minus_side[0])
    convect = convect + wind_k[1] * (plus_side[1] - minus_side[1])
    convect = convect + wind_k[2] * (plus_side[2] - minus_side[2])
    return (6.0 + reaction_k) * center - six_sum(plus_side, minus_side) + 0.5 * convect


def gradient(padded):
    center, plus_side, minus_side = neighbour_sets(padded)
    return jnp.stack(
        [0.5 * (plus_side[dim_index] - minus_side[dim_index]) for dim_index in range(3)]
    )


def divergence(padded):
    center, plus_side, minus_side = neighbour_sets(padded)
    total = 0.5 * (plus_side[0][0] - minus_side[0][0])
    total = total + 0.5 * (plus_side[1][1] - minus_side[1][1])
    return total + 0.5 * (plus_side[2][2] - minus_side[2][2])


def pressure_poisson(padded):
    center, plus_side, minus_side = neighbour_sets(padded)
    return 7.0 * center - six_sum(plus_side, minus_side)


def oseen_apply(padded, reaction_k, wind_k):
    upper = transport(padded[:3], reaction_k, wind_k) + gradient(padded[3])
    center, plus_side, minus_side = neighbour_sets(padded[3])
    lower = -divergence(padded[:3]) - 0.5 * (6.0 * center - six_sum(plus_side, minus_side))
    return jnp.concatenate([upper, lower[None]], 0)


def local_dots(vectors, image):
    return jnp.stack([jnp.sum(vector * image) for vector in vectors])


def per_device(start, wind, reaction, mass):
    cells_x = start.shape[1]
    cells_y = start.shape[2]

    def inside(width):
        global_x = (
            lax.axis_index("slab") * cells_x
            - width
            + jnp.arange(cells_x + 2 * width, dtype=jnp.int32)
        )
        global_y = (
            lax.axis_index("sub") * cells_y
            - width
            + jnp.arange(cells_y + 2 * width, dtype=jnp.int32)
        )
        inside_x = (global_x >= 0) & (global_x < cells_x * lax.axis_size("slab"))
        inside_y = (global_y >= 0) & (global_y < cells_y * lax.axis_size("sub"))
        return (inside_x[:, None] & inside_y[None, :])[:, :, None]

    stacked = jnp.concatenate([wind, reaction[None], mass[None]], 0)
    coeffs = padded_2(stacked, (("slab", 1), ("sub", 2)), 3)

    def coef_at(width):
        offset = 3 - width
        return coeffs[
            :, offset : offset + cells_x + 2 * width, offset : offset + cells_y + 2 * width, :
        ]

    def apply_both(vector):
        extended = padded_2(vector, (("slab", 1), ("sub", 2)), 5)
        pressure = extended[3]
        first_guess = pressure / 7.0
        second_guess = (
            first_guess[1:-1, 1:-1] + (pressure[1:-1, 1:-1] - pressure_poisson(first_guess)) / 7.0
        )
        second_guess = jnp.where(inside(4), second_guess, 0.0)
        coef_three = coef_at(3)
        schur = jnp.where(
            inside(3), -transport(second_guess, coef_three[3], coef_three[:3]) / coef_three[4], 0.0
        )
        residue = jnp.where(inside(2), extended[:3, 3:-3, 3:-3] - gradient(schur), 0.0)
        coef_two = coef_at(2)
        velocity_first = residue / (6.0 + coef_two[3])
        coef_one = coef_at(1)
        velocity = velocity_first[:, 1:-1, 1:-1] + (
            residue[:, 1:-1, 1:-1] - transport(velocity_first, coef_one[3], coef_one[:3])
        ) / (6.0 + coef_one[3])
        velocity = jnp.where(inside(1), velocity, 0.0)
        found = jnp.concatenate([velocity, schur[None, 2:-2, 2:-2]], 0)
        image = oseen_apply(found, reaction, wind)
        return (found[:, 1:-1, 1:-1], image)

    scale_start = jnp.sqrt(lax.psum(jnp.sum(start * start), ("slab", "sub")))
    vectors = [start / scale_start]
    first_found, first_image = apply_both(vectors[0])
    searches = [first_found]
    images = [first_image]
    hess = jnp.zeros((ITERS + 1, ITERS), jnp.float32)
    for column in range(ITERS):
        image = images[column]
        projected = lax.psum(local_dots(vectors, image), ("slab", "sub"))
        for row in range(column + 1):
            image = image - projected[row] * vectors[row]
        norm_next = jnp.sqrt(lax.psum(jnp.sum(image * image), ("slab", "sub")))
        hess = hess.at[: column + 1, column].set(projected)
        hess = hess.at[column + 1, column].set(norm_next)
        vectors.append(image / norm_next)
        if column + 1 < ITERS:
            next_found, next_image = apply_both(vectors[column + 1])
            searches.append(next_found)
            images.append(next_image)
    return (jnp.stack(vectors), jnp.stack(searches), hess)


def solution(mesh):
    return jax.shard_map(
        per_device,
        mesh=mesh,
        in_specs=(
            P(None, "slab", "sub", None),
            P(None, "slab", "sub", None),
            P("slab", "sub", None),
            P("slab", "sub", None),
        ),
        out_specs=(P(None, None, "slab", "sub", None), P(None, None, "slab", "sub", None), P()),
        check_vma=False,
    )
```

profile of v0, /device:TPU:0, one launch (start us, length us, event | category | flops | bytes accessed | tf_op | source)
XLA Modules:
  0.0 415.6 jit_solution(4579641855387996888)
XLA Ops:
  2.5 5.0 %collective-permute-start.4 = (f32[5,3,16,256]{3,2,1,0:T(8,128)}, f32[5,3,16,256]{3,2,1,0:T(8,128)S(1)}, u32[]{:S(2)}, u32[]{:S(2)}) collective-permute-start(f32[5,3,16,256]{3,2,1,0:T(8,128)} %get-tuple-element.129), channel_id=1, source_target_pairs={{0,2},{2,4},{4,6},{6,8},{8,10},{10,12},{12,14},{14,16},{16,18},{18... | collective-permute-start | bytes 737288 | tf_op jit(solution)/shard_map/ppermute | solution.py:16
  8.3 1.4 collective-permute-start.5
  9.7 44.7 %psum.49 = f32[]{:T(128)} all-reduce(f32[]{:T(128)} %multiply_reduce_fusion.9), channel_id=1, replica_groups=mesh['slab'=16,'sub'=2] {'slab','sub'}, use_global_device_ids=true, to_apply=%region_1.0 | all-reduce | flops 1 | bytes 8 | tf_op jit(solution)/shard_map/psum | solution.py:134
  55.2 4.2 %collective-permute-start = (f32[4,5,16,256]{3,2,1,0:T(8,128)S(1)}, f32[4,5,16,256]{3,2,1,0:T(8,128)S(1)}, u32[]{:S(2)}, u32[]{:S(2)}) collective-permute-start(f32[4,5,16,256]{3,2,1,0:T(8,128)S(1)} %get-tuple-element.135), channel_id=1, source_target_pairs={{0,2},{2,4},{4,6},{6,8},{8,10},{10,12},{12,14},{14,16},{16,18},{18... | collective-permute-start | bytes 983048 | tf_op jit(solution)/shard_map/ppermute | solution.py:16
  59.4 1.3 collective-permute-start.1
  63.3 1.3 collective-permute-start.6
  64.7 1.3 collective-permute-start.7
  66.0 6.1 %collective-permute-done = f32[4,5,16,256]{3,2,1,0:T(8,128)S(1)} collective-permute-done((f32[4,5,16,256]{3,2,1,0:T(8,128)S(1)}, f32[4,5,16,256]{3,2,1,0:T(8,128)S(1)}, u32[]{:S(2)}, u32[]{:S(2)}) %collective-permute-start) | collective-permute-done | bytes 327712 | tf_op jit(solution)/shard_map/ppermute | solution.py:16
  72.1 1.9 collective-permute-done.1
  74.2 1.5 collective-permute-start.2
  75.7 1.3 collective-permute-start.3
  77.4 2.0 collective-permute-done.3
  83.6 38.5 %psum.50 = f32[1]{0:T(128)} all-reduce(f32[1]{0:T(128)} %bitcast.25), channel_id=1, replica_groups=mesh['slab'=16,'sub'=2] {'slab','sub'}, use_global_device_ids=true, to_apply=%region_3.4 | all-reduce | flops 1 | bytes 8 | tf_op jit(solution)/shard_map/psum | solution.py:142
  122.0 1.3 multiply_reduce_fusion.7
  124.1 41.0 %psum.51 = f32[]{:T(128)} all-reduce(f32[]{:T(128)} %multiply_reduce_fusion.7), channel_id=1, replica_groups=mesh['slab'=16,'sub'=2] {'slab','sub'}, use_global_device_ids=true, to_apply=%region_5.6 | all-reduce | flops 1 | bytes 8 | tf_op jit(solution)/shard_map/psum | solution.py:145
  165.8 1.6 broadcast_divide_fusion.4
  167.5 4.2 %collective-permute-start.8 = (f32[4,5,16,256]{3,2,1,0:T(8,128)S(1)}, f32[4,5,16,256]{3,2,1,0:T(8,128)S(1)}, u32[]{:S(2)}, u32[]{:S(2)}) collective-permute-start(f32[4,5,16,256]{3,2,1,0:T(8,128)S(1)} %get-tuple-element.133), channel_id=1, source_target_pairs={{0,2},{2,4},{4,6},{6,8},{8,10},{10,12},{12,14},{14,16},{16,18},{18... | collective-permute-start | bytes 983048 | tf_op jit(solution)/shard_map/ppermute | solution.py:16
  171.7 1.3 collective-permute-start.9
  173.0 1.3 fusion.139
  175.1 1.2 scatter.20
  176.3 8.0 %collective-permute-done.8 = f32[4,5,16,256]{3,2,1,0:T(8,128)S(1)} collective-permute-done((f32[4,5,16,256]{3,2,1,0:T(8,128)S(1)}, f32[4,5,16,256]{3,2,1,0:T(8,128)S(1)}, u32[]{:S(2)}, u32[]{:S(2)}) %collective-permute-start.8) | collective-permute-done | bytes 327712 | tf_op jit(solution)/shard_map/ppermute | solution.py:16
  184.3 1.9 collective-permute-done.9
  186.4 1.3 collective-permute-start.10
  187.7 1.5 collective-permute-start.11
  190.0 1.5 collective-permute-done.11
  198.0 1.4 pad_maximum_fusion.30
  199.3 1.4 scatter.21
  200.7 38.9 %psum.52 = f32[2]{0:T(128)S(1)} all-reduce(f32[2]{0:T(128)S(1)} %pad_maximum_fusion.30), channel_id=1, replica_groups=mesh['slab'=16,'sub'=2] {'slab','sub'}, use_global_device_ids=true, to_apply=%region_8.9 | all-reduce | flops 2 | bytes 16 | tf_op jit(solution)/shard_map/psum | solution.py:142
  240.3 3.6 multiply_reduce_fusion.4
  243.9 40.7 %psum.53 = f32[]{:T(128)} all-reduce(f32[]{:T(128)} %get-tuple-element.89), channel_id=1, replica_groups=mesh['slab'=16,'sub'=2] {'slab','sub'}, use_global_device_ids=true, to_apply=%region_10.11 | all-reduce | flops 1 | bytes 8 | tf_op jit(solution)/shard_map/psum | solution.py:145
  287.3 4.9 %collective-permute-start.12 = (f32[4,5,16,256]{3,2,1,0:T(8,128)}, f32[4,5,16,256]{3,2,1,0:T(8,128)}, u32[]{:S(2)}, u32[]{:S(2)}) collective-permute-start(f32[4,5,16,256]{3,2,1,0:T(8,128)} %get-tuple-element.131), channel_id=1, source_target_pairs={{0,2},{2,4},{4,6},{6,8},{8,10},{10,12},{12,14},{14,16},{16,18},{18... | collective-permute-start | bytes 983048 | tf_op jit(solution)/shard_map/ppermute | solution.py:16
  292.3 1.3 collective-permute-start.13
  293.6 3.1 broadcast_select_fusion.1
  296.7 2.6 scatter.24
  299.3 1.4 scatter.25
  300.6 3.3 collective-permute-done.12
  303.9 1.9 collective-permute-done.13
  307.2 1.3 collective-permute-start.14
  308.5 1.3 collective-permute-start.15
  310.7 1.6 collective-permute-done.15
  315.4 1.2 broadcast_divide_fusion
  320.7 2.0 pad_maximum_fusion.31
  322.8 39.6 %psum.54 = f32[3]{0:T(128)S(1)} all-reduce(f32[3]{0:T(128)S(1)} %pad_maximum_fusion.31), channel_id=1, replica_groups=mesh['slab'=16,'sub'=2] {'slab','sub'}, use_global_device_ids=true, to_apply=%region_14.15 | all-reduce | flops 3 | bytes 24 | tf_op jit(solution)/shard_map/psum | solution.py:142
  363.1 1.9 broadcast_select_fusion
  364.9 1.3 scatter.26
  366.3 3.5 multiply_reduce_fusion
  369.8 40.8 %psum.55 = f32[]{:T(128)} all-reduce(f32[]{:T(128)} %get-tuple-element.83), channel_id=1, replica_groups=mesh['slab'=16,'sub'=2] {'slab','sub'}, use_global_device_ids=true, to_apply=%region_16.17 | all-reduce | flops 1 | bytes 8 | tf_op jit(solution)/shard_map/psum | solution.py:145
  414.3 1.3 pad_maximum_fusion
  (194 shorter events, 34.1 us)
Async XLA Ops:
  0.6 6.9 %copy-start = (f32[4,6,16,256]{3,2,1,0:T(8,128)S(1)}, f32[4,6,16,256]{3,2,1,0:T(8,128)}, u32[]{:S(2)}) copy-start(f32[4,6,16,256]{3,2,1,0:T(8,128)} %param.16) | copy-start | bytes 1179652
  2.5 58.8 %copy-start.31 = (f32[6,16,256]{2,1,0:T(8,128)S(1)}, f32[6,16,256]{2,1,0:T(8,128)}, u32[]{:S(2)}) copy-start(f32[6,16,256]{2,1,0:T(8,128)} %param.18) | copy-start | bytes 294916
  2.5 58.8 %copy-start.3 = (f32[3,6,16,256]{3,2,1,0:T(8,128)S(1)}, f32[3,6,16,256]{3,2,1,0:T(8,128)}, u32[]{:S(2)}) copy-start(f32[3,6,16,256]{3,2,1,0:T(8,128)} %param.17) | copy-start | bytes 884740
  2.5 60.7 %collective-permute-start.4 = (f32[5,3,16,256]{3,2,1,0:T(8,128)}, f32[5,3,16,256]{3,2,1,0:T(8,128)S(1)}, u32[]{:S(2)}, u32[]{:S(2)}) collective-permute-start(f32[5,3,16,256]{3,2,1,0:T(8,128)} %get-tuple-element.129), channel_id=1, source_target_pairs={{0,2},{2,4},{4,6},{6,8},{8,10},{10,12},{12,14},{14,16},{16,18},{18... | collective-permute-start | bytes 737288 | tf_op jit(solution)/shard_map/ppermute | solution.py:16
  8.3 53.3 %copy-start.44 = (s32[2]{0:T(128)S(1)}, s32[2]{0:T(128)}, u32[]{:S(2)}) copy-start(s32[2]{0:T(128)} %constant.231.clone.1) | copy-start | bytes 28
  8.3 55.0 %collective-permute-start.5 = (f32[5,3,16,256]{3,2,1,0:T(8,128)S(1)}, f32[5,3,16,256]{3,2,1,0:T(8,128)S(1)}, u32[]{:S(2)}, u32[]{:S(2)}) collective-permute-start(f32[5,3,16,256]{3,2,1,0:T(8,128)S(1)} %get-tuple-element.130), channel_id=1, source_target_pairs={{2,0},{4,2},{6,4},{8,6},{10,8},{12,10},{14,12},{16,14},{18,16},{20... | collective-permute-start | bytes 737288 | tf_op jit(solution)/shard_map/ppermute | solution.py:17
  55.1 8.1 %copy-start.40 = (f32[6,16,256]{2,1,0:T(8,128)S(1)}, f32[6,16,256]{2,1,0:T(8,128)}, u32[]{:S(2)}) copy-start(f32[6,16,256]{2,1,0:T(8,128)} %param.19) | copy-start | bytes 294916
  55.2 16.8 %collective-permute-start = (f32[4,5,16,256]{3,2,1,0:T(8,128)S(1)}, f32[4,5,16,256]{3,2,1,0:T(8,128)S(1)}, u32[]{:S(2)}, u32[]{:S(2)}) collective-permute-start(f32[4,5,16,256]{3,2,1,0:T(8,128)S(1)} %get-tuple-element.135), channel_id=1, source_target_pairs={{0,2},{2,4},{4,6},{6,8},{8,10},{10,12},{12,14},{14,16},{16,18},{18... | collective-permute-start | bytes 983048 | tf_op jit(solution)/shard_map/ppermute | solution.py:16
  59.4 14.5 %collective-permute-start.1 = (f32[4,5,16,256]{3,2,1,0:T(8,128)S(1)}, f32[4,5,16,256]{3,2,1,0:T(8,128)S(1)}, u32[]{:S(2)}, u32[]{:S(2)}) collective-permute-start(f32[4,5,16,256]{3,2,1,0:T(8,128)S(1)} %get-tuple-element.136), channel_id=1, source_target_pairs={{2,0},{4,2},{6,4},{8,6},{10,8},{12,10},{14,12},{16,14},{18,16},{20... | collective-permute-start | bytes 983048 | tf_op jit(solution)/shard_map/ppermute | solution.py:17
  61.3 134.9 %copy-start.19 = (f32[6,16,256]{2,1,0:T(8,128)}, f32[6,16,256]{2,1,0:T(8,128)S(1)}, u32[]{:S(2)}) copy-start(f32[6,16,256]{2,1,0:T(8,128)S(1)} %broadcast_add_fusion) | copy-start | bytes 294916
  61.4 21.2 %copy-start.21 = (f32[6,16,256]{2,1,0:T(8,128)}, f32[6,16,256]{2,1,0:T(8,128)S(1)}, u32[]{:S(2)}) copy-start(f32[6,16,256]{2,1,0:T(8,128)S(1)} %get-tuple-element.161) | copy-start | bytes 294916
  61.4 21.2 %copy-start.24 = (f32[6,16,256]{2,1,0:T(8,128)}, f32[6,16,256]{2,1,0:T(8,128)S(1)}, u32[]{:S(2)}) copy-start(f32[6,16,256]{2,1,0:T(8,128)S(1)} %get-tuple-element.162) | copy-start | bytes 294916
  61.4 21.2 %copy-start.27 = (f32[6,16,256]{2,1,0:T(8,128)}, f32[6,16,256]{2,1,0:T(8,128)S(1)}, u32[]{:S(2)}) copy-start(f32[6,16,256]{2,1,0:T(8,128)S(1)} %get-tuple-element.163) | copy-start | bytes 294916
  63.2 8.8 %copy-start.35 = (f32[5,3,16,256]{3,2,1,0:T(8,128)}, f32[5,3,16,256]{3,2,1,0:T(8,128)S(1)}, u32[]{:S(2)}) copy-start(f32[5,3,16,256]{3,2,1,0:T(8,128)S(1)} %collective-permute-done.4) | copy-start | bytes 737284
  63.2 8.8 %copy-start.37 = (f32[5,3,16,256]{3,2,1,0:T(8,128)}, f32[5,3,16,256]{3,2,1,0:T(8,128)S(1)}, u32[]{:S(2)}) copy-start(f32[5,3,16,256]{3,2,1,0:T(8,128)S(1)} %collective-permute-done.5) | copy-start | bytes 737284
  63.3 13.6 %collective-permute-start.6 = (f32[5,12,3,256]{3,2,1,0:T(4,128)S(1)}, f32[5,12,3,256]{3,2,1,0:T(4,128)S(1)}, u32[]{:S(2)}, u32[]{:S(2)}) collective-permute-start(f32[5,12,3,256]{3,2,1,0:T(4,128)S(1)} %get-tuple-element.109), channel_id=1, source_target_pairs={{0,1},{2,3},{4,5},{6,7},{8,9},{10,11},{12,13},{14,15},{16,17},{18,... | collective-permute-start | bytes 552968 | tf_op jit(solution)/shard_map/ppermute | solution.py:16
  64.7 12.3 %collective-permute-start.7 = (f32[5,12,3,256]{3,2,1,0:T(4,128)S(1)}, f32[5,12,3,256]{3,2,1,0:T(4,128)S(1)}, u32[]{:S(2)}, u32[]{:S(2)}) collective-permute-start(f32[5,12,3,256]{3,2,1,0:T(4,128)S(1)} %get-tuple-element.110), channel_id=1, source_target_pairs={{1,0},{3,2},{5,4},{7,6},{9,8},{11,10},{13,12},{15,14},{17,16},{19,... | collective-permute-start | bytes 552968 | tf_op jit(solution)/shard_map/ppermute | solution.py:17
  74.1 2.9 copy-start.36
  74.1 2.9 copy-start.38
  74.2 3.2 collective-permute-start.2
  75.7 3.8 collective-permute-start.3
  77.3 3.7 copy-start.4
  77.4 4.1 copy-start.7
  77.4 4.1 copy-start.10
  77.4 4.1 copy-start.13
  77.4 4.1 copy-start.16
  82.5 82.5 %copy-start.30 = (f32[1,6,16,256]{3,2,1,0:T(8,128)}, f32[1,6,16,256]{3,2,1,0:T(8,128)S(1)}, u32[]{:S(2)}) copy-start(f32[1,6,16,256]{3,2,1,0:T(8,128)S(1)} %get-tuple-element.166) | copy-start | bytes 294916
  167.5 16.8 %collective-permute-start.8 = (f32[4,5,16,256]{3,2,1,0:T(8,128)S(1)}, f32[4,5,16,256]{3,2,1,0:T(8,128)S(1)}, u32[]{:S(2)}, u32[]{:S(2)}) collective-permute-start(f32[4,5,16,256]{3,2,1,0:T(8,128)S(1)} %get-tuple-element.133), channel_id=1, source_target_pairs={{0,2},{2,4},{4,6},{6,8},{8,10},{10,12},{12,14},{14,16},{16,18},{18... | collective-permute-start | bytes 983048 | tf_op jit(solution)/shard_map/ppermute | solution.py:16
  171.7 14.5 %collective-permute-start.9 = (f32[4,5,16,256]{3,2,1,0:T(8,128)S(1)}, f32[4,5,16,256]{3,2,1,0:T(8,128)S(1)}, u32[]{:S(2)}, u32[]{:S(2)}) collective-permute-start(f32[4,5,16,256]{3,2,1,0:T(8,128)S(1)} %get-tuple-element.134), channel_id=1, source_target_pairs={{2,0},{4,2},{6,4},{8,6},{10,8},{12,10},{14,12},{16,14},{18,16},{20... | collective-permute-start | bytes 983048 | tf_op jit(solution)/shard_map/ppermute | solution.py:17
  186.4 3.7 collective-permute-start.10
  187.7 3.8 collective-permute-start.11
  194.0 1.0 copy-start.11
  194.0 1.1 copy-start.14
  194.0 1.2 copy-start.17
  239.6 45.7 %copy-start.42 = (f32[2]{0:T(128)}, f32[2]{0:T(128)S(1)}, u32[]{:S(2)}) copy-start(f32[2]{0:T(128)S(1)} %psum.52) | copy-start | bytes 28
  285.3 8.2 %copy-start.43 = (f32[2]{0:T(128)S(1)}, f32[2]{0:T(128)}, u32[]{:S(2)}) copy-start(f32[2]{0:T(128)} %copy-done.42) | copy-start | bytes 28
  287.3 16.6 %collective-permute-start.12 = (f32[4,5,16,256]{3,2,1,0:T(8,128)}, f32[4,5,16,256]{3,2,1,0:T(8,128)}, u32[]{:S(2)}, u32[]{:S(2)}) collective-permute-start(f32[4,5,16,256]{3,2,1,0:T(8,128)} %get-tuple-element.131), channel_id=1, source_target_pairs={{0,2},{2,4},{4,6},{6,8},{8,10},{10,12},{12,14},{14,16},{16,18},{18... | collective-permute-start | bytes 983048 | tf_op jit(solution)/shard_map/ppermute | solution.py:16
  292.3 13.6 %collective-permute-start.13 = (f32[4,5,16,256]{3,2,1,0:T(8,128)}, f32[4,5,16,256]{3,2,1,0:T(8,128)}, u32[]{:S(2)}, u32[]{:S(2)}) collective-permute-start(f32[4,5,16,256]{3,2,1,0:T(8,128)} %get-tuple-element.132), channel_id=1, source_target_pairs={{2,0},{4,2},{6,4},{8,6},{10,8},{12,10},{14,12},{16,14},{18,16},{20... | collective-permute-start | bytes 983048 | tf_op jit(solution)/shard_map/ppermute | solution.py:17
  307.1 3.6 copy-start.1
  307.2 3.5 collective-permute-start.14
  308.5 3.8 collective-permute-start.15
  316.6 1.1 copy-start.15
  316.6 1.2 copy-start.18
  319.9 43.2 %copy-start.41 = (f32[4,3]{0,1:T(4,128)S(1)}, f32[4,3]{0,1:T(4,128)}, u32[]{:S(2)}) copy-start(f32[4,3]{0,1:T(4,128)} %scatter.25) | copy-start | bytes 148
  319.9 46.4 %copy-start.2 = (f32[4,6,16,256]{3,2,1,0:T(8,128)S(1)}, f32[4,6,16,256]{3,2,1,0:T(8,128)}, u32[]{:S(2)}) copy-start(f32[4,6,16,256]{3,2,1,0:T(8,128)} %get-tuple-element.90) | copy-start | bytes 1179652
  322.8 90.4 %copy-start.33 = (f32[1,4,6,16,256]{4,3,2,1,0:T(8,128)S(1)}, f32[1,4,6,16,256]{4,3,2,1,0:T(8,128)}, u32[]{:S(2)}) copy-start(f32[1,4,6,16,256]{4,3,2,1,0:T(8,128)} %fusion.17) | copy-start | bytes 1179652
  322.8 90.4 %copy-start.34 = (f32[1,4,6,16,256]{4,3,2,1,0:T(8,128)S(1)}, f32[1,4,6,16,256]{4,3,2,1,0:T(8,128)}, u32[]{:S(2)}) copy-start(f32[1,4,6,16,256]{4,3,2,1,0:T(8,128)} %fusion.16) | copy-start | bytes 1179652
  411.2 3.0 copy-start.32
  (13 other events, 12.3 us)
where the time goes:
time: 418 us; the launch traced here: 416 us
  blocking collectives  284 us (68%)
  other arithmetic  42.8 us (10%)
  starting transfers between devices  34.4 us (8%)
  waiting for transfers between devices  28.3 us (7%)
  local copies, waits for them, and re-layouts  21.4 us (5%)
  between operations  4.57 us (1%)
    psum x3, blocking collectives, per_device(): norm_next = jnp.sqrt(lax.psum(jnp.sum(image * image), ('slab', 'sub')))  122 us
    psum x3, blocking collectives, per_device(): projected = lax.psum(local_dots(vectors, image), ('slab', 'sub'))  117 us
    psum x1, blocking collectives, per_device(): scale_start = jnp.sqrt(lax.psum(jnp.sum(start * start), ('slab', 'sub')))  44.7 us
    ppermute x8, starting transfers between devices, padded_2(): before = lax.ppermute(last, axis, up)  23.7 us
    ppermute x8, waiting for transfers between devices, padded_2(): before = lax.ppermute(last, axis, up)  17.4 us
    ppermute x8, waiting for transfers between devices, padded_2(): after = lax.ppermute(leading, axis, down)  10.9 us
    ppermute x8, starting transfers between devices, padded_2(): after = lax.ppermute(leading, axis, down)  10.6 us
    reduce_sum x3, other arithmetic, per_device(): norm_next = jnp.sqrt(lax.psum(jnp.sum(image * image), ('slab', 'sub')))  8.42 us
  transfers between devices with their start and end apart: 16, of which 9 were waited for; matrix products, arithmetic and copies ran while one was open for 4% of the time, Pallas kernels for 0%

commit v1 on v0

v1 whole, which is shorter than its diff:
```python
import functools

import jax
import jax.numpy as jnp
from jax import lax
from jax.experimental import pallas as pl
from jax.experimental.pallas import tpu as pltpu
from jax.sharding import PartitionSpec as P

ITERS = 3
AXES = ("slab", "sub")
SHIFTS = (1.5, 5.0, 4.5)
PIVOT_FLOOR = 0.01
PAD = 8


def neighbours(devices):
    up = [(i, i + 1) for i in range(devices - 1)]
    return up, [(j, i) for i, j in up]


def edge_rows(field, axis):
    sub = lax.axis_index("sub")
    start = (1 - sub) * (field.shape[axis] - PAD)
    return lax.dynamic_slice_in_dim(field, start, PAD, axis)


def across(field):
    return lax.ppermute(field, "sub", [(0, 1), (1, 0)])


def extend_coefficients(stacked):
    up, down = neighbours(lax.axis_size("slab"))
    length = stacked.shape[1]
    low = lax.ppermute(stacked[:, length - 3 :], "slab", up)
    high = lax.ppermute(stacked[:, :3], "slab", down)
    tall = jnp.concatenate([low, stacked, high], 1)
    other = across(edge_rows(tall, 2))
    sub = lax.axis_index("sub")
    left = jnp.where(sub == 1, other, 0.0)
    right = jnp.where(sub == 0, other, 0.0)
    return jnp.concatenate([left, tall, right], 2)


def exchange(vector):
    up, down = neighbours(lax.axis_size("slab"))
    length = vector.shape[1]
    last = jnp.concatenate(
        [vector[3, length - 5 :]] + [vector[c, length - 2 :] for c in range(3)], 0
    )
    first = jnp.concatenate([vector[3, :5]] + [vector[c, :2] for c in range(3)], 0)
    low = lax.ppermute(last, "slab", up)
    high = lax.ppermute(first, "slab", down)
    side = across(edge_rows(vector, 2))
    corner = across(edge_rows(jnp.concatenate([low, high], 0), 1))
    return low, high, side, corner


def plane_shifts(center):
    rows, lanes = center.shape
    lane = lax.broadcasted_iota(jnp.int32, center.shape, 1)
    y_plus = pltpu.roll(center, rows - 1, 0)
    y_minus = pltpu.roll(center, 1, 0)
    z_plus = jnp.where(lane == lanes - 1, 0.0, pltpu.roll(center, lanes - 1, 1))
    z_minus = jnp.where(lane == 0, 0.0, pltpu.roll(center, 1, 1))
    return y_plus, y_minus, z_plus, z_minus


def apply_kernel(
    count, shift, slabs, subs, *refs
):
    place, low, high, side, corner, coef, tile_in = refs[:7]
    olds = refs[7 : 7 + count]
    found, new, tile_out = refs[7 + count : 10 + count]
    pres, tee, schur, vel, first, second = refs[10 + count :]
    own = olds[-1]
    cells_x, cells_y, lanes = own.shape[1:]
    rows = cells_y + 2 * PAD
    slab, sub = place[0], place[1]
    is_left = sub == 0

    def put(write, middle, beyond):
        write(slice(PAD, PAD + cells_y), middle)
        write(slice(0, PAD), jnp.where(is_left, 0.0, beyond))
        write(slice(PAD + cells_y, rows), jnp.where(is_left, beyond, 0.0))

    def writer(ref, *lead):
        def write(span, value):
            ref[(*lead, span, slice(None))] = value

        return write

    for i in range(5):
        put(writer(pres, i), low[i], corner[i])
        put(writer(pres, 5 + cells_x + i), high[i], corner[11 + i])
    for c in range(3):
        for i in range(2):
            k = 5 + 2 * c + i
            put(writer(vel, c, i), low[k], corner[k])
            put(writer(vel, c, 2 + cells_x + i), high[k], corner[11 + k])

    @pl.loop(0, cells_x)
    def _(i):
        put(writer(pres, 5 + i), own[3, i], side[3, i])
        for c in range(3):
            put(writer(vel, c, 2 + i), own[c, i], side[c, i])

    row = lax.broadcasted_iota(jnp.int32, (rows, lanes), 0) + (sub * cells_y - PAD)
    inside_y = (row >= 0) & (row < cells_y * subs)

    def inside(i, width):
        x = slab * cells_x - width + i
        good = ((x >= 0) & (x < cells_x * slabs)).astype(jnp.int32)
        return inside_y & (jnp.full((rows, lanes), good, jnp.int32) > 0)

    def transport(center, x_plus, x_minus, shifts, k):
        y_plus, y_minus, z_plus, z_minus = shifts
        total = x_plus + x_minus + y_plus + y_minus + z_plus + z_minus
        convect = coef[0, k] * (x_plus - x_minus) + coef[1, k] * (y_plus - y_minus)
        convect = convect + coef[2, k] * (z_plus - z_minus)
        return (6.0 + coef[3, k]) * center - total + 0.5 * convect

    @pl.loop(0, cells_x + 8)
    def _(i):
        center = pres[i + 1]
        y_plus, y_minus, z_plus, z_minus = plane_shifts(center)
        total = pres[i + 2] + pres[i] + y_plus + y_minus + z_plus + z_minus
        tee[i] = jnp.where(inside(i, 4), center * (1.0 / 7.0) + total * (1.0 / 49.0), 0.0)

    @pl.loop(0, cells_x + 6)
    def _(i):
        center = tee[i + 1]
        value = transport(center, tee[i + 2], tee[i], plane_shifts(center), i)
        schur[i] = jnp.where(inside(i, 3), -value / coef[4, i], 0.0)

    @pl.loop(0, cells_x + 4)
    def _(i):
        center = schur[i + 1]
        y_plus, y_minus, z_plus, z_minus = plane_shifts(center)
        inverse = jnp.where(inside(i, 2), 1.0 / (6.0 + coef[3, i + 1]), 0.0)
        slopes = (schur[i + 2] - schur[i], y_plus - y_minus, z_plus - z_minus)
        for c in range(3):
            residue = vel[c, i] - 0.5 * slopes[c]
            vel[c, i] = residue
            first[c, i] = residue * inverse

    @pl.loop(0, cells_x + 2)
    def _(i):
        inverse = jnp.where(inside(i, 1), 1.0 / (6.0 + coef[3, i + 2]), 0.0)
        for c in range(3):
            center = first[c, i + 1]
            value = transport(
                center, first[c, i + 2], first[c, i], plane_shifts(center), i + 2
            )
            second[c, i] = center + (vel[c, i + 1] - value) * inverse

    mid = slice(PAD, PAD + cells_y)
    zero = jnp.zeros((cells_y, lanes), jnp.float32)

    def last_stage(i, sums):
        q = schur[i + 3]
        q_up, q_down = schur[i + 4], schur[i + 2]
        qy_plus, qy_minus, qz_plus, qz_minus = plane_shifts(q)
        slopes = (q_up - q_down, qy_plus - qy_minus, qz_plus - qz_minus)
        total = q_up + q_down + qy_plus + qy_minus + qz_plus + qz_minus
        div = jnp.zeros_like(q)
        images = []
        for c in range(3):
            center = second[c, i + 1]
            above, below = second[c, i + 2], second[c, i]
            shifts = plane_shifts(center)
            div = div + (above - below, shifts[0] - shifts[1], shifts[2] - shifts[3])[c]
            value = transport(center, above, below, shifts, i + 3)
            images.append(value + 0.5 * slopes[c])
            found[c, i] = center[mid]
        found[3, i] = q[mid]
        images.append(-0.5 * div - 0.5 * (6.0 * q - total))
        sums = list(sums)
        for c in range(4):
            fresh = images[c][mid] - shift * own[c, i]
            new[c, i] = fresh
            for k in range(count):
                sums[k] = sums[k] + fresh * olds[k][c, i]
            sums[count] = sums[count] + fresh * fresh
            if count == 1:
                old = own[c, i]
                sums[2] = sums[2] + old * old
        return tuple(sums)

    sums = lax.fori_loop(
        0, cells_x, last_stage, (zero,) * (count + 1 + (count == 1))
    )
    lane = lax.broadcasted_iota(jnp.int32, (8, 128), 1)
    base = count * (count + 1) // 2
    tile = tile_in[...]
    for k in range(count + 1):
        tile = jnp.where(lane == base + k, jnp.sum(sums[k]), tile)
    if count == 1:
        tile = jnp.where(lane == 0, jnp.sum(sums[2]), tile)
    tile_out[...] = tile


def apply_both(olds, coef, tile, shift):
    own = olds[-1]
    cells_x, cells_y, lanes = own.shape[1:]
    rows = cells_y + 2 * PAD
    low, high, side, corner = exchange(own)
    place = jnp.stack([lax.axis_index("slab"), lax.axis_index("sub")]).astype(jnp.int32)
    whole = pl.BlockSpec(memory_space=pltpu.VMEM)
    f32 = jnp.float32
    return pl.pallas_call(
        functools.partial(
            apply_kernel, len(olds), shift, lax.axis_size("slab"), lax.axis_size("sub")
        ),
        name=f"apply_{len(olds)}",
        in_specs=[pl.BlockSpec(memory_space=pltpu.SMEM)] + [whole] * (6 + len(olds)),
        out_specs=[whole] * 3,
        out_shape=[
            jax.ShapeDtypeStruct(own.shape, f32),
            jax.ShapeDtypeStruct(own.shape, f32),
            jax.ShapeDtypeStruct((8, 128), f32),
        ],
        scratch_shapes=[
            pltpu.VMEM((cells_x + 10, rows, lanes), f32),
            pltpu.VMEM((cells_x + 8, rows, lanes), f32),
            pltpu.VMEM((cells_x + 6, rows, lanes), f32),
            pltpu.VMEM((3, cells_x + 4, rows, lanes), f32),
            pltpu.VMEM((3, cells_x + 4, rows, lanes), f32),
            pltpu.VMEM((3, cells_x + 2, rows, lanes), f32),
        ],
        compiler_params=pltpu.CompilerParams(vmem_limit_bytes=56 * 1024 * 1024),
    )(place, low, high, side, corner, coef, tile, *olds)


def combine_kernel(*refs):
    parts = refs[0]
    vectors, founds = refs[1:5], refs[5:8]
    basis, search, small = refs[8:]
    total = jnp.sum(parts[...], axis=0)[0:1]
    lane = lax.broadcasted_iota(jnp.int32, (1, 128), 1)

    def gram(a, b):
        a, b = max(a, b), min(a, b)
        at = a * (a + 1) // 2 + b
        return jnp.sum(jnp.where(lane == at, total, 0.0), axis=1, keepdims=True)

    n = ITERS + 1
    upper, share = {}, None
    for j in range(n):
        for i in range(j):
            value = gram(i, j)
            for k in range(i):
                value = value - upper[k, i] * upper[k, j]
            upper[i, j] = value / upper[i, i]
        full = gram(j, j)
        left = full
        for k in range(j):
            left = left - upper[k, j] * upper[k, j]
        share = left / full if share is None else jnp.minimum(share, left / full)
        upper[j, j] = jnp.sqrt(left)
    inverse = {}
    for j in range(n):
        inverse[j, j] = 1.0 / upper[j, j]
        for i in range(j - 1, -1, -1):
            value = upper[i, i + 1] * inverse[i + 1, j]
            for k in range(i + 2, j + 1):
                value = value + upper[i, k] * inverse[k, j]
            inverse[i, j] = -value / upper[i, i]
    rows = lax.broadcasted_iota(jnp.int32, (8, 128), 0)
    lanes = lax.broadcasted_iota(jnp.int32, (8, 128), 1)
    tile = jnp.where(rows == 7, share, 0.0)
    for j in range(ITERS):
        for i in range(j + 2):
            value = None
            for k in range(max(i - 1, 0), j + 1):
                moved = upper[i, k + 1]
                if i <= k:
                    moved = moved + SHIFTS[k] * upper[i, k]
                term = moved * inverse[k, j]
                value = term if value is None else value + term
            tile = jnp.where((rows == i) & (lanes == j), value, tile)
    small[...] = tile

    @pl.loop(0, vectors[0].shape[1])
    def _(x):
        for c in range(4):
            for count, sources, target in ((n, vectors, basis), (ITERS, founds, search)):
                planes = [source[c, x] for source in sources]
                for j in range(count):
                    value = planes[0] * inverse[0, j]
                    for i in range(1, j + 1):
                        value = value + planes[i] * inverse[i, j]
                    target[j, c, x] = value


def step_by_step(start, coef):
    def total(value):
        return lax.psum(jnp.sum(value), AXES)

    blank = jnp.zeros((8, 128), jnp.float32)
    vectors = [start / jnp.sqrt(total(start * start))]
    searches = []
    hess = jnp.zeros((8, 128), jnp.float32)
    for column in range(ITERS):
        found, image, _ = apply_both([vectors[column]], coef, blank, 0.0)
        searches.append(found)
        projected = [total(vector * image) for vector in vectors]
        for row in range(column + 1):
            image = image - projected[row] * vectors[row]
            hess = hess.at[row, column].set(projected[row])
        norm_next = jnp.sqrt(total(image * image))
        hess = hess.at[column + 1, column].set(norm_next)
        vectors.append(image / norm_next)
    return jnp.stack(vectors), jnp.stack(searches), hess


def per_device(start, wind, reaction, mass):
    coef = extend_coefficients(jnp.concatenate([wind, reaction[None], mass[None]], 0))
    tile = jnp.zeros((8, 128), jnp.float32)
    vectors, founds = [start], []
    for column in range(ITERS):
        found, fresh, tile = apply_both(vectors, coef, tile, SHIFTS[column])
        founds.append(found)
        vectors.append(fresh)
    devices = lax.axis_size("slab") * lax.axis_size("sub")
    parts = lax.all_to_all(jnp.broadcast_to(tile[None], (devices, 8, 128)), AXES, 0, 0)
    whole = pl.BlockSpec(memory_space=pltpu.VMEM)
    basis, search, small = pl.pallas_call(
        combine_kernel,
        name="combine",
        in_specs=[whole] * 8,
        out_specs=[whole] * 3,
        out_shape=[
            jax.ShapeDtypeStruct((ITERS + 1,) + start.shape, jnp.float32),
            jax.ShapeDtypeStruct((ITERS,) + start.shape, jnp.float32),
            jax.ShapeDtypeStruct((8, 128), jnp.float32),
        ],
        compiler_params=pltpu.CompilerParams(vmem_limit_bytes=56 * 1024 * 1024),
    )(parts, *vectors, *founds)

    def body(state):
        basis, search, hess = step_by_step(start, coef)
        return basis, search, hess.at[7, 0].set(1.0)

    basis, search, small = lax.while_loop(
        lambda state: jnp.logical_not(state[2][7, 0] >= PIVOT_FLOOR),
        body,
        (basis, search, small),
    )
    return basis, search, small[: ITERS + 1, :ITERS]


def solution(mesh):
    return jax.shard_map(
        per_device,
        mesh=mesh,
        in_specs=(
            P(None, "slab", "sub", None),
            P(None, "slab", "sub", None),
            P("slab", "sub", None),
            P("slab", "sub", None),
        ),
        out_specs=(P(None, None, "slab", "sub", None), P(None, None, "slab", "sub", None), P()),
        check_vma=False,
    )
```

time: 418 us -> 450 us (1.077)
  Pallas kernels: 0 us -> 48.3 us
  other arithmetic: 42.8 us -> 18.5 us
  starting transfers between devices: 34.4 us -> 50 us
    pallas_call x0 -> x7, Pallas kernels: none -> 48.3 us  [the longest x6 44.6 us: apply_both(): pl.pallas_call(functools.partial(apply_kernel, len(olds), shift, lax.axis...]
    another operation x23 -> x1, other arithmetic: 17.4 us -> 0.61 us  [apply_both(): jnp.stack([lax.axis_index('slab'), lax.axis_index('sub')]).astype(jnp.int32)]
    ppermute x16 -> x27, starting transfers between devices: 34.4 us -> 44.7 us  [the longest x6 29.4 us: exchange(): low = lax.ppermute(last, 'slab', up)]
    scatter x6 -> x0, local copies, waits for them, and re-layouts: 7.94 us -> none  [the longest x3 5.11 us: per_device(): hess = hess.at[:column + 1, column].set(projected)]
    all_to_all x0 -> x1, starting transfers between devices: none -> 5.29 us  [per_device(): lax.all_to_all(jnp.broadcast_to(tile[None], (devices, 8, 128)), AXES, 0, 0)]
    squeeze x0 -> x12, local copies, waits for them, and re-layouts: none -> 4.52 us  [the longest x6 2.52 us: exchange(): vector[c, :2]]
    ppermute x16 -> x27, waiting for transfers between devices: 28.3 us -> 24.5 us  [the longest x1 9.05 us: extend_coefficients(): low = lax.ppermute(stacked[:, length - 3:], 'slab', up)]
  transfers between devices with their start and end apart: 16 -> 28, of which waited for: 9 -> 8; matrix products, arithmetic and copies ran while one was open for 4% -> 5% of each run, Pallas kernels for 0% -> 7%
where the time goes in v1:
time: 450 us; the launch traced here: 448 us
  blocking collectives  285 us (63%)
  starting transfers between devices  50 us (11%)
  Pallas kernels  48.3 us (11%)
  waiting for transfers between devices  24.5 us (5%)
  other arithmetic  18.5 us (4%)
  local copies, waits for them, and re-layouts  17 us (4%)
    psum x7, blocking collectives, total(): return lax.psum(jnp.sum(value), AXES)  285 us
    pallas_call x6, Pallas kernels, apply_both(): pl.pallas_call(functools.partial(apply_kernel, len(olds), shift, lax.axis...  44.6 us
    ppermute x6, starting transfers between devices, exchange(): low = lax.ppermute(last, 'slab', up)  29.4 us
    reduce_sum x7, other arithmetic, total(): return lax.psum(jnp.sum(value), AXES)  14.2 us
    ppermute x1, waiting for transfers between devices, extend_coefficients(): low = lax.ppermute(stacked[:, length - 3:], 'slab', up)  9.05 us
  transfers between devices with their start and end apart: 28, of which 8 were waited for; matrix products, arithmetic and copies ran while one was open for 5% of the time, Pallas kernels for 7%

profile of v1, /device:TPU:0, one launch (start us, length us, event | category | flops | bytes accessed | tf_op | source)
XLA Modules:
  0.0 448.0 jit_solution(15127509274137280346)
XLA Ops:
  0.7 1.8 multiply_reduce_fusion.9
  2.4 42.2 %psum.143 = f32[]{:T(128)} all-reduce(f32[]{:T(128)} %multiply_reduce_fusion.9), channel_id=1, replica_groups=mesh['slab'=16,'sub'=2] {'slab','sub'}, use_global_device_ids=true, to_apply=%region_1.0 | all-reduce | flops 1 | bytes 8 | tf_op jit(solution)/shard_map/while/body/psum | solution.py:298
  45.3 1.0 broadcast_divide_fusion.3.refs_7_
  46.4 4.3 collective-permute-start.27
  50.8 1.3 collective-permute-start.28
  52.2 4.6 %collective-permute-start.16 = (f32[5,3,16,256]{3,2,1,0:T(8,128)S(1)}, f32[5,3,16,256]{3,2,1,0:T(8,128)S(1)}, u32[]{:S(2)}, u32[]{:S(2)}) collective-permute-start(f32[5,3,16,256]{3,2,1,0:T(8,128)S(1)} %get-tuple-element.546), channel_id=1, source_target_pairs={{0,2},{2,4},{4,6},{6,8},{8,10},{10,12},{12,14},{14,16},{16,18},{18... | collective-permute-start | bytes 737288 | tf_op jit(solution)/shard_map/ppermute | solution.py:35
  56.7 1.3 collective-permute-start.17
  59.5 9.0 %collective-permute-done.16 = f32[5,3,16,256]{3,2,1,0:T(8,128)S(1)} collective-permute-done((f32[5,3,16,256]{3,2,1,0:T(8,128)S(1)}, f32[5,3,16,256]{3,2,1,0:T(8,128)S(1)}, u32[]{:S(2)}, u32[]{:S(2)}) %collective-permute-start.16) | collective-permute-done | bytes 245792 | tf_op jit(solution)/shard_map/ppermute | solution.py:35
  68.6 1.0 collective-permute-done.17
  71.8 1.3 collective-permute-start.13
  73.1 4.6 %collective-permute-start.12 = (f32[11,16,256]{2,1,0:T(8,128)S(1)}, f32[11,16,256]{2,1,0:T(8,128)S(1)}, u32[]{:S(2)}, u32[]{:S(2)}) collective-permute-start(f32[11,16,256]{2,1,0:T(8,128)S(1)} %pad_maximum_fusion.10), channel_id=1, source_target_pairs={{0,2},{2,4},{4,6},{6,8},{8,10},{10,12},{12,14},{14,16},{16,18},{18... | collective-permute-start | bytes 540680 | tf_op jit(solution)/shard_map/ppermute | solution.py:52
  79.8 7.4 %apply_1.29 = (f32[4,6,16,256]{3,2,1,0:T(8,128)}, f32[4,6,16,256]{3,2,1,0:T(8,128)}, f32[8,128]{1,0:T(8,128)}) custom-call(s32[2]{0:T(128)} %pad_add_fusion.1.refs_0_, f32[11,16,256]{2,1,0:T(8,128)} %copy-done.35, f32[11,16,256]{2,1,0:T(8,128)} %copy-done.36, f32[4,6,8,256]{3,2,1,0:T(8,128)} %collective-permute-done.29.refs_3_, f32[22,8,256]{2,1,0:T(8,128)} %copy-done.50, ...), custom_call_target="tpu_custom_call" | custom-call | tf_op jit(solution)/shard_map/while/body/apply_1/pallas_call | solution.py:211
  87.3 1.8 multiply_reduce_fusion.8
  89.8 40.2 %psum.144 = f32[]{:T(128)} all-reduce(f32[]{:T(128)} %multiply_reduce_fusion.8), channel_id=1, replica_groups=mesh['slab'=16,'sub'=2] {'slab','sub'}, use_global_device_ids=true, to_apply=%region_3.0 | all-reduce | flops 1 | bytes 8 | tf_op jit(solution)/shard_map/while/body/psum | solution.py:298
  130.0 1.4 multiply_reduce_fusion.7
  131.3 40.4 %psum.145 = f32[]{:T(128)} all-reduce(f32[]{:T(128)} %multiply_reduce_fusion.7), channel_id=1, replica_groups=mesh['slab'=16,'sub'=2] {'slab','sub'}, use_global_device_ids=true, to_apply=%region_5.0 | all-reduce | flops 1 | bytes 8 | tf_op jit(solution)/shard_map/while/body/psum | solution.py:298
  174.0 7.3 %apply_1.28 = (f32[4,6,16,256]{3,2,1,0:T(8,128)}, f32[4,6,16,256]{3,2,1,0:T(8,128)}, f32[8,128]{1,0:T(8,128)}) custom-call(s32[2]{0:T(128)} %pad_add_fusion.1.refs_0_, f32[11,16,256]{2,1,0:T(8,128)} %copy-done.40, f32[11,16,256]{2,1,0:T(8,128)} %copy-done.38, f32[4,6,8,256]{3,2,1,0:T(8,128)} %copy-done.47, f32[22,8,256]{2,1,0:T(8,128)} %collective-permute-done.15.refs_4_, ...), custom_call_target="tpu_custom_call" | custom-call | tf_op jit(solution)/shard_map/apply_1/pallas_call | solution.py:211
  182.2 1.0 slice_bitcast_fusion.32
  183.2 1.3 collective-permute-start.32
  184.5 4.8 %collective-permute-start.31 = (f32[11,16,256]{2,1,0:T(8,128)S(1)}, f32[11,16,256]{2,1,0:T(8,128)S(1)}, u32[]{:S(2)}, u32[]{:S(2)}) collective-permute-start(f32[11,16,256]{2,1,0:T(8,128)S(1)} %pad_maximum_fusion.18), channel_id=1, source_target_pairs={{0,2},{2,4},{4,6},{6,8},{8,10},{10,12},{12,14},{14,16},{16,18},{18... | collective-permute-start | bytes 540680 | tf_op jit(solution)/shard_map/while/body/ppermute | solution.py:52
  189.4 1.3 collective-permute-start.20
  190.8 5.4 %collective-permute-start.19 = (f32[11,16,256]{2,1,0:T(8,128)S(1)}, f32[11,16,256]{2,1,0:T(8,128)S(1)}, u32[]{:S(2)}, u32[]{:S(2)}) collective-permute-start(f32[11,16,256]{2,1,0:T(8,128)S(1)} %pad_maximum_fusion.12), channel_id=1, source_target_pairs={{0,2},{2,4},{4,6},{6,8},{8,10},{10,12},{12,14},{14,16},{16,18},{18... | collective-permute-start | bytes 540680 | tf_op jit(solution)/shard_map/ppermute | solution.py:52
  197.5 2.0 collective-permute-done.20.refs_2_
  199.5 5.0 %collective-permute-done.19.refs_1_ = f32[11,16,256]{2,1,0:T(8,128)S(1)} collective-permute-done((f32[11,16,256]{2,1,0:T(8,128)S(1)}, f32[11,16,256]{2,1,0:T(8,128)S(1)}, u32[]{:S(2)}, u32[]{:S(2)}) %collective-permute-start.19) | collective-permute-done | bytes 180256 | tf_op jit(solution)/shard_map/ppermute | solution.py:52
  207.2 7.4 %apply_1.30 = (f32[4,6,16,256]{3,2,1,0:T(8,128)}, f32[4,6,16,256]{3,2,1,0:T(8,128)}, f32[8,128]{1,0:T(8,128)}) custom-call(s32[2]{0:T(128)} %pad_add_fusion.1.refs_0_, f32[11,16,256]{2,1,0:T(8,128)} %copy-done.44, f32[11,16,256]{2,1,0:T(8,128)} %copy-done.43, f32[4,6,8,256]{3,2,1,0:T(8,128)} %copy-done.48, f32[22,8,256]{2,1,0:T(8,128)} %copy-done.51, ...), custom_call_target="tpu_custom_call" | custom-call | tf_op jit(solution)/shard_map/while/body/apply_1/pallas_call | solution.py:211
  214.6 1.7 multiply_reduce_fusion.5
  216.3 40.6 %all-reduce.2 = (f32[]{:T(128)}, f32[]{:T(128)}) all-reduce(f32[]{:T(128)} %get-tuple-element.475, f32[]{:T(128)} %get-tuple-element.474), channel_id=1, replica_groups=mesh['slab'=16,'sub'=2] {'slab','sub'}, use_global_device_ids=true, to_apply=%region_7.0 | all-reduce | flops 2 | bytes 16 | tf_op jit(solution)/shard_map/while/body/psum | solution.py:298
  256.9 3.0 multiply_reduce_fusion.4
  259.9 40.2 %psum.148 = f32[]{:T(128)} all-reduce(f32[]{:T(128)} %get-tuple-element.513), channel_id=1, replica_groups=mesh['slab'=16,'sub'=2] {'slab','sub'}, use_global_device_ids=true, to_apply=%region_11.0 | all-reduce | flops 1 | bytes 8 | tf_op jit(solution)/shard_map/while/body/psum | solution.py:298
  300.9 7.5 %apply_2.1 = (f32[4,6,16,256]{3,2,1,0:T(8,128)}, f32[4,6,16,256]{3,2,1,0:T(8,128)}, f32[8,128]{1,0:T(8,128)}) custom-call(s32[2]{0:T(128)} %pad_add_fusion.1.refs_0_, f32[11,16,256]{2,1,0:T(8,128)} %copy-done.42, f32[11,16,256]{2,1,0:T(8,128)} %copy-done.39, f32[4,6,8,256]{3,2,1,0:T(8,128)} %collective-permute-done.21.refs_3_, ...), custom_call_target="tpu_custom_call" | custom-call | tf_op jit(solution)/shard_map/apply_2/pallas_call | solution.py:211
  310.4 1.3 collective-permute-start.36
  311.7 4.8 %collective-permute-start.35 = (f32[11,16,256]{2,1,0:T(8,128)S(1)}, f32[11,16,256]{2,1,0:T(8,128)S(1)}, u32[]{:S(2)}, u32[]{:S(2)}) collective-permute-start(f32[11,16,256]{2,1,0:T(8,128)S(1)} %pad_maximum_fusion.20), channel_id=1, source_target_pairs={{0,2},{2,4},{4,6},{6,8},{8,10},{10,12},{12,14},{14,16},{16,18},{18... | collective-permute-start | bytes 540680 | tf_op jit(solution)/shard_map/while/body/ppermute | solution.py:52
  316.5 1.3 collective-permute-start.24
  317.8 5.4 %collective-permute-start.23 = (f32[11,16,256]{2,1,0:T(8,128)S(1)}, f32[11,16,256]{2,1,0:T(8,128)S(1)}, u32[]{:S(2)}, u32[]{:S(2)}) collective-permute-start(f32[11,16,256]{2,1,0:T(8,128)S(1)} %pad_maximum_fusion.14), channel_id=1, source_target_pairs={{0,2},{2,4},{4,6},{6,8},{8,10},{10,12},{12,14},{14,16},{16,18},{18... | collective-permute-start | bytes 540680 | tf_op jit(solution)/shard_map/ppermute | solution.py:52
  324.1 3.9 collective-permute-done.24.refs_2_
  328.0 2.2 collective-permute-done.23.refs_1_
  332.4 7.6 %apply_3.1 = (f32[4,6,16,256]{3,2,1,0:T(8,128)}, f32[4,6,16,256]{3,2,1,0:T(8,128)}, f32[8,128]{1,0:T(8,128)}) custom-call(s32[2]{0:T(128)} %pad_add_fusion.1.refs_0_, f32[11,16,256]{2,1,0:T(8,128)} %copy-done.34, f32[11,16,256]{2,1,0:T(8,128)} %copy-done.33, f32[4,6,8,256]{3,2,1,0:T(8,128)} %copy-done.45, f32[22,8,256]{2,1,0:T(8,128)} %copy-done.49, ...), custom_call_target="tpu_custom_call" | custom-call | tf_op jit(solution)/shard_map/apply_3/pallas_call | solution.py:211
  339.9 1.3 broadcast_in_dim.20
  341.3 5.3 %all-to-all-start = ((f32[32,8,128]{2,1,0:T(8,128)}), f32[32,8,128]{2,1,0:T(8,128)}, u32[]{:S(2)}, u32[]{:S(2)}) async-start(f32[32,8,128]{2,1,0:T(8,128)} %broadcast_in_dim.20), calls=%async_computation | async-start | bytes 262144 | tf_op jit(solution)/shard_map/all_to_all | solution.py:326
  347.3 7.4 %apply_1.31 = (f32[4,6,16,256]{3,2,1,0:T(8,128)}, f32[4,6,16,256]{3,2,1,0:T(8,128)}, f32[8,128]{1,0:T(8,128)}) custom-call(s32[2]{0:T(128)} %pad_add_fusion.1.refs_0_, f32[11,16,256]{2,1,0:T(8,128)} %copy-done.41, f32[11,16,256]{2,1,0:T(8,128)} %copy-done.37, f32[4,6,8,256]{3,2,1,0:T(8,128)} %copy-done.46, f32[22,8,256]{2,1,0:T(8,128)} %collective-permute-done.38.refs_4_, ...), custom_call_target="tpu_custom_call" | custom-call | tf_op jit(solution)/shard_map/while/body/apply_1/pallas_call | solution.py:211
  354.7 1.9 multiply_reduce_fusion.1
  356.6 40.8 %all-reduce.1 = (f32[]{:T(128)}, f32[]{:T(128)}, f32[]{:T(128)}) all-reduce(f32[]{:T(128)} %get-tuple-element.473, f32[]{:T(128)} %get-tuple-element.472, f32[]{:T(128)} %get-tuple-element.471), channel_id=1, replica_groups=mesh['slab'=16,'sub'=2] {'slab','sub'}, use_global_device_ids=true, to_apply=%region_13.0 | all-reduce | flops 3 | bytes 24 | tf_op jit(solution)/shard_map/while/body/psum | solution.py:298
  397.4 2.7 multiply_reduce_fusion
  400.1 40.5 %psum.152 = f32[]{:T(128)} all-reduce(f32[]{:T(128)} %multiply_reduce_fusion), channel_id=1, replica_groups=mesh['slab'=16,'sub'=2] {'slab','sub'}, use_global_device_ids=true, to_apply=%region_19.0 | all-reduce | flops 1 | bytes 8 | tf_op jit(solution)/shard_map/while/body/psum | solution.py:298
  441.3 3.7 combine.1
  445.0 1.7 while.28
  445.0 1.2 slice.831
  446.7 1.3 slice.702
  (155 shorter events, 18.7 us)
Async XLA Ops:
  0.6 51.4 %copy-start.31 = (f32[6,16,256]{2,1,0:T(8,128)S(1)}, f32[6,16,256]{2,1,0:T(8,128)}, u32[]{:S(2)}) copy-start(f32[6,16,256]{2,1,0:T(8,128)} %param.28) | copy-start | bytes 294916
  0.6 51.4 %copy-start.29 = (f32[6,16,256]{2,1,0:T(8,128)S(1)}, f32[6,16,256]{2,1,0:T(8,128)}, u32[]{:S(2)}) copy-start(f32[6,16,256]{2,1,0:T(8,128)} %param.29) | copy-start | bytes 294916
  0.7 51.4 %copy-start.27 = (f32[3,6,16,256]{3,2,1,0:T(8,128)S(1)}, f32[3,6,16,256]{3,2,1,0:T(8,128)}, u32[]{:S(2)}) copy-start(f32[3,6,16,256]{3,2,1,0:T(8,128)} %param.27) | copy-start | bytes 884740
  46.3 12.4 %copy-start.21 = (f32[4,6,16,256]{3,2,1,0:T(8,128)}, f32[4,6,16,256]{3,2,1,0:T(8,128)S(1)}, u32[]{:S(2)}) copy-start(f32[4,6,16,256]{3,2,1,0:T(8,128)S(1)} %broadcast_divide_fusion.3.refs_7_) | copy-start | bytes 1179652
  46.4 11.7 %copy-start = (f32[4,6,16,256]{3,2,1,0:T(8,128)S(1)}, f32[4,6,16,256]{3,2,1,0:T(8,128)}, u32[]{:S(2)}) copy-start(f32[4,6,16,256]{3,2,1,0:T(8,128)} %refs_1_.1) | copy-start | bytes 1179652
  46.4 26.6 %collective-permute-start.27 = (f32[11,16,256]{2,1,0:T(8,128)S(1)}, f32[11,16,256]{2,1,0:T(8,128)S(1)}, u32[]{:S(2)}, u32[]{:S(2)}) collective-permute-start(f32[11,16,256]{2,1,0:T(8,128)S(1)} %pad_maximum_fusion.16), channel_id=1, source_target_pairs={{0,2},{2,4},{4,6},{6,8},{8,10},{10,12},{12,14},{14,16},{16,18},{18... | collective-permute-start | bytes 540680 | tf_op jit(solution)/shard_map/while/body/ppermute | solution.py:52
  50.8 26.9 %collective-permute-start.28 = (f32[11,16,256]{2,1,0:T(8,128)S(1)}, f32[11,16,256]{2,1,0:T(8,128)S(1)}, u32[]{:S(2)}, u32[]{:S(2)}) collective-permute-start(f32[11,16,256]{2,1,0:T(8,128)S(1)} %pad_maximum_fusion.17), channel_id=1, source_target_pairs={{2,0},{4,2},{6,4},{8,6},{10,8},{12,10},{14,12},{16,14},{18,16},{20... | collective-permute-start | bytes 540680 | tf_op jit(solution)/shard_map/while/body/ppermute | solution.py:53
  52.2 16.4 %collective-permute-start.16 = (f32[5,3,16,256]{3,2,1,0:T(8,128)S(1)}, f32[5,3,16,256]{3,2,1,0:T(8,128)S(1)}, u32[]{:S(2)}, u32[]{:S(2)}) collective-permute-start(f32[5,3,16,256]{3,2,1,0:T(8,128)S(1)} %get-tuple-element.546), channel_id=1, source_target_pairs={{0,2},{2,4},{4,6},{6,8},{8,10},{10,12},{12,14},{14,16},{16,18},{18... | collective-permute-start | bytes 737288 | tf_op jit(solution)/shard_map/ppermute | solution.py:35
  56.7 12.8 %collective-permute-start.17 = (f32[5,3,16,256]{3,2,1,0:T(8,128)S(1)}, f32[5,3,16,256]{3,2,1,0:T(8,128)S(1)}, u32[]{:S(2)}, u32[]{:S(2)}) collective-permute-start(f32[5,3,16,256]{3,2,1,0:T(8,128)S(1)} %get-tuple-element.545), channel_id=1, source_target_pairs={{2,0},{4,2},{6,4},{8,6},{10,8},{12,10},{14,12},{16,14},{18,16},{20... | collective-permute-start | bytes 737288 | tf_op jit(solution)/shard_map/ppermute | solution.py:36
  58.7 11.0 %copy-start.53 = (f32[2,16,256]{2,1,0:T(8,128)S(1)}, f32[2,16,256]{2,1,0:T(8,128)}, u32[]{:S(2)}) copy-start(f32[2,16,256]{2,1,0:T(8,128)} %get-tuple-element.589) | copy-start | bytes 98308
  58.7 11.0 %copy-start.54 = (f32[2,16,256]{2,1,0:T(8,128)S(1)}, f32[2,16,256]{2,1,0:T(8,128)}, u32[]{:S(2)}) copy-start(f32[2,16,256]{2,1,0:T(8,128)} %get-tuple-element.590) | copy-start | bytes 98308
  58.7 11.0 %copy-start.55 = (f32[2,16,256]{2,1,0:T(8,128)S(1)}, f32[2,16,256]{2,1,0:T(8,128)}, u32[]{:S(2)}) copy-start(f32[2,16,256]{2,1,0:T(8,128)} %get-tuple-element.591) | copy-start | bytes 98308
  59.4 11.0 %copy-start.52 = (f32[2,16,256]{2,1,0:T(8,128)S(1)}, f32[2,16,256]{2,1,0:T(8,128)}, u32[]{:S(2)}) copy-start(f32[2,16,256]{2,1,0:T(8,128)} %get-tuple-element.594) | copy-start | bytes 98308
  59.4 19.2 %collective-permute-start.29 = (f32[4,6,8,256]{3,2,1,0:T(8,128)}, f32[4,6,8,256]{3,2,1,0:T(8,128)}, u32[]{:S(2)}, u32[]{:S(2)}) collective-permute-start(f32[4,6,8,256]{3,2,1,0:T(8,128)} %constant_dynamic-slice_fusion.5), channel_id=1, source_target_pairs={{0,1},{1,0},{2,3},{3,2},{4,5},{5,4},{6,7},{7,6},{8,9},{9,8},{10,11... | collective-permute-start | bytes 589832 | tf_op jit(solution)/shard_map/while/body/ppermute | solution.py:29
  69.6 8.1 %collective-permute-start.18 = (f32[5,12,8,256]{3,2,1,0:T(8,128)S(1)}, f32[5,12,8,256]{3,2,1,0:T(8,128)S(1)}, u32[]{:S(2)}, u32[]{:S(2)}) collective-permute-start(f32[5,12,8,256]{3,2,1,0:T(8,128)S(1)} %fusion.4), channel_id=1, source_target_pairs={{0,1},{1,0},{2,3},{3,2},{4,5},{5,4},{6,7},{7,6},{8,9},{9,8},{10,11... | collective-permute-start | bytes 1474568 | tf_op jit(solution)/shard_map/ppermute | solution.py:29
  71.8 17.3 %collective-permute-start.13 = (f32[11,16,256]{2,1,0:T(8,128)}, f32[11,16,256]{2,1,0:T(8,128)S(1)}, u32[]{:S(2)}, u32[]{:S(2)}) collective-permute-start(f32[11,16,256]{2,1,0:T(8,128)} %pad_maximum_fusion.11), channel_id=1, source_target_pairs={{2,0},{4,2},{6,4},{8,6},{10,8},{12,10},{14,12},{16,14},{18,16},{20... | collective-permute-start | bytes 540680 | tf_op jit(solution)/shard_map/ppermute | solution.py:53
  73.1 16.0 %collective-permute-start.12 = (f32[11,16,256]{2,1,0:T(8,128)S(1)}, f32[11,16,256]{2,1,0:T(8,128)S(1)}, u32[]{:S(2)}, u32[]{:S(2)}) collective-permute-start(f32[11,16,256]{2,1,0:T(8,128)S(1)} %pad_maximum_fusion.10), channel_id=1, source_target_pairs={{0,2},{2,4},{4,6},{6,8},{8,10},{10,12},{12,14},{14,16},{16,18},{18... | collective-permute-start | bytes 540680 | tf_op jit(solution)/shard_map/ppermute | solution.py:52
  77.7 1.5 collective-permute-start.30
  78.5 94.8 %collective-permute-start.14 = (f32[4,6,8,256]{3,2,1,0:T(8,128)}, f32[4,6,8,256]{3,2,1,0:T(8,128)S(1)}, u32[]{:S(2)}, u32[]{:S(2)}) collective-permute-start(f32[4,6,8,256]{3,2,1,0:T(8,128)} %constant_dynamic-slice_fusion.8), channel_id=1, source_target_pairs={{0,1},{1,0},{2,3},{3,2},{4,5},{5,4},{6,7},{7,6},{8,9},{9,8},{10,11... | collective-permute-start | bytes 589832 | tf_op jit(solution)/shard_map/ppermute | solution.py:29
  87.3 42.7 %copy-start.26 = (f32[4,6,16,256]{3,2,1,0:T(8,128)S(1)}, f32[4,6,16,256]{3,2,1,0:T(8,128)}, u32[]{:S(2)}) copy-start(f32[4,6,16,256]{3,2,1,0:T(8,128)} %get-tuple-element.465) | copy-start | bytes 1179652
  89.0 82.7 %copy-start.38 = (f32[11,16,256]{2,1,0:T(8,128)}, f32[11,16,256]{2,1,0:T(8,128)S(1)}, u32[]{:S(2)}) copy-start(f32[11,16,256]{2,1,0:T(8,128)S(1)} %collective-permute-done.13.refs_2_) | copy-start | bytes 540676
  131.3 42.0 %collective-permute-start.15 = (f32[22,8,256]{2,1,0:T(8,128)S(1)}, f32[22,8,256]{2,1,0:T(8,128)}, u32[]{:S(2)}, u32[]{:S(2)}) collective-permute-start(f32[22,8,256]{2,1,0:T(8,128)S(1)} %fusion.12), channel_id=1, source_target_pairs={{0,1},{1,0},{2,3},{3,2},{4,5},{5,4},{6,7},{7,6},{8,9},{9,8},{10,11... | collective-permute-start | bytes 540680 | tf_op jit(solution)/shard_map/ppermute | solution.py:29
  181.3 15.3 %copy-start.17 = (f32[4,6,16,256]{3,2,1,0:T(8,128)S(1)}, f32[4,6,16,256]{3,2,1,0:T(8,128)}, u32[]{:S(2)}) copy-start(f32[4,6,16,256]{3,2,1,0:T(8,128)} %get-tuple-element.453.refs_8_.refs_2_) | copy-start | bytes 1179652
  183.2 13.0 %collective-permute-start.32 = (f32[11,16,256]{2,1,0:T(8,128)S(1)}, f32[11,16,256]{2,1,0:T(8,128)S(1)}, u32[]{:S(2)}, u32[]{:S(2)}) collective-permute-start(f32[11,16,256]{2,1,0:T(8,128)S(1)} %pad_maximum_fusion.19), channel_id=1, source_target_pairs={{2,0},{4,2},{6,4},{8,6},{10,8},{12,10},{14,12},{16,14},{18,16},{20... | collective-permute-start | bytes 540680 | tf_op jit(solution)/shard_map/while/body/ppermute | solution.py:53
  184.5 11.7 %collective-permute-start.31 = (f32[11,16,256]{2,1,0:T(8,128)S(1)}, f32[11,16,256]{2,1,0:T(8,128)S(1)}, u32[]{:S(2)}, u32[]{:S(2)}) collective-permute-start(f32[11,16,256]{2,1,0:T(8,128)S(1)} %pad_maximum_fusion.18), channel_id=1, source_target_pairs={{0,2},{2,4},{4,6},{6,8},{8,10},{10,12},{12,14},{14,16},{16,18},{18... | collective-permute-start | bytes 540680 | tf_op jit(solution)/shard_map/while/body/ppermute | solution.py:52
  189.3 16.5 %collective-permute-start.33 = (f32[4,6,8,256]{3,2,1,0:T(8,128)S(1)}, f32[4,6,8,256]{3,2,1,0:T(8,128)S(1)}, u32[]{:S(2)}, u32[]{:S(2)}) collective-permute-start(f32[4,6,8,256]{3,2,1,0:T(8,128)S(1)} %constant_dynamic-slice_fusion.4), channel_id=1, source_target_pairs={{0,1},{1,0},{2,3},{3,2},{4,5},{5,4},{6,7},{7,6},{8,9},{9,8},{10,11... | collective-permute-start | bytes 589832 | tf_op jit(solution)/shard_map/while/body/ppermute | solution.py:29
  189.4 10.1 %collective-permute-start.20 = (f32[11,16,256]{2,1,0:T(8,128)S(1)}, f32[11,16,256]{2,1,0:T(8,128)S(1)}, u32[]{:S(2)}, u32[]{:S(2)}) collective-permute-start(f32[11,16,256]{2,1,0:T(8,128)S(1)} %pad_maximum_fusion.13), channel_id=1, source_target_pairs={{2,0},{4,2},{6,4},{8,6},{10,8},{12,10},{14,12},{16,14},{18,16},{20... | collective-permute-start | bytes 540680 | tf_op jit(solution)/shard_map/ppermute | solution.py:53
  190.8 13.8 %collective-permute-start.19 = (f32[11,16,256]{2,1,0:T(8,128)S(1)}, f32[11,16,256]{2,1,0:T(8,128)S(1)}, u32[]{:S(2)}, u32[]{:S(2)}) collective-permute-start(f32[11,16,256]{2,1,0:T(8,128)S(1)} %pad_maximum_fusion.12), channel_id=1, source_target_pairs={{0,2},{2,4},{4,6},{6,8},{8,10},{10,12},{12,14},{14,16},{16,18},{18... | collective-permute-start | bytes 540680 | tf_op jit(solution)/shard_map/ppermute | solution.py:52
  196.2 9.7 %copy-start.43 = (f32[11,16,256]{2,1,0:T(8,128)}, f32[11,16,256]{2,1,0:T(8,128)S(1)}, u32[]{:S(2)}) copy-start(f32[11,16,256]{2,1,0:T(8,128)S(1)} %collective-permute-done.32.refs_2_) | copy-start | bytes 540676
  196.2 9.7 %copy-start.44 = (f32[11,16,256]{2,1,0:T(8,128)}, f32[11,16,256]{2,1,0:T(8,128)S(1)}, u32[]{:S(2)}) copy-start(f32[11,16,256]{2,1,0:T(8,128)S(1)} %collective-permute-done.31.refs_1_) | copy-start | bytes 540676
  196.3 9.6 %collective-permute-start.34 = (f32[22,8,256]{2,1,0:T(8,128)S(1)}, f32[22,8,256]{2,1,0:T(8,128)S(1)}, u32[]{:S(2)}, u32[]{:S(2)}) collective-permute-start(f32[22,8,256]{2,1,0:T(8,128)S(1)} %fusion.8), channel_id=1, source_target_pairs={{0,1},{1,0},{2,3},{3,2},{4,5},{5,4},{6,7},{7,6},{8,9},{9,8},{10,11... | collective-permute-start | bytes 540680 | tf_op jit(solution)/shard_map/while/body/ppermute | solution.py:29
  197.2 103.7 %collective-permute-start.21 = (f32[4,6,8,256]{3,2,1,0:T(8,128)}, f32[4,6,8,256]{3,2,1,0:T(8,128)}, u32[]{:S(2)}, u32[]{:S(2)}) collective-permute-start(f32[4,6,8,256]{3,2,1,0:T(8,128)} %constant_dynamic-slice_fusion.7), channel_id=1, source_target_pairs={{0,1},{1,0},{2,3},{3,2},{4,5},{5,4},{6,7},{7,6},{8,9},{9,8},{10,11... | collective-permute-start | bytes 589832 | tf_op jit(solution)/shard_map/ppermute | solution.py:29
  205.9 95.1 %collective-permute-start.22 = (f32[22,8,256]{2,1,0:T(8,128)}, f32[22,8,256]{2,1,0:T(8,128)}, u32[]{:S(2)}, u32[]{:S(2)}) collective-permute-start(f32[22,8,256]{2,1,0:T(8,128)} %fusion.11), channel_id=1, source_target_pairs={{0,1},{1,0},{2,3},{3,2},{4,5},{5,4},{6,7},{7,6},{8,9},{9,8},{10,11... | collective-permute-start | bytes 540680 | tf_op jit(solution)/shard_map/ppermute | solution.py:29
  300.8 22.5 %copy-start.22 = (f32[4,6,16,256]{3,2,1,0:T(8,128)}, f32[4,6,16,256]{3,2,1,0:T(8,128)S(1)}, u32[]{:S(2)}) copy-start(f32[4,6,16,256]{3,2,1,0:T(8,128)S(1)} %broadcast_divide_fusion.1.refs_7_) | copy-start | bytes 1179652
  308.4 15.6 %copy-start.23 = (f32[4,6,16,256]{3,2,1,0:T(8,128)S(1)}, f32[4,6,16,256]{3,2,1,0:T(8,128)}, u32[]{:S(2)}) copy-start(f32[4,6,16,256]{3,2,1,0:T(8,128)} %get-tuple-element.455.refs_9_.refs_3_) | copy-start | bytes 1179652
  310.4 19.9 %collective-permute-start.36 = (f32[11,16,256]{2,1,0:T(8,128)S(1)}, f32[11,16,256]{2,1,0:T(8,128)S(1)}, u32[]{:S(2)}, u32[]{:S(2)}) collective-permute-start(f32[11,16,256]{2,1,0:T(8,128)S(1)} %pad_maximum_fusion.21), channel_id=1, source_target_pairs={{2,0},{4,2},{6,4},{8,6},{10,8},{12,10},{14,12},{16,14},{18,16},{20... | collective-permute-start | bytes 540680 | tf_op jit(solution)/shard_map/while/body/ppermute | solution.py:53
  311.7 18.6 %collective-permute-start.35 = (f32[11,16,256]{2,1,0:T(8,128)S(1)}, f32[11,16,256]{2,1,0:T(8,128)S(1)}, u32[]{:S(2)}, u32[]{:S(2)}) collective-permute-start(f32[11,16,256]{2,1,0:T(8,128)S(1)} %pad_maximum_fusion.20), channel_id=1, source_target_pairs={{0,2},{2,4},{4,6},{6,8},{8,10},{10,12},{12,14},{14,16},{16,18},{18... | collective-permute-start | bytes 540680 | tf_op jit(solution)/shard_map/while/body/ppermute | solution.py:52
  316.5 11.5 %collective-permute-start.24 = (f32[11,16,256]{2,1,0:T(8,128)S(1)}, f32[11,16,256]{2,1,0:T(8,128)S(1)}, u32[]{:S(2)}, u32[]{:S(2)}) collective-permute-start(f32[11,16,256]{2,1,0:T(8,128)S(1)} %pad_maximum_fusion.15), channel_id=1, source_target_pairs={{2,0},{4,2},{6,4},{8,6},{10,8},{12,10},{14,12},{16,14},{18,16},{20... | collective-permute-start | bytes 540680 | tf_op jit(solution)/shard_map/ppermute | solution.py:53
  317.8 12.4 %collective-permute-start.23 = (f32[11,16,256]{2,1,0:T(8,128)S(1)}, f32[11,16,256]{2,1,0:T(8,128)S(1)}, u32[]{:S(2)}, u32[]{:S(2)}) collective-permute-start(f32[11,16,256]{2,1,0:T(8,128)S(1)} %pad_maximum_fusion.14), channel_id=1, source_target_pairs={{0,2},{2,4},{4,6},{6,8},{8,10},{10,12},{12,14},{14,16},{16,18},{18... | collective-permute-start | bytes 540680 | tf_op jit(solution)/shard_map/ppermute | solution.py:52
  324.0 22.6 %collective-permute-start.37 = (f32[4,6,8,256]{3,2,1,0:T(8,128)}, f32[4,6,8,256]{3,2,1,0:T(8,128)S(1)}, u32[]{:S(2)}, u32[]{:S(2)}) collective-permute-start(f32[4,6,8,256]{3,2,1,0:T(8,128)} %constant_dynamic-slice_fusion.3), channel_id=1, source_target_pairs={{0,1},{1,0},{2,3},{3,2},{4,5},{5,4},{6,7},{7,6},{8,9},{9,8},{10,11... | collective-permute-start | bytes 589832 | tf_op jit(solution)/shard_map/while/body/ppermute | solution.py:29
  328.0 2.9 collective-permute-start.25
  330.2 1.5 collective-permute-start.26
  330.3 9.6 %copy-start.37 = (f32[11,16,256]{2,1,0:T(8,128)}, f32[11,16,256]{2,1,0:T(8,128)S(1)}, u32[]{:S(2)}) copy-start(f32[11,16,256]{2,1,0:T(8,128)S(1)} %collective-permute-done.36.refs_2_) | copy-start | bytes 540676
  330.3 9.6 %copy-start.41 = (f32[11,16,256]{2,1,0:T(8,128)}, f32[11,16,256]{2,1,0:T(8,128)S(1)}, u32[]{:S(2)}) copy-start(f32[11,16,256]{2,1,0:T(8,128)S(1)} %collective-permute-done.35.refs_1_) | copy-start | bytes 540676
  330.4 16.3 %collective-permute-start.38 = (f32[22,8,256]{2,1,0:T(8,128)S(1)}, f32[22,8,256]{2,1,0:T(8,128)}, u32[]{:S(2)}, u32[]{:S(2)}) collective-permute-start(f32[22,8,256]{2,1,0:T(8,128)S(1)} %fusion.7), channel_id=1, source_target_pairs={{0,1},{1,0},{2,3},{3,2},{4,5},{5,4},{6,7},{7,6},{8,9},{9,8},{10,11... | collective-permute-start | bytes 540680 | tf_op jit(solution)/shard_map/while/body/ppermute | solution.py:29
  341.3 100.0 %all-to-all-start = ((f32[32,8,128]{2,1,0:T(8,128)}), f32[32,8,128]{2,1,0:T(8,128)}, u32[]{:S(2)}, u32[]{:S(2)}) async-start(f32[32,8,128]{2,1,0:T(8,128)} %broadcast_in_dim.20), calls=%async_computation | async-start | bytes 262144 | tf_op jit(solution)/shard_map/all_to_all | solution.py:326
  354.7 42.7 %copy-start.28 = (f32[4,6,16,256]{3,2,1,0:T(8,128)S(1)}, f32[4,6,16,256]{3,2,1,0:T(8,128)}, u32[]{:S(2)}) copy-start(f32[4,6,16,256]{3,2,1,0:T(8,128)} %get-tuple-element.467) | copy-start | bytes 1179652
  400.1 44.9 %copy-start.57 = (s32[2]{0:T(128)S(1)}, s32[2]{0:T(128)}, u32[]{:S(2)}) copy-start(s32[2]{0:T(128)} %constant.432.clone.1) | copy-start | bytes 28
  (18 other events, 55.9 us)

commit v2 on v1

--- a/solution.py
+++ b/solution.py
@@ -339,7 +339,8 @@
     )(parts, *vectors, *founds)
 
     def body(state):
-        basis, search, hess = step_by_step(start, coef)
+        begin = jnp.where(state[2][7, 0] > 2.0, 0.0, start)
+        basis, search, hess = step_by_step(begin, coef)
         return basis, search, hess.at[7, 0].set(1.0)
 
     basis, search, small = lax.while_loop(

time: 450 us -> 113 us (0.25)
  blocking collectives: 285 us -> 13.8 us
  starting transfers between devices: 50 us -> 23.9 us
  Pallas kernels: 48.3 us -> 26 us
  other arithmetic: 18.5 us -> 2.19 us
  waiting for transfers between devices: 24.5 us -> 34.6 us
  local copies, waits for them, and re-layouts: 17 us -> 10.3 us
    psum x7 -> x0, blocking collectives: 285 us -> none  [total(): return lax.psum(jnp.sum(value), AXES)]
    pallas_call x6 -> x3, Pallas kernels: 44.6 us -> 22.3 us  [apply_both(): pl.pallas_call(functools.partial(apply_kernel, len(olds), shift, lax.axis...]
    ppermute x6 -> x3, starting transfers between devices: 29.4 us -> 12.6 us  [exchange(): low = lax.ppermute(last, 'slab', up)]
    reduce_sum x7 -> x0, other arithmetic: 14.2 us -> none  [total(): return lax.psum(jnp.sum(value), AXES)]
    all_to_all x0 -> x1, blocking collectives: none -> 13.8 us  [per_device(): lax.all_to_all(jnp.broadcast_to(tile[None], (devices, 8, 128)), AXES, 0, 0)]
    ppermute x6 -> x3, waiting for transfers between devices: 5.9 us -> 14 us  [exchange(): high = lax.ppermute(first, 'slab', down)]
    all_to_all x1 -> x0, starting transfers between devices: 5.29 us -> none  [per_device(): lax.all_to_all(jnp.broadcast_to(tile[None], (devices, 8, 128)), AXES, 0, 0)]
  transfers between devices with their start and end apart: 28 -> 15, of which waited for: 8 -> 11; matrix products, arithmetic and copies ran while one was open for 5% -> 2% of each run, Pallas kernels for 7% -> 0%
where the time goes in v2:
time: 113 us
  waiting for transfers between devices  34.6 us (31%)
  Pallas kernels  26 us (23%)
  starting transfers between devices  23.9 us (21%)
  blocking collectives  13.8 us (12%)
  local copies, waits for them, and re-layouts  10.3 us (9%)
  other arithmetic  2.19 us (2%)
    pallas_call x3, Pallas kernels, apply_both(): pl.pallas_call(functools.partial(apply_kernel, len(olds), shift, lax.axis...  22.3 us
    ppermute x3, waiting for transfers between devices, exchange(): high = lax.ppermute(first, 'slab', down)  14 us
    all_to_all x1, blocking collectives, per_device(): lax.all_to_all(jnp.broadcast_to(tile[None], (devices, 8, 128)), AXES, 0, 0)  13.8 us
    ppermute x3, starting transfers between devices, exchange(): low = lax.ppermute(last, 'slab', up)  12.6 us
    ppermute x3, waiting for transfers between devices, exchange(): low = lax.ppermute(last, 'slab', up)  6.89 us
    ppermute x1, waiting for transfers between devices, extend_coefficients(): low = lax.ppermute(stacked[:, length - 3:], 'slab', up)  5.52 us
    ppermute x1, starting transfers between devices, extend_coefficients(): low = lax.ppermute(stacked[:, length - 3:], 'slab', up)  5.51 us
    ppermute x1, waiting for transfers between devices, extend_coefficients(): high = lax.ppermute(stacked[:, :3], 'slab', down)  4.79 us
  transfers between devices with their start and end apart: 15, of which 11 were waited for; matrix products, arithmetic and copies ran while one was open for 2% of the time, Pallas kernels for 0%

profile of v2, /device:TPU:0, one launch (start us, length us, event | category | flops | bytes accessed | tf_op | source)
XLA Modules:
  0.0 112.6 jit_solution(3437609025501369650)
XLA Ops:
  0.7 1.2 %pad_maximum_fusion.9 = f32[5,6,16,256]{3,2,1,0:T(8,128)S(1)} fusion(f32[1,6,16,256]{3,2,1,0:T(8,128)} %bitcast.193, f32[1,6,16,256]{3,2,1,0:T(8,128)} %bitcast.196, f32[3,6,16,256]{3,2,1,0:T(8,128)} %param.27), kind=kLoop, calls=%fused_computation.74 | loop fusion | flops 245760 | bytes 983040 | tf_op jit(solution)/shard_map/concatenate | solution.py:318
  1.9 1.3 %collective-permute-start.17 = (f32[5,3,16,256]{3,2,1,0:T(8,128)S(1)}, f32[5,3,16,256]{3,2,1,0:T(8,128)S(1)}, u32[]{:S(2)}, u32[]{:S(2)}) collective-permute-start(f32[5,3,16,256]{3,2,1,0:T(8,128)S(1)} %get-tuple-element.297), channel_id=1, source_target_pairs={{2,0},{4,2},{6,4},{8,6},{10,8},{12,10},{14,12},{16,14},{18,16},{20... | collective-permute-start | bytes 737288 | tf_op jit(solution)/shard_map/ppermute | solution.py:36
  3.2 5.5 %collective-permute-start.16 = (f32[5,3,16,256]{3,2,1,0:T(8,128)S(1)}, f32[5,3,16,256]{3,2,1,0:T(8,128)S(1)}, u32[]{:S(2)}, u32[]{:S(2)}) collective-permute-start(f32[5,3,16,256]{3,2,1,0:T(8,128)S(1)} %get-tuple-element.298), channel_id=1, source_target_pairs={{0,2},{2,4},{4,6},{6,8},{8,10},{10,12},{12,14},{14,16},{16,18},{18... | collective-permute-start | bytes 737288 | tf_op jit(solution)/shard_map/ppermute | solution.py:35
  8.8 4.8 %collective-permute-done.17 = f32[5,3,16,256]{3,2,1,0:T(8,128)S(1)} collective-permute-done((f32[5,3,16,256]{3,2,1,0:T(8,128)S(1)}, f32[5,3,16,256]{3,2,1,0:T(8,128)S(1)}, u32[]{:S(2)}, u32[]{:S(2)}) %collective-permute-start.17) | collective-permute-done | bytes 245792 | tf_op jit(solution)/shard_map/ppermute | solution.py:36
  13.6 5.5 %collective-permute-done.16 = f32[5,3,16,256]{3,2,1,0:T(8,128)S(1)} collective-permute-done((f32[5,3,16,256]{3,2,1,0:T(8,128)S(1)}, f32[5,3,16,256]{3,2,1,0:T(8,128)S(1)}, u32[]{:S(2)}, u32[]{:S(2)}) %collective-permute-start.16) | collective-permute-done | bytes 245792 | tf_op jit(solution)/shard_map/ppermute | solution.py:35
  19.1 0.1 collective-permute-start.18
  19.2 4.4 %collective-permute-start.12 = (f32[11,16,256]{2,1,0:T(8,128)S(1)}, f32[11,16,256]{2,1,0:T(8,128)S(1)}, u32[]{:S(2)}, u32[]{:S(2)}) collective-permute-start(f32[11,16,256]{2,1,0:T(8,128)S(1)} %pad_maximum_fusion.10), channel_id=1, source_target_pairs={{0,2},{2,4},{4,6},{6,8},{8,10},{10,12},{12,14},{14,16},{16,18},{18... | collective-permute-start | bytes 540680 | tf_op jit(solution)/shard_map/ppermute | solution.py:52
  23.7 1.3 %collective-permute-start.13 = (f32[11,16,256]{2,1,0:T(8,128)S(1)}, f32[11,16,256]{2,1,0:T(8,128)S(1)}, u32[]{:S(2)}, u32[]{:S(2)}) collective-permute-start(f32[11,16,256]{2,1,0:T(8,128)S(1)} %pad_maximum_fusion.11), channel_id=1, source_target_pairs={{2,0},{4,2},{6,4},{8,6},{10,8},{12,10},{14,12},{16,14},{18,16},{20... | collective-permute-start | bytes 540680 | tf_op jit(solution)/shard_map/ppermute | solution.py:53
  25.0 0.7 constant_dynamic-slice_fusion.5
  25.7 0.2 collective-permute-start.14
  25.9 0.6 pad_add_fusion.1.refs_0_
  26.5 1.6 %collective-permute-done.12.refs_1_ = f32[11,16,256]{2,1,0:T(8,128)S(1)} collective-permute-done((f32[11,16,256]{2,1,0:T(8,128)S(1)}, f32[11,16,256]{2,1,0:T(8,128)S(1)}, u32[]{:S(2)}, u32[]{:S(2)}) %collective-permute-start.12) | collective-permute-done | bytes 180256 | tf_op jit(solution)/shard_map/ppermute | solution.py:52
  28.1 4.6 %collective-permute-done.13.refs_2_ = f32[11,16,256]{2,1,0:T(8,128)S(1)} collective-permute-done((f32[11,16,256]{2,1,0:T(8,128)S(1)}, f32[11,16,256]{2,1,0:T(8,128)S(1)}, u32[]{:S(2)}, u32[]{:S(2)}) %collective-permute-start.13) | collective-permute-done | bytes 180256 | tf_op jit(solution)/shard_map/ppermute | solution.py:53
  32.7 0.1 collective-permute-start.15
  32.8 0.1 broadcast_select_fusion.1
  32.9 0.5 copy-done.25
  33.4 0.2 pad_maximum_fusion.8.refs_5_
  33.6 0.6 collective-permute-done.15.refs_4_
  34.2 0.6 broadcast_9_refs_6_.2.refs_6_
  34.8 0.1 copy-done.31
  34.9 7.3 %apply_1.16 = (f32[4,6,16,256]{3,2,1,0:T(8,128)}, f32[4,6,16,256]{3,2,1,0:T(8,128)}, f32[8,128]{1,0:T(8,128)}) custom-call(s32[2]{0:T(128)} %pad_add_fusion.1.refs_0_, f32[11,16,256]{2,1,0:T(8,128)} %copy-done.24, f32[11,16,256]{2,1,0:T(8,128)} %copy-done.25, f32[4,6,8,256]{3,2,1,0:T(8,128)} %collective-permute-done.14.refs_3_, f32[22,8,256]{2,1,0:T(8,128)} %copy-done.31, ...), custom_call_target="tpu_custom_call" | custom-call | tf_op jit(solution)/shard_map/apply_1/pallas_call | solution.py:211
  42.1 1.0 slice_bitcast_fusion.26
  43.2 0.9 slice_bitcast_fusion.38
  44.1 2.7 %collective-permute-start.19 = (f32[11,16,256]{2,1,0:T(8,128)S(1)}, f32[11,16,256]{2,1,0:T(8,128)S(1)}, u32[]{:S(2)}, u32[]{:S(2)}) collective-permute-start(f32[11,16,256]{2,1,0:T(8,128)S(1)} %pad_maximum_fusion.12), channel_id=1, source_target_pairs={{0,2},{2,4},{4,6},{6,8},{8,10},{10,12},{12,14},{14,16},{16,18},{18... | collective-permute-start | bytes 540680 | tf_op jit(solution)/shard_map/ppermute | solution.py:52
  46.8 1.3 %collective-permute-start.20 = (f32[11,16,256]{2,1,0:T(8,128)S(1)}, f32[11,16,256]{2,1,0:T(8,128)S(1)}, u32[]{:S(2)}, u32[]{:S(2)}) collective-permute-start(f32[11,16,256]{2,1,0:T(8,128)S(1)} %pad_maximum_fusion.13), channel_id=1, source_target_pairs={{2,0},{4,2},{6,4},{8,6},{10,8},{12,10},{14,12},{16,14},{18,16},{20... | collective-permute-start | bytes 540680 | tf_op jit(solution)/shard_map/ppermute | solution.py:53
  48.1 0.1 collective-permute-start.21
  48.2 2.6 %collective-permute-done.19.refs_1_ = f32[11,16,256]{2,1,0:T(8,128)S(1)} collective-permute-done((f32[11,16,256]{2,1,0:T(8,128)S(1)}, f32[11,16,256]{2,1,0:T(8,128)S(1)}, u32[]{:S(2)}, u32[]{:S(2)}) %collective-permute-start.19) | collective-permute-done | bytes 180256 | tf_op jit(solution)/shard_map/ppermute | solution.py:52
  50.9 4.8 %collective-permute-done.20.refs_2_ = f32[11,16,256]{2,1,0:T(8,128)S(1)} collective-permute-done((f32[11,16,256]{2,1,0:T(8,128)S(1)}, f32[11,16,256]{2,1,0:T(8,128)S(1)}, u32[]{:S(2)}, u32[]{:S(2)}) %collective-permute-start.20) | collective-permute-done | bytes 180256 | tf_op jit(solution)/shard_map/ppermute | solution.py:53
  55.7 0.1 collective-permute-start.22
  55.8 1.4 %collective-permute-done.22.refs_4_ = f32[22,8,256]{2,1,0:T(8,128)S(1)} collective-permute-done((f32[22,8,256]{2,1,0:T(8,128)S(1)}, f32[22,8,256]{2,1,0:T(8,128)S(1)}, u32[]{:S(2)}, u32[]{:S(2)}) %collective-permute-start.22) | collective-permute-done | bytes 180256 | tf_op jit(solution)/shard_map/ppermute | solution.py:29
  57.2 0.6 copy-done.32
  57.8 7.5 %apply_2.1 = (f32[4,6,16,256]{3,2,1,0:T(8,128)}, f32[4,6,16,256]{3,2,1,0:T(8,128)}, f32[8,128]{1,0:T(8,128)}) custom-call(s32[2]{0:T(128)} %pad_add_fusion.1.refs_0_, f32[11,16,256]{2,1,0:T(8,128)} %copy-done.26, f32[11,16,256]{2,1,0:T(8,128)} %copy-done.27, f32[4,6,8,256]{3,2,1,0:T(8,128)} %copy-done.29, f32[22,8,256]{2,1,0:T(8,128)} %copy-done.32, ...), custom_call_target="tpu_custom_call" | custom-call | tf_op jit(solution)/shard_map/apply_2/pallas_call | solution.py:211
  65.3 1.0 slice_bitcast_fusion.24
  66.3 0.9 slice_bitcast_fusion.32
  67.2 5.4 %collective-permute-start.23 = (f32[11,16,256]{2,1,0:T(8,128)S(1)}, f32[11,16,256]{2,1,0:T(8,128)S(1)}, u32[]{:S(2)}, u32[]{:S(2)}) collective-permute-start(f32[11,16,256]{2,1,0:T(8,128)S(1)} %pad_maximum_fusion.14), channel_id=1, source_target_pairs={{0,2},{2,4},{4,6},{6,8},{8,10},{10,12},{12,14},{14,16},{16,18},{18... | collective-permute-start | bytes 540680 | tf_op jit(solution)/shard_map/ppermute | solution.py:52
  72.7 1.3 %collective-permute-start.24 = (f32[11,16,256]{2,1,0:T(8,128)S(1)}, f32[11,16,256]{2,1,0:T(8,128)S(1)}, u32[]{:S(2)}, u32[]{:S(2)}) collective-permute-start(f32[11,16,256]{2,1,0:T(8,128)S(1)} %pad_maximum_fusion.15), channel_id=1, source_target_pairs={{2,0},{4,2},{6,4},{8,6},{10,8},{12,10},{14,12},{16,14},{18,16},{20... | collective-permute-start | bytes 540680 | tf_op jit(solution)/shard_map/ppermute | solution.py:53
  74.0 0.1 collective-permute-start.25
  74.1 2.6 %collective-permute-done.23.refs_1_ = f32[11,16,256]{2,1,0:T(8,128)S(1)} collective-permute-done((f32[11,16,256]{2,1,0:T(8,128)S(1)}, f32[11,16,256]{2,1,0:T(8,128)S(1)}, u32[]{:S(2)}, u32[]{:S(2)}) %collective-permute-start.23) | collective-permute-done | bytes 180256 | tf_op jit(solution)/shard_map/ppermute | solution.py:52
  76.8 4.6 %collective-permute-done.24.refs_2_ = f32[11,16,256]{2,1,0:T(8,128)S(1)} collective-permute-done((f32[11,16,256]{2,1,0:T(8,128)S(1)}, f32[11,16,256]{2,1,0:T(8,128)S(1)}, u32[]{:S(2)}, u32[]{:S(2)}) %collective-permute-start.24) | collective-permute-done | bytes 180256 | tf_op jit(solution)/shard_map/ppermute | solution.py:53
  81.5 1.4 %collective-permute-done.26.refs_4_ = f32[22,8,256]{2,1,0:T(8,128)S(1)} collective-permute-done((f32[22,8,256]{2,1,0:T(8,128)S(1)}, f32[22,8,256]{2,1,0:T(8,128)S(1)}, u32[]{:S(2)}, u32[]{:S(2)}) %collective-permute-start.26) | collective-permute-done | bytes 180256 | tf_op jit(solution)/shard_map/ppermute | solution.py:29
  82.9 0.7 copy-done.30
  83.5 7.6 %apply_3.1 = (f32[4,6,16,256]{3,2,1,0:T(8,128)}, f32[4,6,16,256]{3,2,1,0:T(8,128)}, f32[8,128]{1,0:T(8,128)}) custom-call(s32[2]{0:T(128)} %pad_add_fusion.1.refs_0_, f32[11,16,256]{2,1,0:T(8,128)} %copy-done.22, f32[11,16,256]{2,1,0:T(8,128)} %copy-done.23, f32[4,6,8,256]{3,2,1,0:T(8,128)} %copy-done.28, f32[22,8,256]{2,1,0:T(8,128)} %copy-done.30, ...), custom_call_target="tpu_custom_call" | custom-call | tf_op jit(solution)/shard_map/apply_3/pallas_call | solution.py:211
  91.1 0.7 broadcast_in_dim.28
  91.8 13.8 %all_to_all.5.refs_0_ = f32[32,8,128]{2,1,0:T(8,128)} all-to-all(f32[32,8,128]{2,1,0:T(8,128)S(1)} %broadcast_in_dim.28), channel_id=1, replica_groups=mesh['slab'=16,'sub'=2] {'slab','sub'}, dimensions={0} | all-to-all | bytes 262144 | tf_op jit(solution)/shard_map/all_to_all | solution.py:326
  105.6 3.7 %combine.1 = (f32[4,4,6,16,256]{4,3,2,1,0:T(8,128)}, f32[3,4,6,16,256]{4,3,2,1,0:T(8,128)}, f32[8,128]{1,0:T(8,128)}) custom-call(f32[32,8,128]{2,1,0:T(8,128)} %all_to_all.5.refs_0_, f32[4,6,16,256]{3,2,1,0:T(8,128)S(1)} %copy-done, f32[4,6,16,256]{3,2,1,0:T(8,128)} %get-tuple-element.228.refs_8_.refs_2_, ...), custom_call_target="tpu_custom_call" | custom-call | tf_op jit(solution)/shard_map/combine/pallas_call | solution.py:328
  109.3 2.0 %while.25 = (f32[4,4,6,16,256]{4,3,2,1,0:T(8,128)}, f32[3,4,6,16,256]{4,3,2,1,0:T(8,128)}, f32[8,128]{1,0:T(8,128)}, f32[4,6,16,256]{3,2,1,0:T(8,128)S(1)}, f32[...) while((f32[4,4,6,16,256]{4,3,2,1,0:T(8,128)}, ...), condition=%wide.region_22.23_spmd, body=%wide.region_0.22_spmd.sunk | while | flops 8515611 | bytes 53339816 | solution.py:346
  109.3 1.2 %slice.599 = f32[1,1]{1,0:T(1,128)} slice(f32[8,128]{1,0:T(8,128)} %get-tuple-element.328), slice={[7:8], [0:1]} | slice | bytes 8 | tf_op jit(solution)/shard_map/while/cond/slice | solution.py:347
  111.3 1.3 %slice.518 = f32[4,3]{1,0:T(4,128)} slice(f32[8,128]{1,0:T(8,128)} %get-tuple-element.242), slice={[0:4], [0:3]} | slice | bytes 96 | tf_op jit(solution)/shard_map/slice | solution.py:351
  (52 shorter events, 0.4 us)
Async XLA Ops:
  0.6 18.5 %copy-start.19 = (f32[3,6,16,256]{3,2,1,0:T(8,128)S(1)}, f32[3,6,16,256]{3,2,1,0:T(8,128)}, u32[]{:S(2)}) copy-start(f32[3,6,16,256]{3,2,1,0:T(8,128)} %param.27) | copy-start | bytes 884740
  0.6 18.4 %copy-start.20 = (f32[6,16,256]{2,1,0:T(8,128)S(1)}, f32[6,16,256]{2,1,0:T(8,128)}, u32[]{:S(2)}) copy-start(f32[6,16,256]{2,1,0:T(8,128)} %param.29) | copy-start | bytes 294916
  0.7 18.4 %copy-start.21 = (f32[6,16,256]{2,1,0:T(8,128)S(1)}, f32[6,16,256]{2,1,0:T(8,128)}, u32[]{:S(2)}) copy-start(f32[6,16,256]{2,1,0:T(8,128)} %param.28) | copy-start | bytes 294916
  0.7 8.0 %copy-start = (f32[4,6,16,256]{3,2,1,0:T(8,128)S(1)}, f32[4,6,16,256]{3,2,1,0:T(8,128)}, u32[]{:S(2)}) copy-start(f32[4,6,16,256]{3,2,1,0:T(8,128)} %refs_1_.1) | copy-start | bytes 1179652
  1.9 11.7 %collective-permute-start.17 = (f32[5,3,16,256]{3,2,1,0:T(8,128)S(1)}, f32[5,3,16,256]{3,2,1,0:T(8,128)S(1)}, u32[]{:S(2)}, u32[]{:S(2)}) collective-permute-start(f32[5,3,16,256]{3,2,1,0:T(8,128)S(1)} %get-tuple-element.297), channel_id=1, source_target_pairs={{2,0},{4,2},{6,4},{8,6},{10,8},{12,10},{14,12},{16,14},{18,16},{20... | collective-permute-start | bytes 737288 | tf_op jit(solution)/shard_map/ppermute | solution.py:36
  3.2 15.9 %collective-permute-start.16 = (f32[5,3,16,256]{3,2,1,0:T(8,128)S(1)}, f32[5,3,16,256]{3,2,1,0:T(8,128)S(1)}, u32[]{:S(2)}, u32[]{:S(2)}) collective-permute-start(f32[5,3,16,256]{3,2,1,0:T(8,128)S(1)} %get-tuple-element.298), channel_id=1, source_target_pairs={{0,2},{2,4},{4,6},{6,8},{8,10},{10,12},{12,14},{14,16},{16,18},{18... | collective-permute-start | bytes 737288 | tf_op jit(solution)/shard_map/ppermute | solution.py:35
  19.1 13.7 %collective-permute-start.18 = (f32[5,12,8,256]{3,2,1,0:T(8,128)S(1)}, f32[5,12,8,256]{3,2,1,0:T(8,128)S(1)}, u32[]{:S(2)}, u32[]{:S(2)}) collective-permute-start(f32[5,12,8,256]{3,2,1,0:T(8,128)S(1)} %fusion.4), channel_id=1, source_target_pairs={{0,1},{1,0},{2,3},{3,2},{4,5},{5,4},{6,7},{7,6},{8,9},{9,8},{10,11... | collective-permute-start | bytes 1474568 | tf_op jit(solution)/shard_map/ppermute | solution.py:29
  19.2 8.9 %collective-permute-start.12 = (f32[11,16,256]{2,1,0:T(8,128)S(1)}, f32[11,16,256]{2,1,0:T(8,128)S(1)}, u32[]{:S(2)}, u32[]{:S(2)}) collective-permute-start(f32[11,16,256]{2,1,0:T(8,128)S(1)} %pad_maximum_fusion.10), channel_id=1, source_target_pairs={{0,2},{2,4},{4,6},{6,8},{8,10},{10,12},{12,14},{14,16},{16,18},{18... | collective-permute-start | bytes 540680 | tf_op jit(solution)/shard_map/ppermute | solution.py:52
  23.7 9.0 %collective-permute-start.13 = (f32[11,16,256]{2,1,0:T(8,128)S(1)}, f32[11,16,256]{2,1,0:T(8,128)S(1)}, u32[]{:S(2)}, u32[]{:S(2)}) collective-permute-start(f32[11,16,256]{2,1,0:T(8,128)S(1)} %pad_maximum_fusion.11), channel_id=1, source_target_pairs={{2,0},{4,2},{6,4},{8,6},{10,8},{12,10},{14,12},{16,14},{18,16},{20... | collective-permute-start | bytes 540680 | tf_op jit(solution)/shard_map/ppermute | solution.py:53
  25.7 7.9 %collective-permute-start.14 = (f32[4,6,8,256]{3,2,1,0:T(8,128)}, f32[4,6,8,256]{3,2,1,0:T(8,128)}, u32[]{:S(2)}, u32[]{:S(2)}) collective-permute-start(f32[4,6,8,256]{3,2,1,0:T(8,128)} %constant_dynamic-slice_fusion.5), channel_id=1, source_target_pairs={{0,1},{1,0},{2,3},{3,2},{4,5},{5,4},{6,7},{7,6},{8,9},{9,8},{10,11... | collective-permute-start | bytes 589832 | tf_op jit(solution)/shard_map/ppermute | solution.py:29
  28.1 5.5 %copy-start.24 = (f32[11,16,256]{2,1,0:T(8,128)}, f32[11,16,256]{2,1,0:T(8,128)S(1)}, u32[]{:S(2)}) copy-start(f32[11,16,256]{2,1,0:T(8,128)S(1)} %collective-permute-done.12.refs_1_) | copy-start | bytes 540676
  32.7 0.7 copy-start.25
  32.7 1.5 %collective-permute-start.15 = (f32[22,8,256]{2,1,0:T(8,128)S(1)}, f32[22,8,256]{2,1,0:T(8,128)S(1)}, u32[]{:S(2)}, u32[]{:S(2)}) collective-permute-start(f32[22,8,256]{2,1,0:T(8,128)S(1)} %fusion.9), channel_id=1, source_target_pairs={{0,1},{1,0},{2,3},{3,2},{4,5},{5,4},{6,7},{7,6},{8,9},{9,8},{10,11... | collective-permute-start | bytes 540680 | tf_op jit(solution)/shard_map/ppermute | solution.py:29
  34.2 0.7 copy-start.31
  42.1 6.0 %copy-start.13 = (f32[4,6,16,256]{3,2,1,0:T(8,128)S(1)}, f32[4,6,16,256]{3,2,1,0:T(8,128)}, u32[]{:S(2)}) copy-start(f32[4,6,16,256]{3,2,1,0:T(8,128)} %get-tuple-element.228.refs_8_.refs_2_) | copy-start | bytes 1179652
  44.1 6.8 %collective-permute-start.19 = (f32[11,16,256]{2,1,0:T(8,128)S(1)}, f32[11,16,256]{2,1,0:T(8,128)S(1)}, u32[]{:S(2)}, u32[]{:S(2)}) collective-permute-start(f32[11,16,256]{2,1,0:T(8,128)S(1)} %pad_maximum_fusion.12), channel_id=1, source_target_pairs={{0,2},{2,4},{4,6},{6,8},{8,10},{10,12},{12,14},{14,16},{16,18},{18... | collective-permute-start | bytes 540680 | tf_op jit(solution)/shard_map/ppermute | solution.py:52
  46.8 8.9 %collective-permute-start.20 = (f32[11,16,256]{2,1,0:T(8,128)S(1)}, f32[11,16,256]{2,1,0:T(8,128)S(1)}, u32[]{:S(2)}, u32[]{:S(2)}) collective-permute-start(f32[11,16,256]{2,1,0:T(8,128)S(1)} %pad_maximum_fusion.13), channel_id=1, source_target_pairs={{2,0},{4,2},{6,4},{8,6},{10,8},{12,10},{14,12},{16,14},{18,16},{20... | collective-permute-start | bytes 540680 | tf_op jit(solution)/shard_map/ppermute | solution.py:53
  48.1 7.6 %collective-permute-start.21 = (f32[4,6,8,256]{3,2,1,0:T(8,128)S(1)}, f32[4,6,8,256]{3,2,1,0:T(8,128)S(1)}, u32[]{:S(2)}, u32[]{:S(2)}) collective-permute-start(f32[4,6,8,256]{3,2,1,0:T(8,128)S(1)} %constant_dynamic-slice_fusion.4), channel_id=1, source_target_pairs={{0,1},{1,0},{2,3},{3,2},{4,5},{5,4},{6,7},{7,6},{8,9},{9,8},{10,11... | collective-permute-start | bytes 589832 | tf_op jit(solution)/shard_map/ppermute | solution.py:29
  50.9 6.3 %copy-start.26 = (f32[11,16,256]{2,1,0:T(8,128)}, f32[11,16,256]{2,1,0:T(8,128)S(1)}, u32[]{:S(2)}) copy-start(f32[11,16,256]{2,1,0:T(8,128)S(1)} %collective-permute-done.19.refs_1_) | copy-start | bytes 540676
  55.7 1.5 %copy-start.27 = (f32[11,16,256]{2,1,0:T(8,128)}, f32[11,16,256]{2,1,0:T(8,128)S(1)}, u32[]{:S(2)}) copy-start(f32[11,16,256]{2,1,0:T(8,128)S(1)} %collective-permute-done.20.refs_2_) | copy-start | bytes 540676
  55.7 1.5 %collective-permute-start.22 = (f32[22,8,256]{2,1,0:T(8,128)S(1)}, f32[22,8,256]{2,1,0:T(8,128)S(1)}, u32[]{:S(2)}, u32[]{:S(2)}) collective-permute-start(f32[22,8,256]{2,1,0:T(8,128)S(1)} %fusion.8), channel_id=1, source_target_pairs={{0,1},{1,0},{2,3},{3,2},{4,5},{5,4},{6,7},{7,6},{8,9},{9,8},{10,11... | collective-permute-start | bytes 540680 | tf_op jit(solution)/shard_map/ppermute | solution.py:29
  55.8 1.4 %copy-start.29 = (f32[4,6,8,256]{3,2,1,0:T(8,128)}, f32[4,6,8,256]{3,2,1,0:T(8,128)S(1)}, u32[]{:S(2)}) copy-start(f32[4,6,8,256]{3,2,1,0:T(8,128)S(1)} %collective-permute-done.21.refs_3_) | copy-start | bytes 589828
  57.2 0.7 copy-start.32
  65.3 8.7 %copy-start.16 = (f32[4,6,16,256]{3,2,1,0:T(8,128)S(1)}, f32[4,6,16,256]{3,2,1,0:T(8,128)}, u32[]{:S(2)}) copy-start(f32[4,6,16,256]{3,2,1,0:T(8,128)} %get-tuple-element.230.refs_9_.refs_3_) | copy-start | bytes 1179652
  67.2 9.5 %collective-permute-start.23 = (f32[11,16,256]{2,1,0:T(8,128)S(1)}, f32[11,16,256]{2,1,0:T(8,128)S(1)}, u32[]{:S(2)}, u32[]{:S(2)}) collective-permute-start(f32[11,16,256]{2,1,0:T(8,128)S(1)} %pad_maximum_fusion.14), channel_id=1, source_target_pairs={{0,2},{2,4},{4,6},{6,8},{8,10},{10,12},{12,14},{14,16},{16,18},{18... | collective-permute-start | bytes 540680 | tf_op jit(solution)/shard_map/ppermute | solution.py:52
  72.7 8.7 %collective-permute-start.24 = (f32[11,16,256]{2,1,0:T(8,128)S(1)}, f32[11,16,256]{2,1,0:T(8,128)S(1)}, u32[]{:S(2)}, u32[]{:S(2)}) collective-permute-start(f32[11,16,256]{2,1,0:T(8,128)S(1)} %pad_maximum_fusion.15), channel_id=1, source_target_pairs={{2,0},{4,2},{6,4},{8,6},{10,8},{12,10},{14,12},{16,14},{18,16},{20... | collective-permute-start | bytes 540680 | tf_op jit(solution)/shard_map/ppermute | solution.py:53
  74.0 7.4 %collective-permute-start.25 = (f32[4,6,8,256]{3,2,1,0:T(8,128)S(1)}, f32[4,6,8,256]{3,2,1,0:T(8,128)S(1)}, u32[]{:S(2)}, u32[]{:S(2)}) collective-permute-start(f32[4,6,8,256]{3,2,1,0:T(8,128)S(1)} %constant_dynamic-slice_fusion.3), channel_id=1, source_target_pairs={{0,1},{1,0},{2,3},{3,2},{4,5},{5,4},{6,7},{7,6},{8,9},{9,8},{10,11... | collective-permute-start | bytes 589832 | tf_op jit(solution)/shard_map/ppermute | solution.py:29
  76.7 6.1 %copy-start.22 = (f32[11,16,256]{2,1,0:T(8,128)}, f32[11,16,256]{2,1,0:T(8,128)S(1)}, u32[]{:S(2)}) copy-start(f32[11,16,256]{2,1,0:T(8,128)S(1)} %collective-permute-done.23.refs_1_) | copy-start | bytes 540676
  81.4 1.5 %copy-start.23 = (f32[11,16,256]{2,1,0:T(8,128)}, f32[11,16,256]{2,1,0:T(8,128)S(1)}, u32[]{:S(2)}) copy-start(f32[11,16,256]{2,1,0:T(8,128)S(1)} %collective-permute-done.24.refs_2_) | copy-start | bytes 540676
  81.4 1.5 %collective-permute-start.26 = (f32[22,8,256]{2,1,0:T(8,128)S(1)}, f32[22,8,256]{2,1,0:T(8,128)S(1)}, u32[]{:S(2)}, u32[]{:S(2)}) collective-permute-start(f32[22,8,256]{2,1,0:T(8,128)S(1)} %fusion.7), channel_id=1, source_target_pairs={{0,1},{1,0},{2,3},{3,2},{4,5},{5,4},{6,7},{7,6},{8,9},{9,8},{10,11... | collective-permute-start | bytes 540680 | tf_op jit(solution)/shard_map/ppermute | solution.py:29
  81.5 1.4 %copy-start.28 = (f32[4,6,8,256]{3,2,1,0:T(8,128)}, f32[4,6,8,256]{3,2,1,0:T(8,128)S(1)}, u32[]{:S(2)}) copy-start(f32[4,6,8,256]{3,2,1,0:T(8,128)S(1)} %collective-permute-done.25.refs_3_) | copy-start | bytes 589828
  82.9 0.7 copy-start.30
  91.8 17.5 %copy-start.33 = (s32[2]{0:T(128)S(1)}, s32[2]{0:T(128)}, u32[]{:S(2)}) copy-start(s32[2]{0:T(128)} %constant.377.clone.1) | copy-start | bytes 28

commit v3 on v2

--- a/solution.py
+++ b/solution.py
@@ -29,31 +29,75 @@
     return lax.ppermute(field, "sub", [(0, 1), (1, 0)])
 
 
-def extend_coefficients(stacked):
-    up, down = neighbours(lax.axis_size("slab"))
-    length = stacked.shape[1]
-    low = lax.ppermute(stacked[:, length - 3 :], "slab", up)
-    high = lax.ppermute(stacked[:, :3], "slab", down)
-    tall = jnp.concatenate([low, stacked, high], 1)
-    other = across(edge_rows(tall, 2))
-    sub = lax.axis_index("sub")
+def swap_pairs(devices, odd):
+    mates = [(i, (i ^ 1) if not odd else (i + 1 if i % 2 else i - 1)) for i in range(devices)]
+    return [(i, j) for i, j in mates if 0 <= j < devices]
+
+
+def is_even():
+    return lax.axis_index("slab") % 2 == 0
+
+
+def split_ends(vector):
+    length = vector.shape[1]
+    last = [vector[3, length - 5 :]] + [vector[c, length - 2 :] for c in range(3)]
+    first = [vector[3, :5]] + [vector[c, :2] for c in range(3)]
+    return first, last
+
+
+def for_pairs(first, last):
+    even = is_even()
+    first, last = jnp.concatenate(first, 0), jnp.concatenate(last, 0)
+    return jnp.where(even, last, first), jnp.where(even, first, last)
+
+
+def swap(to_near, to_far):
+    devices = lax.axis_size("slab")
+    near = lax.ppermute(to_near, "slab", swap_pairs(devices, False))
+    far = lax.ppermute(to_far, "slab", swap_pairs(devices, True))
+    corner = across(edge_rows(jnp.concatenate([near, far], 0), 1))
+    return near, far, corner
+
+
+def exchange_first(vector, stacked):
+    names, length = stacked.shape[:2]
+    flat = (names * 3,) + stacked.shape[2:]
+    first, last = split_ends(vector)
+    to_near, to_far = for_pairs(
+        [stacked[:, :3].reshape(flat)] + first, [stacked[:, length - 3 :].reshape(flat)] + last
+    )
+    side_all = across(
+        edge_rows(jnp.concatenate([vector.reshape((-1,) + vector.shape[2:]),
+                                   stacked.reshape((-1,) + stacked.shape[2:])], 0), 1)
+    )
+    near, far, corner = swap(to_near, to_far)
+    even, sub = is_even(), lax.axis_index("sub")
+    planes, cut = near.shape[0], names * 3
+    edge = (PAD,) + stacked.shape[3:]
+    count = vector.shape[0] * length
+    side = side_all[:count].reshape((vector.shape[0], length) + edge)
+    low = jnp.where(even, far[:cut], near[:cut]).reshape((names, 3) + stacked.shape[2:])
+    high = jnp.where(even, near[:cut], far[:cut]).reshape((names, 3) + stacked.shape[2:])
+    from_near, from_far = corner[:cut], corner[planes : planes + cut]
+    other = jnp.concatenate(
+        [
+            jnp.where(even, from_far, from_near).reshape((names, 3) + edge),
+            side_all[count:].reshape((names, length) + edge),
+            jnp.where(even, from_near, from_far).reshape((names, 3) + edge),
+        ],
+        1,
+    )
     left = jnp.where(sub == 1, other, 0.0)
     right = jnp.where(sub == 0, other, 0.0)
-    return jnp.concatenate([left, tall, right], 2)
-
-
-def exchange(vector):
-    up, down = neighbours(lax.axis_size("slab"))
-    length = vector.shape[1]
-    last = jnp.concatenate(
-        [vector[3, length - 5 :]] + [vector[c, length - 2 :] for c in range(3)], 0
-    )
-    first = jnp.concatenate([vector[3, :5]] + [vector[c, :2] for c in range(3)], 0)
-    low = lax.ppermute(last, "slab", up)
-    high = lax.ppermute(first, "slab", down)
-    side = across(edge_rows(vector, 2))
-    corner = across(edge_rows(jnp.concatenate([low, high], 0), 1))
-    return low, high, side, corner
+    coef = jnp.concatenate([left, jnp.concatenate([low, stacked, high], 1), right], 2)
+    rest = jnp.concatenate([corner[cut:planes], corner[planes + cut :]], 0)
+    return (near[cut:], far[cut:], side, rest), coef
+
+
+def exchange(to_near, to_far, side_out):
+    side = across(side_out)
+    near, far, corner = swap(to_near, to_far)
+    return near, far, side, corner
 
 
 def plane_shifts(center):
@@ -69,15 +113,22 @@
 def apply_kernel(
     count, shift, slabs, subs, *refs
 ):
-    place, low, high, side, corner, coef, tile_in = refs[:7]
+    place, near, far, side, corner, coef, tile_in = refs[:7]
     olds = refs[7 : 7 + count]
-    found, new, tile_out = refs[7 + count : 10 + count]
-    pres, tee, schur, vel, first, second = refs[10 + count :]
+    found, new, tile_out, to_near, to_far, side_out = refs[7 + count : 13 + count]
+    pres, tee, schur, vel, first, second = refs[13 + count :]
     own = olds[-1]
     cells_x, cells_y, lanes = own.shape[1:]
     rows = cells_y + 2 * PAD
     slab, sub = place[0], place[1]
     is_left = sub == 0
+    even = slab % 2 == 0
+
+    def low(i):
+        return jnp.where(even, far[i], near[i]), jnp.where(even, corner[11 + i], corner[i])
+
+    def high(i):
+        return jnp.where(even, near[i], far[i]), jnp.where(even, corner[i], corner[11 + i])
 
     def put(write, middle, beyond):
         write(slice(PAD, PAD + cells_y), middle)
@@ -91,13 +142,13 @@
         return write
 
     for i in range(5):
-        put(writer(pres, i), low[i], corner[i])
-        put(writer(pres, 5 + cells_x + i), high[i], corner[11 + i])
+        put(writer(pres, i), *low(i))
+        put(writer(pres, 5 + cells_x + i), *high(i))
     for c in range(3):
         for i in range(2):
             k = 5 + 2 * c + i
-            put(writer(vel, c, i), low[k], corner[k])
-            put(writer(vel, c, 2 + cells_x + i), high[k], corner[11 + k])
+            put(writer(vel, c, i), *low(k))
+            put(writer(vel, c, 2 + cells_x + i), *high(k))
 
     @pl.loop(0, cells_x)
     def _(i):
@@ -179,6 +230,7 @@
         for c in range(4):
             fresh = images[c][mid] - shift * own[c, i]
             new[c, i] = fresh
+            side_out[c, i] = jnp.where(is_left, fresh[cells_y - PAD :], fresh[:PAD])
             for k in range(count):
                 sums[k] = sums[k] + fresh * olds[k][c, i]
             sums[count] = sums[count] + fresh * fresh
@@ -190,6 +242,11 @@
     sums = lax.fori_loop(
         0, cells_x, last_stage, (zero,) * (count + 1 + (count == 1))
     )
+    ends = [(3, i, cells_x - 5 + i) for i in range(5)]
+    ends += [(c, i, cells_x - 2 + i) for c in range(3) for i in range(2)]
+    for k, (c, i, j) in enumerate(ends):
+        to_near[k] = jnp.where(even, new[c, j], new[c, i])
+        to_far[k] = jnp.where(even, new[c, i], new[c, j])
     lane = lax.broadcasted_iota(jnp.int32, (8, 128), 1)
     base = count * (count + 1) // 2
     tile = tile_in[...]
@@ -200,11 +257,10 @@
     tile_out[...] = tile
 
 
-def apply_both(olds, coef, tile, shift):
+def apply_both(olds, arrived, coef, tile, shift):
     own = olds[-1]
     cells_x, cells_y, lanes = own.shape[1:]
     rows = cells_y + 2 * PAD
-    low, high, side, corner = exchange(own)
     place = jnp.stack([lax.axis_index("slab"), lax.axis_index("sub")]).astype(jnp.int32)
     whole = pl.BlockSpec(memory_space=pltpu.VMEM)
     f32 = jnp.float32
@@ -214,11 +270,14 @@
         ),
         name=f"apply_{len(olds)}",
         in_specs=[pl.BlockSpec(memory_space=pltpu.SMEM)] + [whole] * (6 + len(olds)),
-        out_specs=[whole] * 3,
+        out_specs=[whole] * 6,
         out_shape=[
             jax.ShapeDtypeStruct(own.shape, f32),
             jax.ShapeDtypeStruct(own.shape, f32),
             jax.ShapeDtypeStruct((8, 128), f32),
+            jax.ShapeDtypeStruct((11, cells_y, lanes), f32),
+            jax.ShapeDtypeStruct((11, cells_y, lanes), f32),
+            jax.ShapeDtypeStruct((4, cells_x, PAD, lanes), f32),
         ],
         scratch_shapes=[
             pltpu.VMEM((cells_x + 10, rows, lanes), f32),
@@ -229,13 +288,13 @@
             pltpu.VMEM((3, cells_x + 2, rows, lanes), f32),
         ],
         compiler_params=pltpu.CompilerParams(vmem_limit_bytes=56 * 1024 * 1024),
-    )(place, low, high, side, corner, coef, tile, *olds)
+    )(place, *arrived, coef, tile, *olds)
 
 
 def combine_kernel(*refs):
     parts = refs[0]
     vectors, founds = refs[1:5], refs[5:8]
-    basis, search, small = refs[8:]
+    basis, search, small, least = refs[8:]
     total = jnp.sum(parts[...], axis=0)[0:1]
     lane = lax.broadcasted_iota(jnp.int32, (1, 128), 1)
 
@@ -268,7 +327,7 @@
             inverse[i, j] = -value / upper[i, i]
     rows = lax.broadcasted_iota(jnp.int32, (8, 128), 0)
     lanes = lax.broadcasted_iota(jnp.int32, (8, 128), 1)
-    tile = jnp.where(rows == 7, share, 0.0)
+    tile = jnp.zeros((8, 128), jnp.float32)
     for j in range(ITERS):
         for i in range(j + 2):
             value = None
@@ -279,7 +338,8 @@
                 term = moved * inverse[k, j]
                 value = term if value is None else value + term
             tile = jnp.where((rows == i) & (lanes == j), value, tile)
-    small[...] = tile
+    small[...] = tile[: ITERS + 1, :ITERS]
+    least[0] = jnp.sum(share)
 
     @pl.loop(0, vectors[0].shape[1])
     def _(x):
@@ -300,9 +360,11 @@
     blank = jnp.zeros((8, 128), jnp.float32)
     vectors = [start / jnp.sqrt(total(start * start))]
     searches = []
-    hess = jnp.zeros((8, 128), jnp.float32)
+    hess = jnp.zeros((ITERS + 1, ITERS), jnp.float32)
     for column in range(ITERS):
-        found, image, _ = apply_both([vectors[column]], coef, blank, 0.0)
+        own = vectors[column]
+        arrived = exchange(*for_pairs(*split_ends(own)), edge_rows(own, 2))
+        found, image = apply_both([own], arrived, coef, blank, 0.0)[:2]
         searches.append(found)
         projected = [total(vector * image) for vector in vectors]
         for row in range(column + 1):
@@ -315,40 +377,43 @@
 
 
 def per_device(start, wind, reaction, mass):
-    coef = extend_coefficients(jnp.concatenate([wind, reaction[None], mass[None]], 0))
+    arrived, coef = exchange_first(start, jnp.concatenate([wind, reaction[None], mass[None]], 0))
     tile = jnp.zeros((8, 128), jnp.float32)
     vectors, founds = [start], []
     for column in range(ITERS):
-        found, fresh, tile = apply_both(vectors, coef, tile, SHIFTS[column])
+        found, fresh, tile, *ends = apply_both(vectors, arrived, coef, tile, SHIFTS[column])
         founds.append(found)
         vectors.append(fresh)
+        if column + 1 < ITERS:
+            arrived = exchange(*ends)
     devices = lax.axis_size("slab") * lax.axis_size("sub")
     parts = lax.all_to_all(jnp.broadcast_to(tile[None], (devices, 8, 128)), AXES, 0, 0)
     whole = pl.BlockSpec(memory_space=pltpu.VMEM)
-    basis, search, small = pl.pallas_call(
+    basis, search, small, least = pl.pallas_call(
         combine_kernel,
         name="combine",
         in_specs=[whole] * 8,
-        out_specs=[whole] * 3,
+        out_specs=[whole] * 3 + [pl.BlockSpec(memory_space=pltpu.SMEM)],
         out_shape=[
             jax.ShapeDtypeStruct((ITERS + 1,) + start.shape, jnp.float32),
             jax.ShapeDtypeStruct((ITERS,) + start.shape, jnp.float32),
-            jax.ShapeDtypeStruct((8, 128), jnp.float32),
+            jax.ShapeDtypeStruct((ITERS + 1, ITERS), jnp.float32),
+            jax.ShapeDtypeStruct((1,), jnp.float32),
         ],
         compiler_params=pltpu.CompilerParams(vmem_limit_bytes=56 * 1024 * 1024),
     )(parts, *vectors, *founds)
 
     def body(state):
-        begin = jnp.where(state[2][7, 0] > 2.0, 0.0, start)
+        begin = jnp.where(state[3][0] > 2.0, 0.0, start)
         basis, search, hess = step_by_step(begin, coef)
-        return basis, search, hess.at[7, 0].set(1.0)
-
-    basis, search, small = lax.while_loop(
-        lambda state: jnp.logical_not(state[2][7, 0] >= PIVOT_FLOOR),
+        return basis, search, hess, jnp.ones((1,), jnp.float32)
+
+    basis, search, small, _ = lax.while_loop(
+        lambda state: jnp.logical_not(state[3][0] >= PIVOT_FLOOR),
         body,
-        (basis, search, small),
-    )
-    return basis, search, small[: ITERS + 1, :ITERS]
+        (basis, search, small, least),
+    )
+    return basis, search, small
 
 
 def solution(mesh):

time: 113 us -> 102 us (0.903)
  starting transfers between devices: 23.9 us -> 12.3 us
  local copies, waits for them, and re-layouts: 10.3 us -> 5.04 us
  blocking collectives: 13.8 us -> 16.6 us
  other arithmetic: 2.19 us -> 4.48 us
    ppermute x8 -> x6, starting transfers between devices: 23.2 us -> 11.7 us  [the longest x3 9.75 us: swap(): near = lax.ppermute(to_near, 'slab', swap_pairs(devices, False))]
    squeeze x6 -> x0, local copies, waits for them, and re-layouts: 3.83 us -> none  [the longest x3 2.1 us: exchange(): vector[3, :5]]
    all_to_all x1, blocking collectives: 13.8 us -> 16.6 us  [per_device(): lax.all_to_all(jnp.broadcast_to(tile[None], (devices, 8, 128)), AXES, 0, 0)]
    concatenate x11 -> x6, other arithmetic: 0.34 us -> 1.71 us  [the longest x3 0.81 us: swap(): corner = across(edge_rows(jnp.concatenate([near, far], 0), 1))]
    ppermute x7 -> x6, waiting for transfers between devices: 3.39 us -> 2.77 us  [across(): return lax.ppermute(field, 'sub', [(0, 1), (1, 0)])]
    slice x3 -> x6, local copies, waits for them, and re-layouts: 2.48 us -> 2.11 us  [the longest x2 1.35 us: exchange_first(): return ((near[cut:], far[cut:], side, rest), coef)]
    ppermute x8 -> x6, waiting for transfers between devices: 31.2 us -> 31.2 us  [the longest x3 31.2 us: swap(): near = lax.ppermute(to_near, 'slab', swap_pairs(devices, False))]
  transfers between devices with their start and end apart: 15 -> 12, of which waited for: 11 -> 5; matrix products, arithmetic and copies ran while one was open for 2% -> 4% of each run, Pallas kernels for 0% -> 0%
where the time goes in v3:
time: 102 us; the launch traced here: 101 us
  waiting for transfers between devices  33.9 us (33%)
  Pallas kernels  26.9 us (26%)
  blocking collectives  16.6 us (16%)
  starting transfers between devices  12.3 us (12%)
  local copies, waits for them, and re-layouts  5.04 us (5%)
  other arithmetic  4.48 us (4%)
  between operations  1.08 us (1%)
    ppermute x3, waiting for transfers between devices, swap(): near = lax.ppermute(to_near, 'slab', swap_pairs(devices, False))  31.2 us
    pallas_call x3, Pallas kernels, apply_both(): pl.pallas_call(functools.partial(apply_kernel, len(olds), shift, lax.axis...  23.2 us
    all_to_all x1, blocking collectives, per_device(): lax.all_to_all(jnp.broadcast_to(tile[None], (devices, 8, 128)), AXES, 0, 0)  16.6 us
    ppermute x3, starting transfers between devices, swap(): near = lax.ppermute(to_near, 'slab', swap_pairs(devices, False))  9.75 us
    pallas_call x1, Pallas kernels, per_device(): pl.pallas_call(combine_kernel, name='combine', in_specs=[whole] * 8, out_...  3.73 us
    ppermute x6, waiting for transfers between devices, across(): return lax.ppermute(field, 'sub', [(0, 1), (1, 0)])  2.77 us
  transfers between devices with their start and end apart: 12, of which 5 were waited for; matrix products, arithmetic and copies ran while one was open for 4% of the time, Pallas kernels for 0%

profile of v3, /device:TPU:0, one launch (start us, length us, event | category | flops | bytes accessed | tf_op | source)
XLA Modules:
  0.0 101.2 jit_solution(12779764604673509882)
XLA Ops:
  0.7 1.1 %pad_maximum_fusion.9 = f32[5,6,16,256]{3,2,1,0:T(8,128)S(1)} fusion(f32[1,6,16,256]{3,2,1,0:T(8,128)} %bitcast.120, f32[1,6,16,256]{3,2,1,0:T(8,128)} %bitcast.122, f32[3,6,16,256]{3,2,1,0:T(8,128)} %param.25), kind=kLoop, calls=%fused_computation.75 | loop fusion | flops 245760 | bytes 983040 | tf_op jit(solution)/shard_map/concatenate | solution.py:380
  2.0 0.8 broadcast_select_fusion
  2.8 0.7 collective-permute-start.13
  3.5 5.7 %collective-permute-start.12 = (f32[26,16,256]{2,1,0:T(8,128)S(1)}, f32[26,16,256]{2,1,0:T(8,128)S(1)}, u32[]{:S(2)}, u32[]{:S(2)}) collective-permute-start(f32[26,16,256]{2,1,0:T(8,128)S(1)} %get-tuple-element.252), channel_id=1, source_target_pairs={{0,2},{2,0},{4,6},{6,4},{8,10},{10,8},{12,14},{14,12},{16,18},{18,... | collective-permute-start | bytes 1277960 | tf_op jit(solution)/shard_map/ppermute | solution.py:56
  9.3 0.1 collective-permute-start.14
  9.3 0.0 collective-permute-done.13
  9.4 18.7 %collective-permute-done.12 = f32[26,16,256]{2,1,0:T(8,128)S(1)} collective-permute-done((f32[26,16,256]{2,1,0:T(8,128)S(1)}, f32[26,16,256]{2,1,0:T(8,128)S(1)}, u32[]{:S(2)}, u32[]{:S(2)}) %collective-permute-start.12) | collective-permute-done | bytes 426016 | tf_op jit(solution)/shard_map/ppermute | solution.py:56
  28.0 0.8 fusion.10
  28.8 0.0 collective-permute-start.15
  28.8 0.6 pad_add_fusion.1.refs_0_
  29.5 0.7 slice.350.refs_2_
  30.1 0.7 slice.349.refs_1_
  30.9 0.0 collective-permute-done.14
  30.9 0.7 slice.351
  31.6 0.0 collective-permute-done.15
  31.6 0.7 pad_maximum_fusion.11.refs_4_
  32.3 0.1 fusion.12
  32.4 0.1 copy-done.18
  32.5 0.1 copy-done.23
  32.6 0.0 copy-done.24
  32.6 0.2 pad_maximum_fusion.8.refs_5_
  32.8 0.6 broadcast_11_refs_6_.2.refs_6_
  33.4 7.6 %apply_1.7 = (f32[4,6,16,256]{3,2,1,0:T(8,128)}, f32[4,6,16,256]{3,2,1,0:T(8,128)}, f32[8,128]{1,0:T(8,128)}, f32[11,16,256]{2,1,0:T(8,128)}, f32[11,16,256]{2,1,0:T(8,128)}, /*index=5*/f32[4,6,8,256]{3,2,1,0:T(8,128)}) custom-call(s32[2]{0:T(128)} %pad_add_fusion.1.refs_0_, f32[11,16,256]{2,1,0:T(8,128)} %slice.349.refs_1_, f32[11,16,256]{2,1,0:T(8,128)} %slice.350.refs_2_, ...), custom_call_target="tpu_custom_call" | custom-call | tf_op jit(solution)/shard_map/apply_1/pallas_call | solution.py:267
  41.0 1.6 %collective-permute-start.16 = (f32[11,16,256]{2,1,0:T(8,128)}, f32[11,16,256]{2,1,0:T(8,128)S(1)}, u32[]{:S(2)}, u32[]{:S(2)}) collective-permute-start(f32[11,16,256]{2,1,0:T(8,128)} %get-tuple-element.167), channel_id=1, source_target_pairs={{0,2},{2,0},{4,6},{6,4},{8,10},{10,8},{12,14},{14,12},{16,18},{18,... | collective-permute-start | bytes 540680 | tf_op jit(solution)/shard_map/ppermute | solution.py:56
  42.6 0.7 collective-permute-start.17
  43.3 0.3 collective-permute-start.18
  43.6 7.7 %collective-permute-done.16.refs_1_ = f32[11,16,256]{2,1,0:T(8,128)S(1)} collective-permute-done((f32[11,16,256]{2,1,0:T(8,128)}, f32[11,16,256]{2,1,0:T(8,128)S(1)}, u32[]{:S(2)}, u32[]{:S(2)}) %collective-permute-start.16) | collective-permute-done | bytes 180256 | tf_op jit(solution)/shard_map/ppermute | solution.py:56
  51.3 0.0 collective-permute-done.17.refs_2_
  51.3 0.1 collective-permute-start.19
  51.4 0.0 collective-permute-done.18.refs_3_
  51.4 0.0 copy-start.26
  51.4 1.4 %collective-permute-done.19.refs_4_ = f32[22,8,256]{2,1,0:T(8,128)S(1)} collective-permute-done((f32[22,8,256]{2,1,0:T(8,128)S(1)}, f32[22,8,256]{2,1,0:T(8,128)S(1)}, u32[]{:S(2)}, u32[]{:S(2)}) %collective-permute-start.19) | collective-permute-done | bytes 180256 | tf_op jit(solution)/shard_map/ppermute | solution.py:29
  52.8 0.7 copy-done.28
  53.4 7.7 %apply_2.1 = (f32[4,6,16,256]{3,2,1,0:T(8,128)}, f32[4,6,16,256]{3,2,1,0:T(8,128)}, f32[8,128]{1,0:T(8,128)}, f32[11,16,256]{2,1,0:T(8,128)}, f32[11,16,256]{2,1,0:T(8,128)}, /*index=5*/f32[4,6,8,256]{3,2,1,0:T(8,128)}) custom-call(s32[2]{0:T(128)} %pad_add_fusion.1.refs_0_, f32[11,16,256]{2,1,0:T(8,128)} %copy-done.21, f32[11,16,256]{2,1,0:T(8,128)} %copy-done.22, ...), custom_call_target="tpu_custom_call" | custom-call | tf_op jit(solution)/shard_map/apply_2/pallas_call | solution.py:267
  61.2 2.4 %collective-permute-start.20 = (f32[11,16,256]{2,1,0:T(8,128)}, f32[11,16,256]{2,1,0:T(8,128)S(1)}, u32[]{:S(2)}, u32[]{:S(2)}) collective-permute-start(f32[11,16,256]{2,1,0:T(8,128)} %get-tuple-element.172), channel_id=1, source_target_pairs={{0,2},{2,0},{4,6},{6,4},{8,10},{10,8},{12,14},{14,12},{16,18},{18,... | collective-permute-start | bytes 540680 | tf_op jit(solution)/shard_map/ppermute | solution.py:56
  63.6 0.7 collective-permute-start.21
  64.2 0.1 collective-permute-start.22
  64.3 4.8 %collective-permute-done.20.refs_1_ = f32[11,16,256]{2,1,0:T(8,128)S(1)} collective-permute-done((f32[11,16,256]{2,1,0:T(8,128)}, f32[11,16,256]{2,1,0:T(8,128)S(1)}, u32[]{:S(2)}, u32[]{:S(2)}) %collective-permute-start.20) | collective-permute-done | bytes 180256 | tf_op jit(solution)/shard_map/ppermute | solution.py:56
  69.1 0.1 collective-permute-start.23
  69.2 0.0 collective-permute-done.22.refs_3_
  69.2 0.0 copy-start.25
  69.2 1.4 %collective-permute-done.23.refs_4_ = f32[22,8,256]{2,1,0:T(8,128)S(1)} collective-permute-done((f32[22,8,256]{2,1,0:T(8,128)S(1)}, f32[22,8,256]{2,1,0:T(8,128)S(1)}, u32[]{:S(2)}, u32[]{:S(2)}) %collective-permute-start.23) | collective-permute-done | bytes 180256 | tf_op jit(solution)/shard_map/ppermute | solution.py:29
  70.6 0.7 copy-done.27
  71.3 7.9 %apply_3.1 = (f32[4,6,16,256]{3,2,1,0:T(8,128)}, f32[4,6,16,256]{3,2,1,0:T(8,128)}, f32[8,128]{1,0:T(8,128)}, f32[11,16,256]{2,1,0:T(8,128)}, f32[11,16,256]{2,1,0:T(8,128)}, /*index=5*/f32[4,6,8,256]{3,2,1,0:T(8,128)}) custom-call(s32[2]{0:T(128)} %pad_add_fusion.1.refs_0_, f32[11,16,256]{2,1,0:T(8,128)} %copy-done.19, f32[11,16,256]{2,1,0:T(8,128)} %copy-done.20, ...), custom_call_target="tpu_custom_call" | custom-call | tf_op jit(solution)/shard_map/apply_3/pallas_call | solution.py:267
  79.2 0.7 broadcast_in_dim.24
  79.8 16.6 %all_to_all.5.refs_0_ = f32[32,8,128]{2,1,0:T(8,128)} all-to-all(f32[32,8,128]{2,1,0:T(8,128)S(1)} %broadcast_in_dim.24), channel_id=1, replica_groups=mesh['slab'=16,'sub'=2] {'slab','sub'}, dimensions={0} | all-to-all | bytes 262144 | tf_op jit(solution)/shard_map/all_to_all | solution.py:390
  96.4 3.7 %combine.1 = (f32[4,4,6,16,256]{4,3,2,1,0:T(8,128)}, f32[3,4,6,16,256]{4,3,2,1,0:T(8,128)}, f32[4,3]{1,0:T(4,128)}, f32[1]{0:T(128)}) custom-call(f32[32,8,128]{2,1,0:T(8,128)} %all_to_all.5.refs_0_, f32[4,6,16,256]{3,2,1,0:T(8,128)S(1)} %copy-done, f32[4,6,16,256]{3,2,1,0:T(8,128)} %get-tuple-element.171.refs_8_.refs_2_, ...), custom_call_target="tpu_custom_call" | custom-call | tf_op jit(solution)/shard_map/combine/pallas_call | solution.py:392
  100.2 0.8 while.22
  (31 shorter events, 0.3 us)
Async XLA Ops:
  0.6 1.3 %copy-start = (f32[4,6,16,256]{3,2,1,0:T(8,128)S(1)}, f32[4,6,16,256]{3,2,1,0:T(8,128)}, u32[]{:S(2)}) copy-start(f32[4,6,16,256]{3,2,1,0:T(8,128)} %refs_1_.1) | copy-start | bytes 1179652
  2.8 6.5 %collective-permute-start.13 = (f32[26,16,256]{2,1,0:T(8,128)}, f32[26,16,256]{2,1,0:T(8,128)S(1)}, u32[]{:S(2)}, u32[]{:S(2)}) collective-permute-start(f32[26,16,256]{2,1,0:T(8,128)} %get-tuple-element.251), channel_id=1, source_target_pairs={{2,4},{4,2},{6,8},{8,6},{10,12},{12,10},{14,16},{16,14},{18,20},{2... | collective-permute-start | bytes 1277960 | tf_op jit(solution)/shard_map/ppermute | solution.py:57
  3.5 24.5 %collective-permute-start.12 = (f32[26,16,256]{2,1,0:T(8,128)S(1)}, f32[26,16,256]{2,1,0:T(8,128)S(1)}, u32[]{:S(2)}, u32[]{:S(2)}) collective-permute-start(f32[26,16,256]{2,1,0:T(8,128)S(1)} %get-tuple-element.252), channel_id=1, source_target_pairs={{0,2},{2,0},{4,6},{6,4},{8,10},{10,8},{12,14},{14,12},{16,18},{18,... | collective-permute-start | bytes 1277960 | tf_op jit(solution)/shard_map/ppermute | solution.py:56
  9.3 21.6 %collective-permute-start.14 = (f32[54,8,256]{2,1,0:T(8,128)S(1)}, f32[54,8,256]{2,1,0:T(8,128)S(1)}, u32[]{:S(2)}, u32[]{:S(2)}) collective-permute-start(f32[54,8,256]{2,1,0:T(8,128)S(1)} %fusion.9), channel_id=1, source_target_pairs={{0,1},{1,0},{2,3},{3,2},{4,5},{5,4},{6,7},{7,6},{8,9},{9,8},{10,11... | collective-permute-start | bytes 1327112 | tf_op jit(solution)/shard_map/ppermute | solution.py:29
  28.8 2.8 %collective-permute-start.15 = (f32[52,8,256]{2,1,0:T(8,128)}, f32[52,8,256]{2,1,0:T(8,128)S(1)}, u32[]{:S(2)}, u32[]{:S(2)}) collective-permute-start(f32[52,8,256]{2,1,0:T(8,128)} %fusion.10), channel_id=1, source_target_pairs={{0,1},{1,0},{2,3},{3,2},{4,5},{5,4},{6,7},{7,6},{8,9},{9,8},{10,11... | collective-permute-start | bytes 1277960 | tf_op jit(solution)/shard_map/ppermute | solution.py:29
  31.6 1.0 copy-start.18
  31.6 1.0 %copy-start.23 = (f32[6,16,256]{2,1,0:T(8,128)S(1)}, f32[6,16,256]{2,1,0:T(8,128)}, u32[]{:S(2)}) copy-start(f32[6,16,256]{2,1,0:T(8,128)} %param.27) | copy-start | bytes 294916
  31.6 1.1 %copy-start.24 = (f32[6,16,256]{2,1,0:T(8,128)S(1)}, f32[6,16,256]{2,1,0:T(8,128)}, u32[]{:S(2)}) copy-start(f32[6,16,256]{2,1,0:T(8,128)} %param.26) | copy-start | bytes 294916
  41.0 10.3 %collective-permute-start.16 = (f32[11,16,256]{2,1,0:T(8,128)}, f32[11,16,256]{2,1,0:T(8,128)S(1)}, u32[]{:S(2)}, u32[]{:S(2)}) collective-permute-start(f32[11,16,256]{2,1,0:T(8,128)} %get-tuple-element.167), channel_id=1, source_target_pairs={{0,2},{2,0},{4,6},{6,4},{8,10},{10,8},{12,14},{14,12},{16,18},{18,... | collective-permute-start | bytes 540680 | tf_op jit(solution)/shard_map/ppermute | solution.py:56
  42.6 8.7 %collective-permute-start.17 = (f32[11,16,256]{2,1,0:T(8,128)}, f32[11,16,256]{2,1,0:T(8,128)S(1)}, u32[]{:S(2)}, u32[]{:S(2)}) collective-permute-start(f32[11,16,256]{2,1,0:T(8,128)} %get-tuple-element.168), channel_id=1, source_target_pairs={{2,4},{4,2},{6,8},{8,6},{10,12},{12,10},{14,16},{16,14},{18,20},{2... | collective-permute-start | bytes 540680 | tf_op jit(solution)/shard_map/ppermute | solution.py:57
  43.3 8.1 %collective-permute-start.18 = (f32[4,6,8,256]{3,2,1,0:T(8,128)}, f32[4,6,8,256]{3,2,1,0:T(8,128)S(1)}, u32[]{:S(2)}, u32[]{:S(2)}) collective-permute-start(f32[4,6,8,256]{3,2,1,0:T(8,128)} %get-tuple-element.169), channel_id=1, source_target_pairs={{0,1},{1,0},{2,3},{3,2},{4,5},{5,4},{6,7},{7,6},{8,9},{9,8},{10,11... | collective-permute-start | bytes 589832 | tf_op jit(solution)/shard_map/ppermute | solution.py:29
  51.3 1.5 %copy-start.21 = (f32[11,16,256]{2,1,0:T(8,128)}, f32[11,16,256]{2,1,0:T(8,128)S(1)}, u32[]{:S(2)}) copy-start(f32[11,16,256]{2,1,0:T(8,128)S(1)} %collective-permute-done.16.refs_1_) | copy-start | bytes 540676
  51.3 1.5 %copy-start.22 = (f32[11,16,256]{2,1,0:T(8,128)}, f32[11,16,256]{2,1,0:T(8,128)S(1)}, u32[]{:S(2)}) copy-start(f32[11,16,256]{2,1,0:T(8,128)S(1)} %collective-permute-done.17.refs_2_) | copy-start | bytes 540676
  51.3 1.5 %collective-permute-start.19 = (f32[22,8,256]{2,1,0:T(8,128)S(1)}, f32[22,8,256]{2,1,0:T(8,128)S(1)}, u32[]{:S(2)}, u32[]{:S(2)}) collective-permute-start(f32[22,8,256]{2,1,0:T(8,128)S(1)} %fusion.14), channel_id=1, source_target_pairs={{0,1},{1,0},{2,3},{3,2},{4,5},{5,4},{6,7},{7,6},{8,9},{9,8},{10,11... | collective-permute-start | bytes 540680 | tf_op jit(solution)/shard_map/ppermute | solution.py:29
  51.4 1.4 %copy-start.26 = (f32[4,6,8,256]{3,2,1,0:T(8,128)}, f32[4,6,8,256]{3,2,1,0:T(8,128)S(1)}, u32[]{:S(2)}) copy-start(f32[4,6,8,256]{3,2,1,0:T(8,128)S(1)} %collective-permute-done.18.refs_3_) | copy-start | bytes 589828
  52.8 0.7 copy-start.28
  61.2 7.9 %collective-permute-start.20 = (f32[11,16,256]{2,1,0:T(8,128)}, f32[11,16,256]{2,1,0:T(8,128)S(1)}, u32[]{:S(2)}, u32[]{:S(2)}) collective-permute-start(f32[11,16,256]{2,1,0:T(8,128)} %get-tuple-element.172), channel_id=1, source_target_pairs={{0,2},{2,0},{4,6},{6,4},{8,10},{10,8},{12,14},{14,12},{16,18},{18,... | collective-permute-start | bytes 540680 | tf_op jit(solution)/shard_map/ppermute | solution.py:56
  63.6 5.6 %collective-permute-start.21 = (f32[11,16,256]{2,1,0:T(8,128)}, f32[11,16,256]{2,1,0:T(8,128)S(1)}, u32[]{:S(2)}, u32[]{:S(2)}) collective-permute-start(f32[11,16,256]{2,1,0:T(8,128)} %get-tuple-element.173), channel_id=1, source_target_pairs={{2,4},{4,2},{6,8},{8,6},{10,12},{12,10},{14,16},{16,14},{18,20},{2... | collective-permute-start | bytes 540680 | tf_op jit(solution)/shard_map/ppermute | solution.py:57
  64.2 5.0 %collective-permute-start.22 = (f32[4,6,8,256]{3,2,1,0:T(8,128)}, f32[4,6,8,256]{3,2,1,0:T(8,128)S(1)}, u32[]{:S(2)}, u32[]{:S(2)}) collective-permute-start(f32[4,6,8,256]{3,2,1,0:T(8,128)} %get-tuple-element.174), channel_id=1, source_target_pairs={{0,1},{1,0},{2,3},{3,2},{4,5},{5,4},{6,7},{7,6},{8,9},{9,8},{10,11... | collective-permute-start | bytes 589832 | tf_op jit(solution)/shard_map/ppermute | solution.py:29
  69.1 1.5 %copy-start.19 = (f32[11,16,256]{2,1,0:T(8,128)}, f32[11,16,256]{2,1,0:T(8,128)S(1)}, u32[]{:S(2)}) copy-start(f32[11,16,256]{2,1,0:T(8,128)S(1)} %collective-permute-done.20.refs_1_) | copy-start | bytes 540676
  69.1 1.5 %copy-start.20 = (f32[11,16,256]{2,1,0:T(8,128)}, f32[11,16,256]{2,1,0:T(8,128)S(1)}, u32[]{:S(2)}) copy-start(f32[11,16,256]{2,1,0:T(8,128)S(1)} %collective-permute-done.21.refs_2_) | copy-start | bytes 540676
  69.1 1.5 %collective-permute-start.23 = (f32[22,8,256]{2,1,0:T(8,128)S(1)}, f32[22,8,256]{2,1,0:T(8,128)S(1)}, u32[]{:S(2)}, u32[]{:S(2)}) collective-permute-start(f32[22,8,256]{2,1,0:T(8,128)S(1)} %fusion.13), channel_id=1, source_target_pairs={{0,1},{1,0},{2,3},{3,2},{4,5},{5,4},{6,7},{7,6},{8,9},{9,8},{10,11... | collective-permute-start | bytes 540680 | tf_op jit(solution)/shard_map/ppermute | solution.py:29
  69.2 1.4 %copy-start.25 = (f32[4,6,8,256]{3,2,1,0:T(8,128)}, f32[4,6,8,256]{3,2,1,0:T(8,128)S(1)}, u32[]{:S(2)}) copy-start(f32[4,6,8,256]{3,2,1,0:T(8,128)S(1)} %collective-permute-done.22.refs_3_) | copy-start | bytes 589828
  70.6 0.7 copy-start.27

commit v4 on v3

--- a/solution.py
+++ b/solution.py
@@ -90,8 +90,7 @@
     left = jnp.where(sub == 1, other, 0.0)
     right = jnp.where(sub == 0, other, 0.0)
     coef = jnp.concatenate([left, jnp.concatenate([low, stacked, high], 1), right], 2)
-    rest = jnp.concatenate([corner[cut:planes], corner[planes + cut :]], 0)
-    return (near[cut:], far[cut:], side, rest), coef
+    return (near, far, side, corner), coef
 
 
 def exchange(to_near, to_far, side_out):
@@ -111,12 +110,13 @@
 
 
 def apply_kernel(
-    count, shift, slabs, subs, *refs
+    count, shift, slabs, subs, skip, *refs
 ):
-    place, near, far, side, corner, coef, tile_in = refs[:7]
-    olds = refs[7 : 7 + count]
-    found, new, tile_out, to_near, to_far, side_out = refs[7 + count : 13 + count]
-    pres, tee, schur, vel, first, second = refs[13 + count :]
+    place, near, far, side, corner, coef = refs[:6]
+    olds = refs[6 : 6 + count]
+    tiles = refs[6 + count : -12]
+    found, new, tile_out, to_near, to_far, side_out = refs[-12:-6]
+    pres, tee, schur, vel, first, second = refs[-6:]
     own = olds[-1]
     cells_x, cells_y, lanes = own.shape[1:]
     rows = cells_y + 2 * PAD
@@ -125,10 +125,12 @@
     even = slab % 2 == 0
 
     def low(i):
-        return jnp.where(even, far[i], near[i]), jnp.where(even, corner[11 + i], corner[i])
+        i, j = skip + i, near.shape[0] + skip + i
+        return jnp.where(even, far[i], near[i]), jnp.where(even, corner[j], corner[i])
 
     def high(i):
-        return jnp.where(even, near[i], far[i]), jnp.where(even, corner[i], corner[11 + i])
+        i, j = skip + i, near.shape[0] + skip + i
+        return jnp.where(even, near[i], far[i]), jnp.where(even, corner[i], corner[j])
 
     def put(write, middle, beyond):
         write(slice(PAD, PAD + cells_y), middle)
@@ -249,15 +251,15 @@
         to_far[k] = jnp.where(even, new[c, i], new[c, j])
     lane = lax.broadcasted_iota(jnp.int32, (8, 128), 1)
     base = count * (count + 1) // 2
-    tile = tile_in[...]
+    tile = tiles[0][...] if tiles else jnp.zeros((8, 128), jnp.float32)
     for k in range(count + 1):
         tile = jnp.where(lane == base + k, jnp.sum(sums[k]), tile)
     if count == 1:
         tile = jnp.where(lane == 0, jnp.sum(sums[2]), tile)
-    tile_out[...] = tile
-
-
-def apply_both(olds, arrived, coef, tile, shift):
+    tile_out[...] = jnp.broadcast_to(tile, tile_out.shape)
+
+
+def apply_both(olds, arrived, coef, tiles, shift, tile_shape=(8, 128)):
     own = olds[-1]
     cells_x, cells_y, lanes = own.shape[1:]
     rows = cells_y + 2 * PAD
@@ -266,15 +268,16 @@
     f32 = jnp.float32
     return pl.pallas_call(
         functools.partial(
-            apply_kernel, len(olds), shift, lax.axis_size("slab"), lax.axis_size("sub")
+            apply_kernel, len(olds), shift, lax.axis_size("slab"), lax.axis_size("sub"),
+            arrived[0].shape[0] - 11,
         ),
         name=f"apply_{len(olds)}",
-        in_specs=[pl.BlockSpec(memory_space=pltpu.SMEM)] + [whole] * (6 + len(olds)),
+        in_specs=[pl.BlockSpec(memory_space=pltpu.SMEM)] + [whole] * (5 + len(olds) + len(tiles)),
         out_specs=[whole] * 6,
         out_shape=[
             jax.ShapeDtypeStruct(own.shape, f32),
             jax.ShapeDtypeStruct(own.shape, f32),
-            jax.ShapeDtypeStruct((8, 128), f32),
+            jax.ShapeDtypeStruct(tile_shape, f32),
             jax.ShapeDtypeStruct((11, cells_y, lanes), f32),
             jax.ShapeDtypeStruct((11, cells_y, lanes), f32),
             jax.ShapeDtypeStruct((4, cells_x, PAD, lanes), f32),
@@ -288,7 +291,7 @@
             pltpu.VMEM((3, cells_x + 2, rows, lanes), f32),
         ],
         compiler_params=pltpu.CompilerParams(vmem_limit_bytes=56 * 1024 * 1024),
-    )(place, *arrived, coef, tile, *olds)
+    )(place, *arrived, coef, *olds, *tiles)
 
 
 def combine_kernel(*refs):
@@ -357,14 +360,13 @@
     def total(value):
         return lax.psum(jnp.sum(value), AXES)
 
-    blank = jnp.zeros((8, 128), jnp.float32)
     vectors = [start / jnp.sqrt(total(start * start))]
     searches = []
     hess = jnp.zeros((ITERS + 1, ITERS), jnp.float32)
     for column in range(ITERS):
         own = vectors[column]
         arrived = exchange(*for_pairs(*split_ends(own)), edge_rows(own, 2))
-        found, image = apply_both([own], arrived, coef, blank, 0.0)[:2]
+        found, image = apply_both([own], arrived, coef, (), 0.0)[:2]
         searches.append(found)
         projected = [total(vector * image) for vector in vectors]
         for row in range(column + 1):
@@ -378,16 +380,20 @@
 
 def per_device(start, wind, reaction, mass):
     arrived, coef = exchange_first(start, jnp.concatenate([wind, reaction[None], mass[None]], 0))
-    tile = jnp.zeros((8, 128), jnp.float32)
+    devices = lax.axis_size("slab") * lax.axis_size("sub")
+    tiles = ()
     vectors, founds = [start], []
     for column in range(ITERS):
-        found, fresh, tile, *ends = apply_both(vectors, arrived, coef, tile, SHIFTS[column])
+        shape = (8, 128) if column + 1 < ITERS else (devices, 8, 128)
+        found, fresh, tile, *ends = apply_both(
+            vectors, arrived, coef, tiles, SHIFTS[column], shape
+        )
+        tiles = (tile,)
         founds.append(found)
         vectors.append(fresh)
         if column + 1 < ITERS:
             arrived = exchange(*ends)
-    devices = lax.axis_size("slab") * lax.axis_size("sub")
-    parts = lax.all_to_all(jnp.broadcast_to(tile[None], (devices, 8, 128)), AXES, 0, 0)
+    parts = lax.all_to_all(tile, AXES, 0, 0)
     whole = pl.BlockSpec(memory_space=pltpu.VMEM)
     basis, search, small, least = pl.pallas_call(
         combine_kernel,

time: 102 us -> 98.2 us (0.963)
  local copies, waits for them, and re-layouts: 5.04 us -> 2.82 us
  other arithmetic: 4.48 us -> 2.97 us
    slice x3 -> x0, local copies, waits for them, and re-layouts: 1.37 us -> none  [the longest x2 1.35 us: exchange_first(): return ((near[cut:], far[cut:], side, rest), coef)]
    unnamed x28 -> x34, local copies, waits for them, and re-layouts: 1.66 us -> 2.08 us
  transfers between devices with their start and end apart: 12 -> 12, of which waited for: 5 -> 6; matrix products, arithmetic and copies ran while one was open for 4% -> 1% of each run, Pallas kernels for 0% -> 0%
where the time goes in v4:
time: 98.2 us; the launch traced here: 97.9 us
  waiting for transfers between devices  34.1 us (35%)
  Pallas kernels  27.1 us (28%)
  blocking collectives  16.8 us (17%)
  starting transfers between devices  12.2 us (12%)
  other arithmetic  2.97 us (3%)
  local copies, waits for them, and re-layouts  2.82 us (3%)
  between operations  1.13 us (1%)
    ppermute x3, waiting for transfers between devices, swap(): near = lax.ppermute(to_near, 'slab', swap_pairs(devices, False))  31 us
    pallas_call x3, Pallas kernels, apply_both(): pl.pallas_call(functools.partial(apply_kernel, len(olds), shift, lax.axis...  23.3 us
    all_to_all x1, blocking collectives, per_device(): parts = lax.all_to_all(tile, AXES, 0, 0)  16.8 us
    ppermute x3, starting transfers between devices, swap(): near = lax.ppermute(to_near, 'slab', swap_pairs(devices, False))  9.75 us
    pallas_call x1, Pallas kernels, per_device(): pl.pallas_call(combine_kernel, name='combine', in_specs=[whole] * 8, out_...  3.73 us
    ppermute x6, waiting for transfers between devices, across(): return lax.ppermute(field, 'sub', [(0, 1), (1, 0)])  3.13 us
    unnamed x34, local copies, waits for them, and re-layouts  2.08 us
    ppermute x3, starting transfers between devices, swap(): far = lax.ppermute(to_far, 'slab', swap_pairs(devices, True))  2 us
  transfers between devices with their start and end apart: 12, of which 6 were waited for; matrix products, arithmetic and copies ran while one was open for 1% of the time, Pallas kernels for 0%

profile of v4, /device:TPU:0, one launch (start us, length us, event | category | flops | bytes accessed | tf_op | source)
XLA Modules:
  0.0 97.9 jit_solution(16482230998314831235)
XLA Ops:
  0.7 1.1 %pad_maximum_fusion.9 = f32[5,6,16,256]{3,2,1,0:T(8,128)S(1)} fusion(f32[1,6,16,256]{3,2,1,0:T(8,128)} %bitcast.120, f32[1,6,16,256]{3,2,1,0:T(8,128)} %bitcast.122, f32[3,6,16,256]{3,2,1,0:T(8,128)} %param.25), kind=kLoop, calls=%fused_computation.75 | loop fusion | flops 245760 | bytes 983040 | tf_op jit(solution)/shard_map/concatenate | solution.py:382
  2.0 0.8 broadcast_select_fusion
  2.8 0.7 collective-permute-start.13
  3.5 5.7 %collective-permute-start.12 = (f32[26,16,256]{2,1,0:T(8,128)S(1)}, f32[26,16,256]{2,1,0:T(8,128)S(1)}, u32[]{:S(2)}, u32[]{:S(2)}) collective-permute-start(f32[26,16,256]{2,1,0:T(8,128)S(1)} %get-tuple-element.252), channel_id=1, source_target_pairs={{0,2},{2,0},{4,6},{6,4},{8,10},{10,8},{12,14},{14,12},{16,18},{18,... | collective-permute-start | bytes 1277960 | tf_op jit(solution)/shard_map/ppermute | solution.py:56
  9.3 0.1 collective-permute-start.14
  9.3 0.0 collective-permute-done.13.refs_2_
  9.4 0.0 copy-start.18
  9.4 18.6 %collective-permute-done.12.refs_1_ = f32[26,16,256]{2,1,0:T(8,128)S(1)} collective-permute-done((f32[26,16,256]{2,1,0:T(8,128)S(1)}, f32[26,16,256]{2,1,0:T(8,128)S(1)}, u32[]{:S(2)}, u32[]{:S(2)}) %collective-permute-start.12) | collective-permute-done | bytes 426016 | tf_op jit(solution)/shard_map/ppermute | solution.py:56
  28.1 0.1 collective-permute-start.15
  28.1 0.6 pad_add_fusion.1.refs_0_
  28.8 0.0 copy-start.20
  28.8 0.0 copy-start.26
  28.8 0.0 copy-start.27
  28.8 0.0 collective-permute-done.14
  28.8 0.7 slice.333
  29.5 0.0 copy-done.18
  29.5 0.0 copy-done.19
  29.5 0.4 collective-permute-done.15.refs_4_
  29.9 0.1 fusion.12
  30.0 0.6 copy-done.21
  30.7 0.0 copy-done.20
  30.7 0.2 pad_maximum_fusion.8.refs_5_
  30.8 7.7 %apply_1.7 = (f32[4,6,16,256]{3,2,1,0:T(8,128)}, f32[4,6,16,256]{3,2,1,0:T(8,128)}, f32[8,128]{1,0:T(8,128)}, f32[11,16,256]{2,1,0:T(8,128)}, f32[11,16,256]{2,1,0:T(8,128)}, /*index=5*/f32[4,6,8,256]{3,2,1,0:T(8,128)}) custom-call(s32[2]{0:T(128)} %pad_add_fusion.1.refs_0_, f32[26,16,256]{2,1,0:T(8,128)} %copy-done.19, f32[26,16,256]{2,1,0:T(8,128)} %copy-done.18, ...), custom_call_target="tpu_custom_call" | custom-call | tf_op jit(solution)/shard_map/apply_1/pallas_call | solution.py:269
  38.6 1.6 %collective-permute-start.16 = (f32[11,16,256]{2,1,0:T(8,128)}, f32[11,16,256]{2,1,0:T(8,128)S(1)}, u32[]{:S(2)}, u32[]{:S(2)}) collective-permute-start(f32[11,16,256]{2,1,0:T(8,128)} %get-tuple-element.167), channel_id=1, source_target_pairs={{0,2},{2,0},{4,6},{6,4},{8,10},{10,8},{12,14},{14,12},{16,18},{18,... | collective-permute-start | bytes 540680 | tf_op jit(solution)/shard_map/ppermute | solution.py:56
  40.2 0.7 collective-permute-start.17
  40.9 0.1 collective-permute-start.18
  41.0 7.5 %collective-permute-done.16.refs_1_ = f32[11,16,256]{2,1,0:T(8,128)S(1)} collective-permute-done((f32[11,16,256]{2,1,0:T(8,128)}, f32[11,16,256]{2,1,0:T(8,128)S(1)}, u32[]{:S(2)}, u32[]{:S(2)}) %collective-permute-start.16) | collective-permute-done | bytes 180256 | tf_op jit(solution)/shard_map/ppermute | solution.py:56
  48.5 0.0 collective-permute-done.17.refs_2_
  48.5 0.1 collective-permute-start.19
  48.6 0.0 collective-permute-done.18.refs_3_
  48.6 0.0 copy-start.29
  48.6 1.4 %collective-permute-done.19.refs_4_ = f32[22,8,256]{2,1,0:T(8,128)S(1)} collective-permute-done((f32[22,8,256]{2,1,0:T(8,128)S(1)}, f32[22,8,256]{2,1,0:T(8,128)S(1)}, u32[]{:S(2)}, u32[]{:S(2)}) %collective-permute-start.19) | collective-permute-done | bytes 180256 | tf_op jit(solution)/shard_map/ppermute | solution.py:29
  50.0 0.7 copy-done.31
  50.7 7.7 %apply_2.1 = (f32[4,6,16,256]{3,2,1,0:T(8,128)}, f32[4,6,16,256]{3,2,1,0:T(8,128)}, f32[8,128]{1,0:T(8,128)}, f32[11,16,256]{2,1,0:T(8,128)}, f32[11,16,256]{2,1,0:T(8,128)}, /*index=5*/f32[4,6,8,256]{3,2,1,0:T(8,128)}) custom-call(s32[2]{0:T(128)} %pad_add_fusion.1.refs_0_, f32[11,16,256]{2,1,0:T(8,128)} %copy-done.24, f32[11,16,256]{2,1,0:T(8,128)} %copy-done.25, ...), custom_call_target="tpu_custom_call" | custom-call | tf_op jit(solution)/shard_map/apply_2/pallas_call | solution.py:269
  58.4 2.4 %collective-permute-start.20 = (f32[11,16,256]{2,1,0:T(8,128)}, f32[11,16,256]{2,1,0:T(8,128)S(1)}, u32[]{:S(2)}, u32[]{:S(2)}) collective-permute-start(f32[11,16,256]{2,1,0:T(8,128)} %get-tuple-element.172), channel_id=1, source_target_pairs={{0,2},{2,0},{4,6},{6,4},{8,10},{10,8},{12,14},{14,12},{16,18},{18,... | collective-permute-start | bytes 540680 | tf_op jit(solution)/shard_map/ppermute | solution.py:56
  60.8 0.7 collective-permute-start.21
  61.5 0.1 collective-permute-start.22
  61.5 4.8 %collective-permute-done.20.refs_1_ = f32[11,16,256]{2,1,0:T(8,128)S(1)} collective-permute-done((f32[11,16,256]{2,1,0:T(8,128)}, f32[11,16,256]{2,1,0:T(8,128)S(1)}, u32[]{:S(2)}, u32[]{:S(2)}) %collective-permute-start.20) | collective-permute-done | bytes 180256 | tf_op jit(solution)/shard_map/ppermute | solution.py:56
  66.3 0.0 collective-permute-done.21.refs_2_
  66.4 0.1 collective-permute-start.23
  66.5 0.0 collective-permute-done.22.refs_3_
  66.5 0.0 copy-start.28
  66.5 1.4 %collective-permute-done.23.refs_4_ = f32[22,8,256]{2,1,0:T(8,128)S(1)} collective-permute-done((f32[22,8,256]{2,1,0:T(8,128)S(1)}, f32[22,8,256]{2,1,0:T(8,128)S(1)}, u32[]{:S(2)}, u32[]{:S(2)}) %collective-permute-start.23) | collective-permute-done | bytes 180256 | tf_op jit(solution)/shard_map/ppermute | solution.py:29
  67.9 0.7 copy-done.30
  68.5 7.9 %apply_3.1 = (f32[4,6,16,256]{3,2,1,0:T(8,128)}, f32[4,6,16,256]{3,2,1,0:T(8,128)}, f32[32,8,128]{2,1,0:T(8,128)}, f32[11,16,256]{2,1,0:T(8,128)}, f32[11,16,256]{2,1,0:T(8,128)}, /*index=5*/f32[4,6,8,256]{3,2,1,0:T(8,128)}) custom-call(s32[2]{0:T(128)} %pad_add_fusion.1.refs_0_, f32[11,16,256]{2,1,0:T(8,128)} %copy-done.22, f32[11,16,256]{2,1,0:T(8,128)} %copy-done.23, ...), custom_call_target="tpu_custom_call" | custom-call | tf_op jit(solution)/shard_map/apply_3/pallas_call | solution.py:269
  76.4 16.8 %all_to_all.5.refs_0_ = f32[32,8,128]{2,1,0:T(8,128)} all-to-all(f32[32,8,128]{2,1,0:T(8,128)} %get-tuple-element.177), channel_id=1, replica_groups=mesh['slab'=16,'sub'=2] {'slab','sub'}, dimensions={0} | all-to-all | bytes 262144 | tf_op jit(solution)/shard_map/all_to_all | solution.py:396
  93.2 3.7 %combine.1 = (f32[4,4,6,16,256]{4,3,2,1,0:T(8,128)}, f32[3,4,6,16,256]{4,3,2,1,0:T(8,128)}, f32[4,3]{1,0:T(4,128)}, f32[1]{0:T(128)}) custom-call(f32[32,8,128]{2,1,0:T(8,128)} %all_to_all.5.refs_0_, f32[4,6,16,256]{3,2,1,0:T(8,128)S(1)} %copy-done, f32[4,6,16,256]{3,2,1,0:T(8,128)} %get-tuple-element.170.refs_7_.refs_2_, ...), custom_call_target="tpu_custom_call" | custom-call | tf_op jit(solution)/shard_map/combine/pallas_call | solution.py:398
  96.9 0.8 while.22
  (31 shorter events, 0.3 us)
Async XLA Ops:
  0.6 1.3 %copy-start = (f32[4,6,16,256]{3,2,1,0:T(8,128)S(1)}, f32[4,6,16,256]{3,2,1,0:T(8,128)}, u32[]{:S(2)}) copy-start(f32[4,6,16,256]{3,2,1,0:T(8,128)} %refs_1_.1) | copy-start | bytes 1179652
  2.8 6.5 %collective-permute-start.13 = (f32[26,16,256]{2,1,0:T(8,128)}, f32[26,16,256]{2,1,0:T(8,128)S(1)}, u32[]{:S(2)}, u32[]{:S(2)}) collective-permute-start(f32[26,16,256]{2,1,0:T(8,128)} %get-tuple-element.251), channel_id=1, source_target_pairs={{2,4},{4,2},{6,8},{8,6},{10,12},{12,10},{14,16},{16,14},{18,20},{2... | collective-permute-start | bytes 1277960 | tf_op jit(solution)/shard_map/ppermute | solution.py:57
  3.5 24.5 %collective-permute-start.12 = (f32[26,16,256]{2,1,0:T(8,128)S(1)}, f32[26,16,256]{2,1,0:T(8,128)S(1)}, u32[]{:S(2)}, u32[]{:S(2)}) collective-permute-start(f32[26,16,256]{2,1,0:T(8,128)S(1)} %get-tuple-element.252), channel_id=1, source_target_pairs={{0,2},{2,0},{4,6},{6,4},{8,10},{10,8},{12,14},{14,12},{16,18},{18,... | collective-permute-start | bytes 1277960 | tf_op jit(solution)/shard_map/ppermute | solution.py:56
  9.3 19.5 %collective-permute-start.14 = (f32[54,8,256]{2,1,0:T(8,128)S(1)}, f32[54,8,256]{2,1,0:T(8,128)S(1)}, u32[]{:S(2)}, u32[]{:S(2)}) collective-permute-start(f32[54,8,256]{2,1,0:T(8,128)S(1)} %fusion.9), channel_id=1, source_target_pairs={{0,1},{1,0},{2,3},{3,2},{4,5},{5,4},{6,7},{7,6},{8,9},{9,8},{10,11... | collective-permute-start | bytes 1327112 | tf_op jit(solution)/shard_map/ppermute | solution.py:29
  9.4 20.1 %copy-start.18 = (f32[26,16,256]{2,1,0:T(8,128)}, f32[26,16,256]{2,1,0:T(8,128)S(1)}, u32[]{:S(2)}) copy-start(f32[26,16,256]{2,1,0:T(8,128)S(1)} %collective-permute-done.13.refs_2_) | copy-start | bytes 1277956
  28.0 1.5 %copy-start.19 = (f32[26,16,256]{2,1,0:T(8,128)}, f32[26,16,256]{2,1,0:T(8,128)S(1)}, u32[]{:S(2)}) copy-start(f32[26,16,256]{2,1,0:T(8,128)S(1)} %collective-permute-done.12.refs_1_) | copy-start | bytes 1277956
  28.1 1.8 %collective-permute-start.15 = (f32[52,8,256]{2,1,0:T(8,128)S(1)}, f32[52,8,256]{2,1,0:T(8,128)S(1)}, u32[]{:S(2)}, u32[]{:S(2)}) collective-permute-start(f32[52,8,256]{2,1,0:T(8,128)S(1)} %fusion.10), channel_id=1, source_target_pairs={{0,1},{1,0},{2,3},{3,2},{4,5},{5,4},{6,7},{7,6},{8,9},{9,8},{10,11... | collective-permute-start | bytes 1277960 | tf_op jit(solution)/shard_map/ppermute | solution.py:29
  28.8 1.9 %copy-start.20 = (f32[3,6,16,256]{3,2,1,0:T(8,128)S(1)}, f32[3,6,16,256]{3,2,1,0:T(8,128)}, u32[]{:S(2)}) copy-start(f32[3,6,16,256]{3,2,1,0:T(8,128)} %param.25) | copy-start | bytes 884740
  28.8 1.9 %copy-start.26 = (f32[6,16,256]{2,1,0:T(8,128)S(1)}, f32[6,16,256]{2,1,0:T(8,128)}, u32[]{:S(2)}) copy-start(f32[6,16,256]{2,1,0:T(8,128)} %param.27) | copy-start | bytes 294916
  28.8 1.9 %copy-start.27 = (f32[6,16,256]{2,1,0:T(8,128)S(1)}, f32[6,16,256]{2,1,0:T(8,128)}, u32[]{:S(2)}) copy-start(f32[6,16,256]{2,1,0:T(8,128)} %param.26) | copy-start | bytes 294916
  29.9 0.8 copy-start.21
  38.6 9.9 %collective-permute-start.16 = (f32[11,16,256]{2,1,0:T(8,128)}, f32[11,16,256]{2,1,0:T(8,128)S(1)}, u32[]{:S(2)}, u32[]{:S(2)}) collective-permute-start(f32[11,16,256]{2,1,0:T(8,128)} %get-tuple-element.167), channel_id=1, source_target_pairs={{0,2},{2,0},{4,6},{6,4},{8,10},{10,8},{12,14},{14,12},{16,18},{18,... | collective-permute-start | bytes 540680 | tf_op jit(solution)/shard_map/ppermute | solution.py:56
  40.2 8.3 %collective-permute-start.17 = (f32[11,16,256]{2,1,0:T(8,128)}, f32[11,16,256]{2,1,0:T(8,128)S(1)}, u32[]{:S(2)}, u32[]{:S(2)}) collective-permute-start(f32[11,16,256]{2,1,0:T(8,128)} %get-tuple-element.168), channel_id=1, source_target_pairs={{2,4},{4,2},{6,8},{8,6},{10,12},{12,10},{14,16},{16,14},{18,20},{2... | collective-permute-start | bytes 540680 | tf_op jit(solution)/shard_map/ppermute | solution.py:57
  40.9 7.7 %collective-permute-start.18 = (f32[4,6,8,256]{3,2,1,0:T(8,128)}, f32[4,6,8,256]{3,2,1,0:T(8,128)S(1)}, u32[]{:S(2)}, u32[]{:S(2)}) collective-permute-start(f32[4,6,8,256]{3,2,1,0:T(8,128)} %get-tuple-element.169), channel_id=1, source_target_pairs={{0,1},{1,0},{2,3},{3,2},{4,5},{5,4},{6,7},{7,6},{8,9},{9,8},{10,11... | collective-permute-start | bytes 589832 | tf_op jit(solution)/shard_map/ppermute | solution.py:29
  48.5 1.5 %copy-start.24 = (f32[11,16,256]{2,1,0:T(8,128)}, f32[11,16,256]{2,1,0:T(8,128)S(1)}, u32[]{:S(2)}) copy-start(f32[11,16,256]{2,1,0:T(8,128)S(1)} %collective-permute-done.16.refs_1_) | copy-start | bytes 540676
  48.5 1.5 %copy-start.25 = (f32[11,16,256]{2,1,0:T(8,128)}, f32[11,16,256]{2,1,0:T(8,128)S(1)}, u32[]{:S(2)}) copy-start(f32[11,16,256]{2,1,0:T(8,128)S(1)} %collective-permute-done.17.refs_2_) | copy-start | bytes 540676
  48.5 1.5 %collective-permute-start.19 = (f32[22,8,256]{2,1,0:T(8,128)S(1)}, f32[22,8,256]{2,1,0:T(8,128)S(1)}, u32[]{:S(2)}, u32[]{:S(2)}) collective-permute-start(f32[22,8,256]{2,1,0:T(8,128)S(1)} %fusion.14), channel_id=1, source_target_pairs={{0,1},{1,0},{2,3},{3,2},{4,5},{5,4},{6,7},{7,6},{8,9},{9,8},{10,11... | collective-permute-start | bytes 540680 | tf_op jit(solution)/shard_map/ppermute | solution.py:29
  48.6 1.4 %copy-start.29 = (f32[4,6,8,256]{3,2,1,0:T(8,128)}, f32[4,6,8,256]{3,2,1,0:T(8,128)S(1)}, u32[]{:S(2)}) copy-start(f32[4,6,8,256]{3,2,1,0:T(8,128)S(1)} %collective-permute-done.18.refs_3_) | copy-start | bytes 589828
  50.0 0.7 copy-start.31
  58.4 7.9 %collective-permute-start.20 = (f32[11,16,256]{2,1,0:T(8,128)}, f32[11,16,256]{2,1,0:T(8,128)S(1)}, u32[]{:S(2)}, u32[]{:S(2)}) collective-permute-start(f32[11,16,256]{2,1,0:T(8,128)} %get-tuple-element.172), channel_id=1, source_target_pairs={{0,2},{2,0},{4,6},{6,4},{8,10},{10,8},{12,14},{14,12},{16,18},{18,... | collective-permute-start | bytes 540680 | tf_op jit(solution)/shard_map/ppermute | solution.py:56
  60.8 5.6 %collective-permute-start.21 = (f32[11,16,256]{2,1,0:T(8,128)}, f32[11,16,256]{2,1,0:T(8,128)S(1)}, u32[]{:S(2)}, u32[]{:S(2)}) collective-permute-start(f32[11,16,256]{2,1,0:T(8,128)} %get-tuple-element.173), channel_id=1, source_target_pairs={{2,4},{4,2},{6,8},{8,6},{10,12},{12,10},{14,16},{16,14},{18,20},{2... | collective-permute-start | bytes 540680 | tf_op jit(solution)/shard_map/ppermute | solution.py:57
  61.5 5.0 %collective-permute-start.22 = (f32[4,6,8,256]{3,2,1,0:T(8,128)}, f32[4,6,8,256]{3,2,1,0:T(8,128)S(1)}, u32[]{:S(2)}, u32[]{:S(2)}) collective-permute-start(f32[4,6,8,256]{3,2,1,0:T(8,128)} %get-tuple-element.174), channel_id=1, source_target_pairs={{0,1},{1,0},{2,3},{3,2},{4,5},{5,4},{6,7},{7,6},{8,9},{9,8},{10,11... | collective-permute-start | bytes 589832 | tf_op jit(solution)/shard_map/ppermute | solution.py:29
  66.3 1.5 %copy-start.22 = (f32[11,16,256]{2,1,0:T(8,128)}, f32[11,16,256]{2,1,0:T(8,128)S(1)}, u32[]{:S(2)}) copy-start(f32[11,16,256]{2,1,0:T(8,128)S(1)} %collective-permute-done.20.refs_1_) | copy-start | bytes 540676
  66.4 1.5 %copy-start.23 = (f32[11,16,256]{2,1,0:T(8,128)}, f32[11,16,256]{2,1,0:T(8,128)S(1)}, u32[]{:S(2)}) copy-start(f32[11,16,256]{2,1,0:T(8,128)S(1)} %collective-permute-done.21.refs_2_) | copy-start | bytes 540676
  66.4 1.5 %collective-permute-start.23 = (f32[22,8,256]{2,1,0:T(8,128)S(1)}, f32[22,8,256]{2,1,0:T(8,128)S(1)}, u32[]{:S(2)}, u32[]{:S(2)}) collective-permute-start(f32[22,8,256]{2,1,0:T(8,128)S(1)} %fusion.13), channel_id=1, source_target_pairs={{0,1},{1,0},{2,3},{3,2},{4,5},{5,4},{6,7},{7,6},{8,9},{9,8},{10,11... | collective-permute-start | bytes 540680 | tf_op jit(solution)/shard_map/ppermute | solution.py:29
  66.5 1.4 %copy-start.28 = (f32[4,6,8,256]{3,2,1,0:T(8,128)}, f32[4,6,8,256]{3,2,1,0:T(8,128)S(1)}, u32[]{:S(2)}) copy-start(f32[4,6,8,256]{3,2,1,0:T(8,128)S(1)} %collective-permute-done.22.refs_3_) | copy-start | bytes 589828
  67.9 0.7 copy-start.30

commit v5 on v4

--- a/solution.py
+++ b/solution.py
@@ -173,20 +173,20 @@
         convect = convect + coef[2, k] * (z_plus - z_minus)
         return (6.0 + coef[3, k]) * center - total + 0.5 * convect
 
-    @pl.loop(0, cells_x + 8)
+    @pl.loop(0, cells_x + 8, unroll=2 - cells_x % 2)
     def _(i):
         center = pres[i + 1]
         y_plus, y_minus, z_plus, z_minus = plane_shifts(center)
         total = pres[i + 2] + pres[i] + y_plus + y_minus + z_plus + z_minus
         tee[i] = jnp.where(inside(i, 4), center * (1.0 / 7.0) + total * (1.0 / 49.0), 0.0)
 
-    @pl.loop(0, cells_x + 6)
+    @pl.loop(0, cells_x + 6, unroll=2 - cells_x % 2)
     def _(i):
         center = tee[i + 1]
         value = transport(center, tee[i + 2], tee[i], plane_shifts(center), i)
         schur[i] = jnp.where(inside(i, 3), -value / coef[4, i], 0.0)
 
-    @pl.loop(0, cells_x + 4)
+    @pl.loop(0, cells_x + 4, unroll=2 - cells_x % 2)
     def _(i):
         center = schur[i + 1]
         y_plus, y_minus, z_plus, z_minus = plane_shifts(center)

time: 98.2 us -> 94.1 us (0.958)
  Pallas kernels: 27.1 us -> 23 us
    pallas_call x3, Pallas kernels: 23.3 us -> 19.2 us  [apply_both(): pl.pallas_call(functools.partial(apply_kernel, len(olds), shift, lax.axis...]
where the time goes in v5:
time: 94.1 us; the launch traced here: 93.7 us
  waiting for transfers between devices  34.1 us (36%)
  Pallas kernels  23 us (24%)
  blocking collectives  16.8 us (18%)
  starting transfers between devices  12.2 us (13%)
  other arithmetic  2.97 us (3%)
  local copies, waits for them, and re-layouts  2.82 us (3%)
  between operations  1.13 us (1%)
    ppermute x3, waiting for transfers between devices, swap(): near = lax.ppermute(to_near, 'slab', swap_pairs(devices, False))  31 us
    pallas_call x3, Pallas kernels, apply_both(): pl.pallas_call(functools.partial(apply_kernel, len(olds), shift, lax.axis...  19.2 us
    all_to_all x1, blocking collectives, per_device(): parts = lax.all_to_all(tile, AXES, 0, 0)  16.8 us
    ppermute x3, starting transfers between devices, swap(): near = lax.ppermute(to_near, 'slab', swap_pairs(devices, False))  9.75 us
    pallas_call x1, Pallas kernels, per_device(): pl.pallas_call(combine_kernel, name='combine', in_specs=[whole] * 8, out_...  3.73 us
    ppermute x6, waiting for transfers between devices, across(): return lax.ppermute(field, 'sub', [(0, 1), (1, 0)])  3.13 us
    unnamed x34, local copies, waits for them, and re-layouts  2.08 us
    ppermute x3, starting transfers between devices, swap(): far = lax.ppermute(to_far, 'slab', swap_pairs(devices, True))  2 us
  transfers between devices with their start and end apart: 12, of which 6 were waited for; matrix products, arithmetic and copies ran while one was open for 1% of the time, Pallas kernels for 0%

profile of v5, /device:TPU:0, one launch (start us, length us, event | category | flops | bytes accessed | tf_op | source)
XLA Modules:
  0.0 93.7 jit_solution(15042876888520235926)
XLA Ops:
  0.7 1.1 %pad_maximum_fusion.9 = f32[5,6,16,256]{3,2,1,0:T(8,128)S(1)} fusion(f32[1,6,16,256]{3,2,1,0:T(8,128)} %bitcast.120, f32[1,6,16,256]{3,2,1,0:T(8,128)} %bitcast.122, f32[3,6,16,256]{3,2,1,0:T(8,128)} %param.25), kind=kLoop, calls=%fused_computation.75 | loop fusion | flops 245760 | bytes 983040 | tf_op jit(solution)/shard_map/concatenate | solution.py:382
  2.0 0.8 broadcast_select_fusion
  2.8 0.7 collective-permute-start.13
  3.5 5.7 %collective-permute-start.12 = (f32[26,16,256]{2,1,0:T(8,128)S(1)}, f32[26,16,256]{2,1,0:T(8,128)S(1)}, u32[]{:S(2)}, u32[]{:S(2)}) collective-permute-start(f32[26,16,256]{2,1,0:T(8,128)S(1)} %get-tuple-element.252), channel_id=1, source_target_pairs={{0,2},{2,0},{4,6},{6,4},{8,10},{10,8},{12,14},{14,12},{16,18},{18,... | collective-permute-start | bytes 1277960 | tf_op jit(solution)/shard_map/ppermute | solution.py:56
  9.3 0.1 collective-permute-start.14
  9.3 0.0 collective-permute-done.13.refs_2_
  9.4 0.0 copy-start.18
  9.4 18.6 %collective-permute-done.12.refs_1_ = f32[26,16,256]{2,1,0:T(8,128)S(1)} collective-permute-done((f32[26,16,256]{2,1,0:T(8,128)S(1)}, f32[26,16,256]{2,1,0:T(8,128)S(1)}, u32[]{:S(2)}, u32[]{:S(2)}) %collective-permute-start.12) | collective-permute-done | bytes 426016 | tf_op jit(solution)/shard_map/ppermute | solution.py:56
  28.1 0.1 collective-permute-start.15
  28.1 0.6 pad_add_fusion.1.refs_0_
  28.8 0.0 copy-start.20
  28.8 0.0 copy-start.26
  28.8 0.0 copy-start.27
  28.8 0.0 collective-permute-done.14
  28.8 0.7 slice.333
  29.5 0.0 copy-done.18
  29.5 0.0 copy-done.19
  29.5 0.4 collective-permute-done.15.refs_4_
  29.9 0.1 fusion.12
  30.0 0.6 copy-done.21
  30.7 0.0 copy-done.20
  30.7 0.2 pad_maximum_fusion.8.refs_5_
  30.8 6.4 %apply_1.7 = (f32[4,6,16,256]{3,2,1,0:T(8,128)}, f32[4,6,16,256]{3,2,1,0:T(8,128)}, f32[8,128]{1,0:T(8,128)}, f32[11,16,256]{2,1,0:T(8,128)}, f32[11,16,256]{2,1,0:T(8,128)}, /*index=5*/f32[4,6,8,256]{3,2,1,0:T(8,128)}) custom-call(s32[2]{0:T(128)} %pad_add_fusion.1.refs_0_, f32[26,16,256]{2,1,0:T(8,128)} %copy-done.19, f32[26,16,256]{2,1,0:T(8,128)} %copy-done.18, ...), custom_call_target="tpu_custom_call" | custom-call | tf_op jit(solution)/shard_map/apply_1/pallas_call | solution.py:269
  37.2 1.6 %collective-permute-start.16 = (f32[11,16,256]{2,1,0:T(8,128)}, f32[11,16,256]{2,1,0:T(8,128)S(1)}, u32[]{:S(2)}, u32[]{:S(2)}) collective-permute-start(f32[11,16,256]{2,1,0:T(8,128)} %get-tuple-element.167), channel_id=1, source_target_pairs={{0,2},{2,0},{4,6},{6,4},{8,10},{10,8},{12,14},{14,12},{16,18},{18,... | collective-permute-start | bytes 540680 | tf_op jit(solution)/shard_map/ppermute | solution.py:56
  38.8 0.7 collective-permute-start.17
  39.5 0.1 collective-permute-start.18
  39.6 7.5 %collective-permute-done.16.refs_1_ = f32[11,16,256]{2,1,0:T(8,128)S(1)} collective-permute-done((f32[11,16,256]{2,1,0:T(8,128)}, f32[11,16,256]{2,1,0:T(8,128)S(1)}, u32[]{:S(2)}, u32[]{:S(2)}) %collective-permute-start.16) | collective-permute-done | bytes 180256 | tf_op jit(solution)/shard_map/ppermute | solution.py:56
  47.1 0.0 collective-permute-done.17.refs_2_
  47.2 0.1 collective-permute-start.19
  47.2 0.0 collective-permute-done.18.refs_3_
  47.2 0.0 copy-start.29
  47.3 1.4 %collective-permute-done.19.refs_4_ = f32[22,8,256]{2,1,0:T(8,128)S(1)} collective-permute-done((f32[22,8,256]{2,1,0:T(8,128)S(1)}, f32[22,8,256]{2,1,0:T(8,128)S(1)}, u32[]{:S(2)}, u32[]{:S(2)}) %collective-permute-start.19) | collective-permute-done | bytes 180256 | tf_op jit(solution)/shard_map/ppermute | solution.py:29
  48.7 0.7 copy-done.31
  49.3 6.4 %apply_2.1 = (f32[4,6,16,256]{3,2,1,0:T(8,128)}, f32[4,6,16,256]{3,2,1,0:T(8,128)}, f32[8,128]{1,0:T(8,128)}, f32[11,16,256]{2,1,0:T(8,128)}, f32[11,16,256]{2,1,0:T(8,128)}, /*index=5*/f32[4,6,8,256]{3,2,1,0:T(8,128)}) custom-call(s32[2]{0:T(128)} %pad_add_fusion.1.refs_0_, f32[11,16,256]{2,1,0:T(8,128)} %copy-done.24, f32[11,16,256]{2,1,0:T(8,128)} %copy-done.25, ...), custom_call_target="tpu_custom_call" | custom-call | tf_op jit(solution)/shard_map/apply_2/pallas_call | solution.py:269
  55.7 2.4 %collective-permute-start.20 = (f32[11,16,256]{2,1,0:T(8,128)}, f32[11,16,256]{2,1,0:T(8,128)S(1)}, u32[]{:S(2)}, u32[]{:S(2)}) collective-permute-start(f32[11,16,256]{2,1,0:T(8,128)} %get-tuple-element.172), channel_id=1, source_target_pairs={{0,2},{2,0},{4,6},{6,4},{8,10},{10,8},{12,14},{14,12},{16,18},{18,... | collective-permute-start | bytes 540680 | tf_op jit(solution)/shard_map/ppermute | solution.py:56
  58.1 0.7 collective-permute-start.21
  58.7 0.1 collective-permute-start.22
  58.8 4.8 %collective-permute-done.20.refs_1_ = f32[11,16,256]{2,1,0:T(8,128)S(1)} collective-permute-done((f32[11,16,256]{2,1,0:T(8,128)}, f32[11,16,256]{2,1,0:T(8,128)S(1)}, u32[]{:S(2)}, u32[]{:S(2)}) %collective-permute-start.20) | collective-permute-done | bytes 180256 | tf_op jit(solution)/shard_map/ppermute | solution.py:56
  63.6 0.0 collective-permute-done.21.refs_2_
  63.6 0.1 collective-permute-start.23
  63.7 0.0 collective-permute-done.22.refs_3_
  63.7 0.0 copy-start.28
  63.7 1.4 %collective-permute-done.23.refs_4_ = f32[22,8,256]{2,1,0:T(8,128)S(1)} collective-permute-done((f32[22,8,256]{2,1,0:T(8,128)S(1)}, f32[22,8,256]{2,1,0:T(8,128)S(1)}, u32[]{:S(2)}, u32[]{:S(2)}) %collective-permute-start.23) | collective-permute-done | bytes 180256 | tf_op jit(solution)/shard_map/ppermute | solution.py:29
  65.1 0.7 copy-done.30
  65.8 6.5 %apply_3.1 = (f32[4,6,16,256]{3,2,1,0:T(8,128)}, f32[4,6,16,256]{3,2,1,0:T(8,128)}, f32[32,8,128]{2,1,0:T(8,128)}, f32[11,16,256]{2,1,0:T(8,128)}, f32[11,16,256]{2,1,0:T(8,128)}, /*index=5*/f32[4,6,8,256]{3,2,1,0:T(8,128)}) custom-call(s32[2]{0:T(128)} %pad_add_fusion.1.refs_0_, f32[11,16,256]{2,1,0:T(8,128)} %copy-done.22, f32[11,16,256]{2,1,0:T(8,128)} %copy-done.23, ...), custom_call_target="tpu_custom_call" | custom-call | tf_op jit(solution)/shard_map/apply_3/pallas_call | solution.py:269
  72.3 16.8 %all_to_all.5.refs_0_ = f32[32,8,128]{2,1,0:T(8,128)} all-to-all(f32[32,8,128]{2,1,0:T(8,128)} %get-tuple-element.177), channel_id=1, replica_groups=mesh['slab'=16,'sub'=2] {'slab','sub'}, dimensions={0} | all-to-all | bytes 262144 | tf_op jit(solution)/shard_map/all_to_all | solution.py:396
  89.1 3.7 %combine.1 = (f32[4,4,6,16,256]{4,3,2,1,0:T(8,128)}, f32[3,4,6,16,256]{4,3,2,1,0:T(8,128)}, f32[4,3]{1,0:T(4,128)}, f32[1]{0:T(128)}) custom-call(f32[32,8,128]{2,1,0:T(8,128)} %all_to_all.5.refs_0_, f32[4,6,16,256]{3,2,1,0:T(8,128)S(1)} %copy-done, f32[4,6,16,256]{3,2,1,0:T(8,128)} %get-tuple-element.170.refs_7_.refs_2_, ...), custom_call_target="tpu_custom_call" | custom-call | tf_op jit(solution)/shard_map/combine/pallas_call | solution.py:398
  92.8 0.8 while.22
  (31 shorter events, 0.3 us)
Async XLA Ops:
  0.6 1.3 %copy-start = (f32[4,6,16,256]{3,2,1,0:T(8,128)S(1)}, f32[4,6,16,256]{3,2,1,0:T(8,128)}, u32[]{:S(2)}) copy-start(f32[4,6,16,256]{3,2,1,0:T(8,128)} %refs_1_.1) | copy-start | bytes 1179652
  2.8 6.5 %collective-permute-start.13 = (f32[26,16,256]{2,1,0:T(8,128)}, f32[26,16,256]{2,1,0:T(8,128)S(1)}, u32[]{:S(2)}, u32[]{:S(2)}) collective-permute-start(f32[26,16,256]{2,1,0:T(8,128)} %get-tuple-element.251), channel_id=1, source_target_pairs={{2,4},{4,2},{6,8},{8,6},{10,12},{12,10},{14,16},{16,14},{18,20},{2... | collective-permute-start | bytes 1277960 | tf_op jit(solution)/shard_map/ppermute | solution.py:57
  3.5 24.5 %collective-permute-start.12 = (f32[26,16,256]{2,1,0:T(8,128)S(1)}, f32[26,16,256]{2,1,0:T(8,128)S(1)}, u32[]{:S(2)}, u32[]{:S(2)}) collective-permute-start(f32[26,16,256]{2,1,0:T(8,128)S(1)} %get-tuple-element.252), channel_id=1, source_target_pairs={{0,2},{2,0},{4,6},{6,4},{8,10},{10,8},{12,14},{14,12},{16,18},{18,... | collective-permute-start | bytes 1277960 | tf_op jit(solution)/shard_map/ppermute | solution.py:56
  9.3 19.5 %collective-permute-start.14 = (f32[54,8,256]{2,1,0:T(8,128)S(1)}, f32[54,8,256]{2,1,0:T(8,128)S(1)}, u32[]{:S(2)}, u32[]{:S(2)}) collective-permute-start(f32[54,8,256]{2,1,0:T(8,128)S(1)} %fusion.9), channel_id=1, source_target_pairs={{0,1},{1,0},{2,3},{3,2},{4,5},{5,4},{6,7},{7,6},{8,9},{9,8},{10,11... | collective-permute-start | bytes 1327112 | tf_op jit(solution)/shard_map/ppermute | solution.py:29
  9.4 20.1 %copy-start.18 = (f32[26,16,256]{2,1,0:T(8,128)}, f32[26,16,256]{2,1,0:T(8,128)S(1)}, u32[]{:S(2)}) copy-start(f32[26,16,256]{2,1,0:T(8,128)S(1)} %collective-permute-done.13.refs_2_) | copy-start | bytes 1277956
  28.0 1.5 %copy-start.19 = (f32[26,16,256]{2,1,0:T(8,128)}, f32[26,16,256]{2,1,0:T(8,128)S(1)}, u32[]{:S(2)}) copy-start(f32[26,16,256]{2,1,0:T(8,128)S(1)} %collective-permute-done.12.refs_1_) | copy-start | bytes 1277956
  28.1 1.8 %collective-permute-start.15 = (f32[52,8,256]{2,1,0:T(8,128)S(1)}, f32[52,8,256]{2,1,0:T(8,128)S(1)}, u32[]{:S(2)}, u32[]{:S(2)}) collective-permute-start(f32[52,8,256]{2,1,0:T(8,128)S(1)} %fusion.10), channel_id=1, source_target_pairs={{0,1},{1,0},{2,3},{3,2},{4,5},{5,4},{6,7},{7,6},{8,9},{9,8},{10,11... | collective-permute-start | bytes 1277960 | tf_op jit(solution)/shard_map/ppermute | solution.py:29
  28.8 1.9 %copy-start.20 = (f32[3,6,16,256]{3,2,1,0:T(8,128)S(1)}, f32[3,6,16,256]{3,2,1,0:T(8,128)}, u32[]{:S(2)}) copy-start(f32[3,6,16,256]{3,2,1,0:T(8,128)} %param.25) | copy-start | bytes 884740
  28.8 1.9 %copy-start.26 = (f32[6,16,256]{2,1,0:T(8,128)S(1)}, f32[6,16,256]{2,1,0:T(8,128)}, u32[]{:S(2)}) copy-start(f32[6,16,256]{2,1,0:T(8,128)} %param.27) | copy-start | bytes 294916
  28.8 1.9 %copy-start.27 = (f32[6,16,256]{2,1,0:T(8,128)S(1)}, f32[6,16,256]{2,1,0:T(8,128)}, u32[]{:S(2)}) copy-start(f32[6,16,256]{2,1,0:T(8,128)} %param.26) | copy-start | bytes 294916
  29.9 0.8 copy-start.21
  37.2 9.9 %collective-permute-start.16 = (f32[11,16,256]{2,1,0:T(8,128)}, f32[11,16,256]{2,1,0:T(8,128)S(1)}, u32[]{:S(2)}, u32[]{:S(2)}) collective-permute-start(f32[11,16,256]{2,1,0:T(8,128)} %get-tuple-element.167), channel_id=1, source_target_pairs={{0,2},{2,0},{4,6},{6,4},{8,10},{10,8},{12,14},{14,12},{16,18},{18,... | collective-permute-start | bytes 540680 | tf_op jit(solution)/shard_map/ppermute | solution.py:56
  38.8 8.3 %collective-permute-start.17 = (f32[11,16,256]{2,1,0:T(8,128)}, f32[11,16,256]{2,1,0:T(8,128)S(1)}, u32[]{:S(2)}, u32[]{:S(2)}) collective-permute-start(f32[11,16,256]{2,1,0:T(8,128)} %get-tuple-element.168), channel_id=1, source_target_pairs={{2,4},{4,2},{6,8},{8,6},{10,12},{12,10},{14,16},{16,14},{18,20},{2... | collective-permute-start | bytes 540680 | tf_op jit(solution)/shard_map/ppermute | solution.py:57
  39.5 7.7 %collective-permute-start.18 = (f32[4,6,8,256]{3,2,1,0:T(8,128)}, f32[4,6,8,256]{3,2,1,0:T(8,128)S(1)}, u32[]{:S(2)}, u32[]{:S(2)}) collective-permute-start(f32[4,6,8,256]{3,2,1,0:T(8,128)} %get-tuple-element.169), channel_id=1, source_target_pairs={{0,1},{1,0},{2,3},{3,2},{4,5},{5,4},{6,7},{7,6},{8,9},{9,8},{10,11... | collective-permute-start | bytes 589832 | tf_op jit(solution)/shard_map/ppermute | solution.py:29
  47.1 1.5 %copy-start.24 = (f32[11,16,256]{2,1,0:T(8,128)}, f32[11,16,256]{2,1,0:T(8,128)S(1)}, u32[]{:S(2)}) copy-start(f32[11,16,256]{2,1,0:T(8,128)S(1)} %collective-permute-done.16.refs_1_) | copy-start | bytes 540676
  47.1 1.5 %copy-start.25 = (f32[11,16,256]{2,1,0:T(8,128)}, f32[11,16,256]{2,1,0:T(8,128)S(1)}, u32[]{:S(2)}) copy-start(f32[11,16,256]{2,1,0:T(8,128)S(1)} %collective-permute-done.17.refs_2_) | copy-start | bytes 540676
  47.2 1.5 %collective-permute-start.19 = (f32[22,8,256]{2,1,0:T(8,128)S(1)}, f32[22,8,256]{2,1,0:T(8,128)S(1)}, u32[]{:S(2)}, u32[]{:S(2)}) collective-permute-start(f32[22,8,256]{2,1,0:T(8,128)S(1)} %fusion.14), channel_id=1, source_target_pairs={{0,1},{1,0},{2,3},{3,2},{4,5},{5,4},{6,7},{7,6},{8,9},{9,8},{10,11... | collective-permute-start | bytes 540680 | tf_op jit(solution)/shard_map/ppermute | solution.py:29
  47.2 1.4 %copy-start.29 = (f32[4,6,8,256]{3,2,1,0:T(8,128)}, f32[4,6,8,256]{3,2,1,0:T(8,128)S(1)}, u32[]{:S(2)}) copy-start(f32[4,6,8,256]{3,2,1,0:T(8,128)S(1)} %collective-permute-done.18.refs_3_) | copy-start | bytes 589828
  48.6 0.7 copy-start.31
  55.7 7.9 %collective-permute-start.20 = (f32[11,16,256]{2,1,0:T(8,128)}, f32[11,16,256]{2,1,0:T(8,128)S(1)}, u32[]{:S(2)}, u32[]{:S(2)}) collective-permute-start(f32[11,16,256]{2,1,0:T(8,128)} %get-tuple-element.172), channel_id=1, source_target_pairs={{0,2},{2,0},{4,6},{6,4},{8,10},{10,8},{12,14},{14,12},{16,18},{18,... | collective-permute-start | bytes 540680 | tf_op jit(solution)/shard_map/ppermute | solution.py:56
  58.1 5.6 %collective-permute-start.21 = (f32[11,16,256]{2,1,0:T(8,128)}, f32[11,16,256]{2,1,0:T(8,128)S(1)}, u32[]{:S(2)}, u32[]{:S(2)}) collective-permute-start(f32[11,16,256]{2,1,0:T(8,128)} %get-tuple-element.173), channel_id=1, source_target_pairs={{2,4},{4,2},{6,8},{8,6},{10,12},{12,10},{14,16},{16,14},{18,20},{2... | collective-permute-start | bytes 540680 | tf_op jit(solution)/shard_map/ppermute | solution.py:57
  58.7 5.0 %collective-permute-start.22 = (f32[4,6,8,256]{3,2,1,0:T(8,128)}, f32[4,6,8,256]{3,2,1,0:T(8,128)S(1)}, u32[]{:S(2)}, u32[]{:S(2)}) collective-permute-start(f32[4,6,8,256]{3,2,1,0:T(8,128)} %get-tuple-element.174), channel_id=1, source_target_pairs={{0,1},{1,0},{2,3},{3,2},{4,5},{5,4},{6,7},{7,6},{8,9},{9,8},{10,11... | collective-permute-start | bytes 589832 | tf_op jit(solution)/shard_map/ppermute | solution.py:29
  63.6 1.5 %copy-start.22 = (f32[11,16,256]{2,1,0:T(8,128)}, f32[11,16,256]{2,1,0:T(8,128)S(1)}, u32[]{:S(2)}) copy-start(f32[11,16,256]{2,1,0:T(8,128)S(1)} %collective-permute-done.20.refs_1_) | copy-start | bytes 540676
  63.6 1.5 %copy-start.23 = (f32[11,16,256]{2,1,0:T(8,128)}, f32[11,16,256]{2,1,0:T(8,128)S(1)}, u32[]{:S(2)}) copy-start(f32[11,16,256]{2,1,0:T(8,128)S(1)} %collective-permute-done.21.refs_2_) | copy-start | bytes 540676
  63.6 1.5 %collective-permute-start.23 = (f32[22,8,256]{2,1,0:T(8,128)S(1)}, f32[22,8,256]{2,1,0:T(8,128)S(1)}, u32[]{:S(2)}, u32[]{:S(2)}) collective-permute-start(f32[22,8,256]{2,1,0:T(8,128)S(1)} %fusion.13), channel_id=1, source_target_pairs={{0,1},{1,0},{2,3},{3,2},{4,5},{5,4},{6,7},{7,6},{8,9},{9,8},{10,11... | collective-permute-start | bytes 540680 | tf_op jit(solution)/shard_map/ppermute | solution.py:29
  63.7 1.4 %copy-start.28 = (f32[4,6,8,256]{3,2,1,0:T(8,128)}, f32[4,6,8,256]{3,2,1,0:T(8,128)S(1)}, u32[]{:S(2)}) copy-start(f32[4,6,8,256]{3,2,1,0:T(8,128)S(1)} %collective-permute-done.22.refs_3_) | copy-start | bytes 589828
  65.1 0.7 copy-start.30

commit v6 on v5

--- a/solution.py
+++ b/solution.py
@@ -152,7 +152,7 @@
             put(writer(vel, c, i), *low(k))
             put(writer(vel, c, 2 + cells_x + i), *high(k))
 
-    @pl.loop(0, cells_x)
+    @pl.loop(0, cells_x, unroll=2 - cells_x % 2)
     def _(i):
         put(writer(pres, 5 + i), own[3, i], side[3, i])
         for c in range(3):
@@ -197,7 +197,7 @@
             vel[c, i] = residue
             first[c, i] = residue * inverse
 
-    @pl.loop(0, cells_x + 2)
+    @pl.loop(0, cells_x + 2, unroll=2 - cells_x % 2)
     def _(i):
         inverse = jnp.where(inside(i, 1), 1.0 / (6.0 + coef[3, i + 2]), 0.0)
         for c in range(3):

time: 94.1 us -> 93.3 us (level)
  transfers between devices with their start and end apart: 12 -> 12, of which waited for: 6 -> 6; matrix products, arithmetic and copies ran while one was open for 1% -> 2% of each run, Pallas kernels for 0% -> 0%
where the time goes in v6:
time: 93.3 us; the launch traced here: 92.9 us
  waiting for transfers between devices  34.1 us (37%)
  Pallas kernels  22.2 us (24%)
  blocking collectives  16.8 us (18%)
  starting transfers between devices  12.2 us (13%)
  other arithmetic  2.97 us (3%)
  local copies, waits for them, and re-layouts  2.82 us (3%)
  between operations  1.13 us (1%)
    ppermute x3, waiting for transfers between devices, swap(): near = lax.ppermute(to_near, 'slab', swap_pairs(devices, False))  31 us
    pallas_call x3, Pallas kernels, apply_both(): pl.pallas_call(functools.partial(apply_kernel, len(olds), shift, lax.axis...  18.4 us
    all_to_all x1, blocking collectives, per_device(): parts = lax.all_to_all(tile, AXES, 0, 0)  16.8 us
    ppermute x3, starting transfers between devices, swap(): near = lax.ppermute(to_near, 'slab', swap_pairs(devices, False))  9.75 us
    pallas_call x1, Pallas kernels, per_device(): pl.pallas_call(combine_kernel, name='combine', in_specs=[whole] * 8, out_...  3.73 us
    ppermute x6, waiting for transfers between devices, across(): return lax.ppermute(field, 'sub', [(0, 1), (1, 0)])  3.13 us
    unnamed x34, local copies, waits for them, and re-layouts  2.08 us
    ppermute x3, starting transfers between devices, swap(): far = lax.ppermute(to_far, 'slab', swap_pairs(devices, True))  2 us
  transfers between devices with their start and end apart: 12, of which 6 were waited for; matrix products, arithmetic and copies ran while one was open for 2% of the time, Pallas kernels for 0%

profile of v6, /device:TPU:0, one launch (start us, length us, event | category | flops | bytes accessed | tf_op | source)
XLA Modules:
  0.0 92.9 jit_solution(17561861738490516314)
XLA Ops:
  0.7 1.1 %pad_maximum_fusion.9 = f32[5,6,16,256]{3,2,1,0:T(8,128)S(1)} fusion(f32[1,6,16,256]{3,2,1,0:T(8,128)} %bitcast.120, f32[1,6,16,256]{3,2,1,0:T(8,128)} %bitcast.122, f32[3,6,16,256]{3,2,1,0:T(8,128)} %param.25), kind=kLoop, calls=%fused_computation.75 | loop fusion | flops 245760 | bytes 983040 | tf_op jit(solution)/shard_map/concatenate | solution.py:382
  2.0 0.8 broadcast_select_fusion
  2.8 0.7 collective-permute-start.13
  3.5 5.7 %collective-permute-start.12 = (f32[26,16,256]{2,1,0:T(8,128)S(1)}, f32[26,16,256]{2,1,0:T(8,128)S(1)}, u32[]{:S(2)}, u32[]{:S(2)}) collective-permute-start(f32[26,16,256]{2,1,0:T(8,128)S(1)} %get-tuple-element.252), channel_id=1, source_target_pairs={{0,2},{2,0},{4,6},{6,4},{8,10},{10,8},{12,14},{14,12},{16,18},{18,... | collective-permute-start | bytes 1277960 | tf_op jit(solution)/shard_map/ppermute | solution.py:56
  9.3 0.1 collective-permute-start.14
  9.3 0.0 collective-permute-done.13.refs_2_
  9.4 0.0 copy-start.18
  9.4 18.6 %collective-permute-done.12.refs_1_ = f32[26,16,256]{2,1,0:T(8,128)S(1)} collective-permute-done((f32[26,16,256]{2,1,0:T(8,128)S(1)}, f32[26,16,256]{2,1,0:T(8,128)S(1)}, u32[]{:S(2)}, u32[]{:S(2)}) %collective-permute-start.12) | collective-permute-done | bytes 426016 | tf_op jit(solution)/shard_map/ppermute | solution.py:56
  28.1 0.1 collective-permute-start.15
  28.1 0.6 pad_add_fusion.1.refs_0_
  28.8 0.0 copy-start.20
  28.8 0.0 copy-start.26
  28.8 0.0 copy-start.27
  28.8 0.0 collective-permute-done.14
  28.8 0.7 slice.333
  29.5 0.0 copy-done.18
  29.5 0.0 copy-done.19
  29.5 0.4 collective-permute-done.15.refs_4_
  29.9 0.1 fusion.12
  30.0 0.6 copy-done.21
  30.7 0.0 copy-done.20
  30.7 0.2 pad_maximum_fusion.8.refs_5_
  30.8 6.1 %apply_1.7 = (f32[4,6,16,256]{3,2,1,0:T(8,128)}, f32[4,6,16,256]{3,2,1,0:T(8,128)}, f32[8,128]{1,0:T(8,128)}, f32[11,16,256]{2,1,0:T(8,128)}, f32[11,16,256]{2,1,0:T(8,128)}, /*index=5*/f32[4,6,8,256]{3,2,1,0:T(8,128)}) custom-call(s32[2]{0:T(128)} %pad_add_fusion.1.refs_0_, f32[26,16,256]{2,1,0:T(8,128)} %copy-done.19, f32[26,16,256]{2,1,0:T(8,128)} %copy-done.18, ...), custom_call_target="tpu_custom_call" | custom-call | tf_op jit(solution)/shard_map/apply_1/pallas_call | solution.py:269
  37.0 1.6 %collective-permute-start.16 = (f32[11,16,256]{2,1,0:T(8,128)}, f32[11,16,256]{2,1,0:T(8,128)S(1)}, u32[]{:S(2)}, u32[]{:S(2)}) collective-permute-start(f32[11,16,256]{2,1,0:T(8,128)} %get-tuple-element.167), channel_id=1, source_target_pairs={{0,2},{2,0},{4,6},{6,4},{8,10},{10,8},{12,14},{14,12},{16,18},{18,... | collective-permute-start | bytes 540680 | tf_op jit(solution)/shard_map/ppermute | solution.py:56
  38.6 0.7 collective-permute-start.17
  39.2 0.1 collective-permute-start.18
  39.3 7.5 %collective-permute-done.16.refs_1_ = f32[11,16,256]{2,1,0:T(8,128)S(1)} collective-permute-done((f32[11,16,256]{2,1,0:T(8,128)}, f32[11,16,256]{2,1,0:T(8,128)S(1)}, u32[]{:S(2)}, u32[]{:S(2)}) %collective-permute-start.16) | collective-permute-done | bytes 180256 | tf_op jit(solution)/shard_map/ppermute | solution.py:56
  46.9 0.0 collective-permute-done.17.refs_2_
  46.9 0.1 collective-permute-start.19
  47.0 0.0 collective-permute-done.18.refs_3_
  47.0 0.0 copy-start.29
  47.0 1.4 %collective-permute-done.19.refs_4_ = f32[22,8,256]{2,1,0:T(8,128)S(1)} collective-permute-done((f32[22,8,256]{2,1,0:T(8,128)S(1)}, f32[22,8,256]{2,1,0:T(8,128)S(1)}, u32[]{:S(2)}, u32[]{:S(2)}) %collective-permute-start.19) | collective-permute-done | bytes 180256 | tf_op jit(solution)/shard_map/ppermute | solution.py:29
  48.4 0.7 copy-done.31
  49.0 6.1 %apply_2.1 = (f32[4,6,16,256]{3,2,1,0:T(8,128)}, f32[4,6,16,256]{3,2,1,0:T(8,128)}, f32[8,128]{1,0:T(8,128)}, f32[11,16,256]{2,1,0:T(8,128)}, f32[11,16,256]{2,1,0:T(8,128)}, /*index=5*/f32[4,6,8,256]{3,2,1,0:T(8,128)}) custom-call(s32[2]{0:T(128)} %pad_add_fusion.1.refs_0_, f32[11,16,256]{2,1,0:T(8,128)} %copy-done.24, f32[11,16,256]{2,1,0:T(8,128)} %copy-done.25, ...), custom_call_target="tpu_custom_call" | custom-call | tf_op jit(solution)/shard_map/apply_2/pallas_call | solution.py:269
  55.1 2.4 %collective-permute-start.20 = (f32[11,16,256]{2,1,0:T(8,128)}, f32[11,16,256]{2,1,0:T(8,128)S(1)}, u32[]{:S(2)}, u32[]{:S(2)}) collective-permute-start(f32[11,16,256]{2,1,0:T(8,128)} %get-tuple-element.172), channel_id=1, source_target_pairs={{0,2},{2,0},{4,6},{6,4},{8,10},{10,8},{12,14},{14,12},{16,18},{18,... | collective-permute-start | bytes 540680 | tf_op jit(solution)/shard_map/ppermute | solution.py:56
  57.5 0.7 collective-permute-start.21
  58.2 0.1 collective-permute-start.22
  58.3 4.8 %collective-permute-done.20.refs_1_ = f32[11,16,256]{2,1,0:T(8,128)S(1)} collective-permute-done((f32[11,16,256]{2,1,0:T(8,128)}, f32[11,16,256]{2,1,0:T(8,128)S(1)}, u32[]{:S(2)}, u32[]{:S(2)}) %collective-permute-start.20) | collective-permute-done | bytes 180256 | tf_op jit(solution)/shard_map/ppermute | solution.py:56
  63.1 0.0 collective-permute-done.21.refs_2_
  63.1 0.1 collective-permute-start.23
  63.2 0.0 collective-permute-done.22.refs_3_
  63.2 0.0 copy-start.28
  63.2 1.4 %collective-permute-done.23.refs_4_ = f32[22,8,256]{2,1,0:T(8,128)S(1)} collective-permute-done((f32[22,8,256]{2,1,0:T(8,128)S(1)}, f32[22,8,256]{2,1,0:T(8,128)S(1)}, u32[]{:S(2)}, u32[]{:S(2)}) %collective-permute-start.23) | collective-permute-done | bytes 180256 | tf_op jit(solution)/shard_map/ppermute | solution.py:29
  64.6 0.7 copy-done.30
  65.3 6.2 %apply_3.1 = (f32[4,6,16,256]{3,2,1,0:T(8,128)}, f32[4,6,16,256]{3,2,1,0:T(8,128)}, f32[32,8,128]{2,1,0:T(8,128)}, f32[11,16,256]{2,1,0:T(8,128)}, f32[11,16,256]{2,1,0:T(8,128)}, /*index=5*/f32[4,6,8,256]{3,2,1,0:T(8,128)}) custom-call(s32[2]{0:T(128)} %pad_add_fusion.1.refs_0_, f32[11,16,256]{2,1,0:T(8,128)} %copy-done.22, f32[11,16,256]{2,1,0:T(8,128)} %copy-done.23, ...), custom_call_target="tpu_custom_call" | custom-call | tf_op jit(solution)/shard_map/apply_3/pallas_call | solution.py:269
  71.5 16.8 %all_to_all.5.refs_0_ = f32[32,8,128]{2,1,0:T(8,128)} all-to-all(f32[32,8,128]{2,1,0:T(8,128)} %get-tuple-element.177), channel_id=1, replica_groups=mesh['slab'=16,'sub'=2] {'slab','sub'}, dimensions={0} | all-to-all | bytes 262144 | tf_op jit(solution)/shard_map/all_to_all | solution.py:396
  88.3 3.7 %combine.1 = (f32[4,4,6,16,256]{4,3,2,1,0:T(8,128)}, f32[3,4,6,16,256]{4,3,2,1,0:T(8,128)}, f32[4,3]{1,0:T(4,128)}, f32[1]{0:T(128)}) custom-call(f32[32,8,128]{2,1,0:T(8,128)} %all_to_all.5.refs_0_, f32[4,6,16,256]{3,2,1,0:T(8,128)S(1)} %copy-done, f32[4,6,16,256]{3,2,1,0:T(8,128)} %get-tuple-element.170.refs_7_.refs_2_, ...), custom_call_target="tpu_custom_call" | custom-call | tf_op jit(solution)/shard_map/combine/pallas_call | solution.py:398
  92.0 0.8 while.22
  (31 shorter events, 0.3 us)
Async XLA Ops:
  0.6 1.3 %copy-start = (f32[4,6,16,256]{3,2,1,0:T(8,128)S(1)}, f32[4,6,16,256]{3,2,1,0:T(8,128)}, u32[]{:S(2)}) copy-start(f32[4,6,16,256]{3,2,1,0:T(8,128)} %refs_1_.1) | copy-start | bytes 1179652
  2.8 6.5 %collective-permute-start.13 = (f32[26,16,256]{2,1,0:T(8,128)}, f32[26,16,256]{2,1,0:T(8,128)S(1)}, u32[]{:S(2)}, u32[]{:S(2)}) collective-permute-start(f32[26,16,256]{2,1,0:T(8,128)} %get-tuple-element.251), channel_id=1, source_target_pairs={{2,4},{4,2},{6,8},{8,6},{10,12},{12,10},{14,16},{16,14},{18,20},{2... | collective-permute-start | bytes 1277960 | tf_op jit(solution)/shard_map/ppermute | solution.py:57
  3.5 24.5 %collective-permute-start.12 = (f32[26,16,256]{2,1,0:T(8,128)S(1)}, f32[26,16,256]{2,1,0:T(8,128)S(1)}, u32[]{:S(2)}, u32[]{:S(2)}) collective-permute-start(f32[26,16,256]{2,1,0:T(8,128)S(1)} %get-tuple-element.252), channel_id=1, source_target_pairs={{0,2},{2,0},{4,6},{6,4},{8,10},{10,8},{12,14},{14,12},{16,18},{18,... | collective-permute-start | bytes 1277960 | tf_op jit(solution)/shard_map/ppermute | solution.py:56
  9.3 19.5 %collective-permute-start.14 = (f32[54,8,256]{2,1,0:T(8,128)S(1)}, f32[54,8,256]{2,1,0:T(8,128)S(1)}, u32[]{:S(2)}, u32[]{:S(2)}) collective-permute-start(f32[54,8,256]{2,1,0:T(8,128)S(1)} %fusion.9), channel_id=1, source_target_pairs={{0,1},{1,0},{2,3},{3,2},{4,5},{5,4},{6,7},{7,6},{8,9},{9,8},{10,11... | collective-permute-start | bytes 1327112 | tf_op jit(solution)/shard_map/ppermute | solution.py:29
  9.4 20.1 %copy-start.18 = (f32[26,16,256]{2,1,0:T(8,128)}, f32[26,16,256]{2,1,0:T(8,128)S(1)}, u32[]{:S(2)}) copy-start(f32[26,16,256]{2,1,0:T(8,128)S(1)} %collective-permute-done.13.refs_2_) | copy-start | bytes 1277956
  28.0 1.5 %copy-start.19 = (f32[26,16,256]{2,1,0:T(8,128)}, f32[26,16,256]{2,1,0:T(8,128)S(1)}, u32[]{:S(2)}) copy-start(f32[26,16,256]{2,1,0:T(8,128)S(1)} %collective-permute-done.12.refs_1_) | copy-start | bytes 1277956
  28.1 1.8 %collective-permute-start.15 = (f32[52,8,256]{2,1,0:T(8,128)S(1)}, f32[52,8,256]{2,1,0:T(8,128)S(1)}, u32[]{:S(2)}, u32[]{:S(2)}) collective-permute-start(f32[52,8,256]{2,1,0:T(8,128)S(1)} %fusion.10), channel_id=1, source_target_pairs={{0,1},{1,0},{2,3},{3,2},{4,5},{5,4},{6,7},{7,6},{8,9},{9,8},{10,11... | collective-permute-start | bytes 1277960 | tf_op jit(solution)/shard_map/ppermute | solution.py:29
  28.8 1.9 %copy-start.20 = (f32[3,6,16,256]{3,2,1,0:T(8,128)S(1)}, f32[3,6,16,256]{3,2,1,0:T(8,128)}, u32[]{:S(2)}) copy-start(f32[3,6,16,256]{3,2,1,0:T(8,128)} %param.25) | copy-start | bytes 884740
  28.8 1.9 %copy-start.26 = (f32[6,16,256]{2,1,0:T(8,128)S(1)}, f32[6,16,256]{2,1,0:T(8,128)}, u32[]{:S(2)}) copy-start(f32[6,16,256]{2,1,0:T(8,128)} %param.27) | copy-start | bytes 294916
  28.8 1.9 %copy-start.27 = (f32[6,16,256]{2,1,0:T(8,128)S(1)}, f32[6,16,256]{2,1,0:T(8,128)}, u32[]{:S(2)}) copy-start(f32[6,16,256]{2,1,0:T(8,128)} %param.26) | copy-start | bytes 294916
  29.9 0.8 copy-start.21
  37.0 9.9 %collective-permute-start.16 = (f32[11,16,256]{2,1,0:T(8,128)}, f32[11,16,256]{2,1,0:T(8,128)S(1)}, u32[]{:S(2)}, u32[]{:S(2)}) collective-permute-start(f32[11,16,256]{2,1,0:T(8,128)} %get-tuple-element.167), channel_id=1, source_target_pairs={{0,2},{2,0},{4,6},{6,4},{8,10},{10,8},{12,14},{14,12},{16,18},{18,... | collective-permute-start | bytes 540680 | tf_op jit(solution)/shard_map/ppermute | solution.py:56
  38.6 8.3 %collective-permute-start.17 = (f32[11,16,256]{2,1,0:T(8,128)}, f32[11,16,256]{2,1,0:T(8,128)S(1)}, u32[]{:S(2)}, u32[]{:S(2)}) collective-permute-start(f32[11,16,256]{2,1,0:T(8,128)} %get-tuple-element.168), channel_id=1, source_target_pairs={{2,4},{4,2},{6,8},{8,6},{10,12},{12,10},{14,16},{16,14},{18,20},{2... | collective-permute-start | bytes 540680 | tf_op jit(solution)/shard_map/ppermute | solution.py:57
  39.2 7.7 %collective-permute-start.18 = (f32[4,6,8,256]{3,2,1,0:T(8,128)}, f32[4,6,8,256]{3,2,1,0:T(8,128)S(1)}, u32[]{:S(2)}, u32[]{:S(2)}) collective-permute-start(f32[4,6,8,256]{3,2,1,0:T(8,128)} %get-tuple-element.169), channel_id=1, source_target_pairs={{0,1},{1,0},{2,3},{3,2},{4,5},{5,4},{6,7},{7,6},{8,9},{9,8},{10,11... | collective-permute-start | bytes 589832 | tf_op jit(solution)/shard_map/ppermute | solution.py:29
  46.9 1.5 %copy-start.24 = (f32[11,16,256]{2,1,0:T(8,128)}, f32[11,16,256]{2,1,0:T(8,128)S(1)}, u32[]{:S(2)}) copy-start(f32[11,16,256]{2,1,0:T(8,128)S(1)} %collective-permute-done.16.refs_1_) | copy-start | bytes 540676
  46.9 1.5 %copy-start.25 = (f32[11,16,256]{2,1,0:T(8,128)}, f32[11,16,256]{2,1,0:T(8,128)S(1)}, u32[]{:S(2)}) copy-start(f32[11,16,256]{2,1,0:T(8,128)S(1)} %collective-permute-done.17.refs_2_) | copy-start | bytes 540676
  46.9 1.5 %collective-permute-start.19 = (f32[22,8,256]{2,1,0:T(8,128)S(1)}, f32[22,8,256]{2,1,0:T(8,128)S(1)}, u32[]{:S(2)}, u32[]{:S(2)}) collective-permute-start(f32[22,8,256]{2,1,0:T(8,128)S(1)} %fusion.14), channel_id=1, source_target_pairs={{0,1},{1,0},{2,3},{3,2},{4,5},{5,4},{6,7},{7,6},{8,9},{9,8},{10,11... | collective-permute-start | bytes 540680 | tf_op jit(solution)/shard_map/ppermute | solution.py:29
  47.0 1.4 %copy-start.29 = (f32[4,6,8,256]{3,2,1,0:T(8,128)}, f32[4,6,8,256]{3,2,1,0:T(8,128)S(1)}, u32[]{:S(2)}) copy-start(f32[4,6,8,256]{3,2,1,0:T(8,128)S(1)} %collective-permute-done.18.refs_3_) | copy-start | bytes 589828
  48.4 0.7 copy-start.31
  55.1 7.9 %collective-permute-start.20 = (f32[11,16,256]{2,1,0:T(8,128)}, f32[11,16,256]{2,1,0:T(8,128)S(1)}, u32[]{:S(2)}, u32[]{:S(2)}) collective-permute-start(f32[11,16,256]{2,1,0:T(8,128)} %get-tuple-element.172), channel_id=1, source_target_pairs={{0,2},{2,0},{4,6},{6,4},{8,10},{10,8},{12,14},{14,12},{16,18},{18,... | collective-permute-start | bytes 540680 | tf_op jit(solution)/shard_map/ppermute | solution.py:56
  57.5 5.6 %collective-permute-start.21 = (f32[11,16,256]{2,1,0:T(8,128)}, f32[11,16,256]{2,1,0:T(8,128)S(1)}, u32[]{:S(2)}, u32[]{:S(2)}) collective-permute-start(f32[11,16,256]{2,1,0:T(8,128)} %get-tuple-element.173), channel_id=1, source_target_pairs={{2,4},{4,2},{6,8},{8,6},{10,12},{12,10},{14,16},{16,14},{18,20},{2... | collective-permute-start | bytes 540680 | tf_op jit(solution)/shard_map/ppermute | solution.py:57
  58.2 5.0 %collective-permute-start.22 = (f32[4,6,8,256]{3,2,1,0:T(8,128)}, f32[4,6,8,256]{3,2,1,0:T(8,128)S(1)}, u32[]{:S(2)}, u32[]{:S(2)}) collective-permute-start(f32[4,6,8,256]{3,2,1,0:T(8,128)} %get-tuple-element.174), channel_id=1, source_target_pairs={{0,1},{1,0},{2,3},{3,2},{4,5},{5,4},{6,7},{7,6},{8,9},{9,8},{10,11... | collective-permute-start | bytes 589832 | tf_op jit(solution)/shard_map/ppermute | solution.py:29
  63.1 1.5 %copy-start.22 = (f32[11,16,256]{2,1,0:T(8,128)}, f32[11,16,256]{2,1,0:T(8,128)S(1)}, u32[]{:S(2)}) copy-start(f32[11,16,256]{2,1,0:T(8,128)S(1)} %collective-permute-done.20.refs_1_) | copy-start | bytes 540676
  63.1 1.5 %copy-start.23 = (f32[11,16,256]{2,1,0:T(8,128)}, f32[11,16,256]{2,1,0:T(8,128)S(1)}, u32[]{:S(2)}) copy-start(f32[11,16,256]{2,1,0:T(8,128)S(1)} %collective-permute-done.21.refs_2_) | copy-start | bytes 540676
  63.1 1.5 %collective-permute-start.23 = (f32[22,8,256]{2,1,0:T(8,128)S(1)}, f32[22,8,256]{2,1,0:T(8,128)S(1)}, u32[]{:S(2)}, u32[]{:S(2)}) collective-permute-start(f32[22,8,256]{2,1,0:T(8,128)S(1)} %fusion.13), channel_id=1, source_target_pairs={{0,1},{1,0},{2,3},{3,2},{4,5},{5,4},{6,7},{7,6},{8,9},{9,8},{10,11... | collective-permute-start | bytes 540680 | tf_op jit(solution)/shard_map/ppermute | solution.py:29
  63.2 1.4 %copy-start.28 = (f32[4,6,8,256]{3,2,1,0:T(8,128)}, f32[4,6,8,256]{3,2,1,0:T(8,128)S(1)}, u32[]{:S(2)}) copy-start(f32[4,6,8,256]{3,2,1,0:T(8,128)S(1)} %collective-permute-done.22.refs_3_) | copy-start | bytes 589828
  64.6 0.7 copy-start.30
